TPU v7x, 32 devices: a whole 2x2x4 slice. The times are simulated.
32 devices in a mesh: seq: 16 (over z, y, core), batch: 2 (over x).
Axes of the slice: x: 2, y: 2, z: 4, core: 2. Of those that a mesh axis runs over, the one named last changes fastest.
Arguments:
- hidden_in: bfloat16 [2, 4096, 2304], P('batch', 'seq'), may hold values from -6 to 6
- segment_ids: int32 [2, 4096], P('batch', 'seq'), may hold values from 0 to 15, never falling along the last dimension, each value on 1 to 512 neighbouring positions
- pre_gain: float32 [2304], replicated, may hold values from 0.25 to 1.75
- w_qkv: bfloat16 [2304, 2048], P('seq'), may hold values from -0.27083333 to 0.27083333
- w_out: bfloat16 [1024, 2304], P('seq'), may hold values from -0.1875 to 0.1875
- post_gain: float32 [2304], replicated, may hold values from 0.25 to 1.75
Outputs:
- layer_out: bfloat16 [2, 4096, 2304], P('batch', 'seq')
Inputs may be any that keep to these rules, and one draw needn't show every extreme that they name: `segment_ids`: along each sequence the numbers never fall; a document is 1 to 512 positions long, and each sequence has one of exactly 512.
All inputs are finite; a program needn't handle non-finite values.
Results may differ from a plain program's by a relative error of at most 0.012.
The roundings to bfloat16 on the way count: a program that leaves them out, or rounds other values in their place, can miss the bound.
Values may be sent and summed in bfloat16 or wider, within the bound.
No kernel may reach another device: no remote copies, remote signals or barrier semaphores. Data moves between devices by JAX's collectives and lax.ppermute only.
A program may use at most 128 MiB of HBM per device.

v0:
```python
import math

import jax
import jax.numpy as jnp
from jax import lax
from jax.sharding import PartitionSpec as P

Q_HEADS = 4
KV_HEADS = 2
HEAD = 256
WINDOW = 4096
DOCS = 16


EPS = 1e-06
CAP = 50.0


def from_behind(block, axis, distance):
    devices = range(lax.axis_size(axis))
    route = [(i - distance, i) for i in devices if i - distance in devices]
    return lax.ppermute(block, axis, route)


def rms_scale(values, gain):
    return values * lax.rsqrt(jnp.mean(values * values, axis=-1, keepdims=True) + EPS) * gain


def rotary(values, positions, leading):
    head_size = values.shape[-1]
    half_dim = head_size // 2
    inverse = 1.0 / 10000.0 ** (jnp.arange(half_dim, dtype=jnp.float32) * 2.0 / head_size)
    angles = positions.astype(jnp.float32)[:, None] * inverse[None, :]
    shape = (
        (1,) * leading + (positions.shape[0],) + (1,) * (values.ndim - 2 - leading) + (half_dim,)
    )
    cosine = jnp.cos(angles).reshape(shape)
    sine = jnp.sin(angles).reshape(shape)
    first_half = values[..., :half_dim]
    second_half = values[..., half_dim:]
    return jnp.concatenate(
        [first_half * cosine - second_half * sine, second_half * cosine + first_half * sine],
        axis=-1,
    )


def attend(states, queries, key_block, value_block, query_pos, key_pos, starts):
    running, totals = states
    scores = jnp.einsum(
        "qhgd,khd->qhgk", queries, key_block, preferred_element_type=jnp.float32
    ) * (1.0 / math.sqrt(HEAD))
    capped = CAP * jnp.tanh(scores / CAP)
    allowed = (
        (key_pos[None, :] <= query_pos[:, None])
        & (query_pos[:, None] - key_pos[None, :] < WINDOW)
        & (key_pos[None, :] >= starts[:, None])
    )
    weights = jnp.where(allowed[:, None, None, :], jnp.exp(capped), 0.0)
    totals = totals + jnp.sum(weights, axis=-1)
    running = running + jnp.einsum(
        "qhgk,khd->qhgd",
        weights.astype(jnp.bfloat16),
        value_block,
        preferred_element_type=jnp.float32,
    )
    return (running, totals)


def per_device(hidden_in, segment_ids, pre_gain, w_qkv, w_out, post_gain):
    tok_rows = hidden_in.shape[1]
    seq_count = lax.axis_size("seq")
    seq_index = lax.axis_index("seq")
    groups = Q_HEADS // KV_HEADS
    positions = seq_index * tok_rows + jnp.arange(tok_rows, dtype=jnp.int32)
    widened = hidden_in[0].astype(jnp.float32)
    normed = rms_scale(widened, pre_gain).astype(jnp.bfloat16)
    columns = normed
    projected = jnp.dot(
        columns,
        lax.all_gather(w_qkv, "seq", axis=0, tiled=True),
        preferred_element_type=jnp.float32,
    )
    queries = rotary(
        projected[:, : Q_HEADS * HEAD].reshape(tok_rows, KV_HEADS, groups, HEAD), positions, 0
    ).astype(jnp.bfloat16)
    key_rows = rotary(
        projected[:, Q_HEADS * HEAD : (Q_HEADS + KV_HEADS) * HEAD].reshape(
            tok_rows, KV_HEADS, HEAD
        ),
        positions,
        0,
    ).astype(jnp.bfloat16)
    value_rows = (
        projected[:, (Q_HEADS + KV_HEADS) * HEAD :]
        .reshape(tok_rows, KV_HEADS, HEAD)
        .astype(jnp.bfloat16)
    )
    doc_numbers = jnp.arange(DOCS, dtype=jnp.int32)
    matches = segment_ids[0][:, None] == doc_numbers[None, :]
    local_first = jnp.min(jnp.where(matches, positions[:, None], seq_count * tok_rows), axis=0)
    first_pos = lax.pmin(local_first, "seq")
    starts = jnp.sum(jnp.where(matches, first_pos[None, :], 0), axis=1)
    states = (
        jnp.zeros((tok_rows, KV_HEADS, groups, HEAD), jnp.float32),
        jnp.zeros((tok_rows, KV_HEADS, groups), jnp.float32),
    )
    states = attend(states, queries, key_rows, value_rows, positions, positions, starts)
    hop_count = min(WINDOW // tok_rows, seq_count - 1)

    def relay_step(hop_index, carried):
        moving_keys, moving_values, running, totals = carried
        moving_keys, moving_values = from_behind((moving_keys, moving_values), "seq", 1)
        running, totals = attend(
            (running, totals),
            queries,
            moving_keys,
            moving_values,
            positions,
            positions - hop_index * tok_rows,
            starts,
        )
        return (moving_keys, moving_values, running, totals)

    carried = lax.fori_loop(
        1, hop_count + 1, relay_step, (key_rows, value_rows, states[0], states[1])
    )
    states = (carried[2], carried[3])
    running, totals = states
    attended = (running / totals[..., None]).astype(jnp.bfloat16).reshape(tok_rows, Q_HEADS * HEAD)
    columns = attended
    branch = jnp.dot(
        columns,
        lax.all_gather(w_out, "seq", axis=0, tiled=True),
        preferred_element_type=jnp.float32,
    )
    return (widened + rms_scale(branch, post_gain)).astype(jnp.bfloat16)[None]


def solution(mesh):
    placed = (P("batch", "seq", None), P("batch", "seq"), P(), P("seq", None), P("seq", None), P())
    return jax.shard_map(
        per_device, mesh=mesh, in_specs=placed, out_specs=P("batch", "seq", None), check_vma=False
    )
```

profile of v0, /device:TPU:8, one launch (start us, length us, event | category | flops | bytes accessed | tf_op | source)
XLA Modules:
  0.0 312.8 jit_solution(5718525770423550669)
XLA Ops:
  10.4 11.2 %pmin.7 = s32[16]{0:T(128)S(1)} all-reduce(s32[16]{0:T(128)S(1)} %select_reduce_fusion.1), channel_id=1, replica_groups=mesh['seq'=16,'batch'=2] {'seq'}, use_global_device_ids=true, to_apply=%region_2.3 | all-reduce | flops 16 | bytes 128 | tf_op jit(solution)/shard_map/pmin | solution.py:101
  24.4 66.8 %all-gather.3.cloned.1.call-done = bf16[2304,2048]{1,0:T(8,128)(2,1)} async-done(((bf16[144,2048]{1,0:T(8,128)(2,1)}), bf16[2304,2048]{1,0:T(8,128)(2,1)}) %all-gather.3.cloned.1.call-update) | async-done | bytes 9437200 | tf_op jit(solution)/shard_map/all_gather | solution.py:80
  91.2 5.2 %fusion.23 = f32[256,2048]{1,0:T(8,128)S(1)} fusion(bf16[2304,2048]{1,0:T(8,128)(2,1)} %all-gather.3.cloned.1.call-done, bf16[1,256,2304]{2,1,0:T(8,128)(2,1)S(1)} %copy-done, f32[2304]{0:T(1024)S(1)} %copy-done.7, f32[256]{0:T(256)S(1)} %add_rsqrt_fusion.1), kind=kOutput, calls=%fused_computation.33 | convolution fusion | flops 2418278400 | bytes 12724224 | tf_op jit(solution)/shard_map/dot_general | solution.py:78
  105.1 195.0 %while.22 = (s32[]{:T(128)}, bf16[256,2,256]{2,0,1:T(8,128)(2,1)}, bf16[256,2,256]{2,0,1:T(8,128)(2,1)S(1)}, f32[256,2,2,256]{3,0,2,1:T(8,128)S(1)}, f32[256,2,2...) while((s32[]{:T(128)}, bf16[256,2,256]{2,0,1:T(8,128)(2,1)}, ...), condition=%wide.region_7.8_spmd.clone, body=%wide.region_5.7_spmd.clone.sunk | while | flops 270402048 | bytes 7492809 | solution.py:124
  105.1 2.2 collective-permute-start
  107.3 2.3 collective-permute-start.1
  109.8 6.6 %collective-permute-done = bf16[256,2,256]{2,0,1:T(8,128)(2,1)S(1)} collective-permute-done((bf16[256,2,256]{2,0,1:T(8,128)(2,1)}, bf16[256,2,256]{2,0,1:T(8,128)(2,1)S(1)}, u32[]{:S(2)}, u32[]{:S(2)}) %collective-permute-start) | collective-permute-done | bytes 262176 | tf_op jit(solution)/shard_map/while/body/eval_jaxpr/ppermute | solution.py:22
  121.6 1.9 collective-permute-start.1
  123.7 10.5 %collective-permute-done = bf16[256,2,256]{2,0,1:T(8,128)(2,1)S(1)} collective-permute-done((bf16[256,2,256]{2,0,1:T(8,128)(2,1)}, bf16[256,2,256]{2,0,1:T(8,128)(2,1)S(1)}, u32[]{:S(2)}, u32[]{:S(2)}) %collective-permute-start) | collective-permute-done | bytes 262176 | tf_op jit(solution)/shard_map/while/body/eval_jaxpr/ppermute | solution.py:22
  136.5 3.8 %collective-permute-done.1 = bf16[256,2,256]{2,0,1:T(8,128)(2,1)S(1)} collective-permute-done((bf16[256,2,256]{2,0,1:T(8,128)(2,1)S(1)}, bf16[256,2,256]{2,0,1:T(8,128)(2,1)S(1)}, u32[]{:S(2)}, u32[]{:S(2)}) %collective-permute-start.1) | collective-permute-done | bytes 262176 | tf_op jit(solution)/shard_map/while/body/eval_jaxpr/ppermute | solution.py:22
  142.7 1.9 collective-permute-start.1
  144.8 6.3 %collective-permute-done = bf16[256,2,256]{2,0,1:T(8,128)(2,1)S(1)} collective-permute-done((bf16[256,2,256]{2,0,1:T(8,128)(2,1)}, bf16[256,2,256]{2,0,1:T(8,128)(2,1)S(1)}, u32[]{:S(2)}, u32[]{:S(2)}) %collective-permute-start) | collective-permute-done | bytes 262176 | tf_op jit(solution)/shard_map/while/body/eval_jaxpr/ppermute | solution.py:22
  156.4 1.9 collective-permute-start.1
  158.5 4.8 %collective-permute-done = bf16[256,2,256]{2,0,1:T(8,128)(2,1)S(1)} collective-permute-done((bf16[256,2,256]{2,0,1:T(8,128)(2,1)}, bf16[256,2,256]{2,0,1:T(8,128)(2,1)S(1)}, u32[]{:S(2)}, u32[]{:S(2)}) %collective-permute-start) | collective-permute-done | bytes 262176 | tf_op jit(solution)/shard_map/while/body/eval_jaxpr/ppermute | solution.py:22
  168.5 1.9 collective-permute-start.1
  170.6 4.8 %collective-permute-done = bf16[256,2,256]{2,0,1:T(8,128)(2,1)S(1)} collective-permute-done((bf16[256,2,256]{2,0,1:T(8,128)(2,1)}, bf16[256,2,256]{2,0,1:T(8,128)(2,1)S(1)}, u32[]{:S(2)}, u32[]{:S(2)}) %collective-permute-start) | collective-permute-done | bytes 262176 | tf_op jit(solution)/shard_map/while/body/eval_jaxpr/ppermute | solution.py:22
  180.7 1.9 collective-permute-start.1
  182.8 4.8 %collective-permute-done = bf16[256,2,256]{2,0,1:T(8,128)(2,1)S(1)} collective-permute-done((bf16[256,2,256]{2,0,1:T(8,128)(2,1)}, bf16[256,2,256]{2,0,1:T(8,128)(2,1)S(1)}, u32[]{:S(2)}, u32[]{:S(2)}) %collective-permute-start) | collective-permute-done | bytes 262176 | tf_op jit(solution)/shard_map/while/body/eval_jaxpr/ppermute | solution.py:22
  192.8 1.9 collective-permute-start.1
  194.9 4.8 %collective-permute-done = bf16[256,2,256]{2,0,1:T(8,128)(2,1)S(1)} collective-permute-done((bf16[256,2,256]{2,0,1:T(8,128)(2,1)}, bf16[256,2,256]{2,0,1:T(8,128)(2,1)S(1)}, u32[]{:S(2)}, u32[]{:S(2)}) %collective-permute-start) | collective-permute-done | bytes 262176 | tf_op jit(solution)/shard_map/while/body/eval_jaxpr/ppermute | solution.py:22
  207.1 4.8 %collective-permute-done = bf16[256,2,256]{2,0,1:T(8,128)(2,1)S(1)} collective-permute-done((bf16[256,2,256]{2,0,1:T(8,128)(2,1)}, bf16[256,2,256]{2,0,1:T(8,128)(2,1)S(1)}, u32[]{:S(2)}, u32[]{:S(2)}) %collective-permute-start) | collective-permute-done | bytes 262176 | tf_op jit(solution)/shard_map/while/body/eval_jaxpr/ppermute | solution.py:22
  219.2 4.8 %collective-permute-done = bf16[256,2,256]{2,0,1:T(8,128)(2,1)S(1)} collective-permute-done((bf16[256,2,256]{2,0,1:T(8,128)(2,1)}, bf16[256,2,256]{2,0,1:T(8,128)(2,1)S(1)}, u32[]{:S(2)}, u32[]{:S(2)}) %collective-permute-start) | collective-permute-done | bytes 262176 | tf_op jit(solution)/shard_map/while/body/eval_jaxpr/ppermute | solution.py:22
  231.3 4.8 %collective-permute-done = bf16[256,2,256]{2,0,1:T(8,128)(2,1)S(1)} collective-permute-done((bf16[256,2,256]{2,0,1:T(8,128)(2,1)}, bf16[256,2,256]{2,0,1:T(8,128)(2,1)S(1)}, u32[]{:S(2)}, u32[]{:S(2)}) %collective-permute-start) | collective-permute-done | bytes 262176 | tf_op jit(solution)/shard_map/while/body/eval_jaxpr/ppermute | solution.py:22
  241.4 1.9 collective-permute-start.1
  243.5 4.8 %collective-permute-done = bf16[256,2,256]{2,0,1:T(8,128)(2,1)S(1)} collective-permute-done((bf16[256,2,256]{2,0,1:T(8,128)(2,1)}, bf16[256,2,256]{2,0,1:T(8,128)(2,1)S(1)}, u32[]{:S(2)}, u32[]{:S(2)}) %collective-permute-start) | collective-permute-done | bytes 262176 | tf_op jit(solution)/shard_map/while/body/eval_jaxpr/ppermute | solution.py:22
  253.5 1.9 collective-permute-start.1
  255.6 4.8 %collective-permute-done = bf16[256,2,256]{2,0,1:T(8,128)(2,1)S(1)} collective-permute-done((bf16[256,2,256]{2,0,1:T(8,128)(2,1)}, bf16[256,2,256]{2,0,1:T(8,128)(2,1)S(1)}, u32[]{:S(2)}, u32[]{:S(2)}) %collective-permute-start) | collective-permute-done | bytes 262176 | tf_op jit(solution)/shard_map/while/body/eval_jaxpr/ppermute | solution.py:22
  265.7 1.9 collective-permute-start.1
  267.8 4.8 %collective-permute-done = bf16[256,2,256]{2,0,1:T(8,128)(2,1)S(1)} collective-permute-done((bf16[256,2,256]{2,0,1:T(8,128)(2,1)}, bf16[256,2,256]{2,0,1:T(8,128)(2,1)S(1)}, u32[]{:S(2)}, u32[]{:S(2)}) %collective-permute-start) | collective-permute-done | bytes 262176 | tf_op jit(solution)/shard_map/while/body/eval_jaxpr/ppermute | solution.py:22
  279.9 4.8 %collective-permute-done = bf16[256,2,256]{2,0,1:T(8,128)(2,1)S(1)} collective-permute-done((bf16[256,2,256]{2,0,1:T(8,128)(2,1)}, bf16[256,2,256]{2,0,1:T(8,128)(2,1)S(1)}, u32[]{:S(2)}, u32[]{:S(2)}) %collective-permute-start) | collective-permute-done | bytes 262176 | tf_op jit(solution)/shard_map/while/body/eval_jaxpr/ppermute | solution.py:22
  292.1 4.8 %collective-permute-done = bf16[256,2,256]{2,0,1:T(8,128)(2,1)S(1)} collective-permute-done((bf16[256,2,256]{2,0,1:T(8,128)(2,1)}, bf16[256,2,256]{2,0,1:T(8,128)(2,1)S(1)}, u32[]{:S(2)}, u32[]{:S(2)}) %collective-permute-start) | collective-permute-done | bytes 262176 | tf_op jit(solution)/shard_map/while/body/eval_jaxpr/ppermute | solution.py:22
  300.6 3.9 %multiply_reduce_fusion = (f32[256]{0:T(256)S(1)}, f32[256,2304]{1,0:T(8,128)S(1)}) fusion(bf16[256,1024]{0,1:T(8,128)(2,1)S(1)} %bitcast.66, bf16[1024,2304]{1,0:T(8,128)(2,1)} %all-gather.5.cloned.1.call-done), kind=kOutput, calls=%fused_computation.24 | convolution fusion | flops 1209138944 | bytes 7603200 | tf_op jit(solution)/shard_map/dot_general | solution.py:131
  (188 shorter events, 104.9 us)
Async XLA Ops:
  6.5 84.7 %all-gather.3.cloned.1.call-start = ((), (), s32[]{:S(2)}) async-start(), calls=%async_computation | async-start | bytes 10027008 | tf_op jit(solution)/shard_map/all_gather | solution.py:80
  7.3 293.4 %all-gather.5.cloned.1.call-start = ((), (), s32[]{:S(2)}) async-start(), calls=%async_computation.1 | async-start | bytes 5013504 | tf_op jit(solution)/shard_map/all_gather | solution.py:133
  105.1 11.2 %collective-permute-start = (bf16[256,2,256]{2,0,1:T(8,128)(2,1)}, bf16[256,2,256]{2,0,1:T(8,128)(2,1)S(1)}, u32[]{:S(2)}, u32[]{:S(2)}) collective-permute-start(bf16[256,2,256]{2,0,1:T(8,128)(2,1)} %get-tuple-element.355), channel_id=1, source_target_pairs={{0,2},{2,4},{4,6},{6,8},{8,10},{10,12},{12,14},{14,16},{16,18},{18... | collective-permute-start | bytes 786440 | tf_op jit(solution)/shard_map/while/body/eval_jaxpr/ppermute | solution.py:22
  107.3 11.9 %collective-permute-start.1 = (bf16[256,2,256]{2,0,1:T(8,128)(2,1)S(1)}, bf16[256,2,256]{2,0,1:T(8,128)(2,1)S(1)}, u32[]{:S(2)}, u32[]{:S(2)}) collective-permute-start(bf16[256,2,256]{2,0,1:T(8,128)(2,1)S(1)} %get-tuple-element.356), channel_id=1, source_target_pairs={{0,2},{2,4},{4,6},{6,8},{8,10},{10,12},{12,14},{14,16},{16,18},{18... | collective-permute-start | bytes 786440 | tf_op jit(solution)/shard_map/while/body/eval_jaxpr/ppermute | solution.py:22
  119.7 14.5 %collective-permute-start = (bf16[256,2,256]{2,0,1:T(8,128)(2,1)}, bf16[256,2,256]{2,0,1:T(8,128)(2,1)S(1)}, u32[]{:S(2)}, u32[]{:S(2)}) collective-permute-start(bf16[256,2,256]{2,0,1:T(8,128)(2,1)} %get-tuple-element.355), channel_id=1, source_target_pairs={{0,2},{2,4},{4,6},{6,8},{8,10},{10,12},{12,14},{14,16},{16,18},{18... | collective-permute-start | bytes 786440 | tf_op jit(solution)/shard_map/while/body/eval_jaxpr/ppermute | solution.py:22
  121.6 18.7 %collective-permute-start.1 = (bf16[256,2,256]{2,0,1:T(8,128)(2,1)S(1)}, bf16[256,2,256]{2,0,1:T(8,128)(2,1)S(1)}, u32[]{:S(2)}, u32[]{:S(2)}) collective-permute-start(bf16[256,2,256]{2,0,1:T(8,128)(2,1)S(1)} %get-tuple-element.356), channel_id=1, source_target_pairs={{0,2},{2,4},{4,6},{6,8},{8,10},{10,12},{12,14},{14,16},{16,18},{18... | collective-permute-start | bytes 786440 | tf_op jit(solution)/shard_map/while/body/eval_jaxpr/ppermute | solution.py:22
  140.8 10.3 %collective-permute-start = (bf16[256,2,256]{2,0,1:T(8,128)(2,1)}, bf16[256,2,256]{2,0,1:T(8,128)(2,1)S(1)}, u32[]{:S(2)}, u32[]{:S(2)}) collective-permute-start(bf16[256,2,256]{2,0,1:T(8,128)(2,1)} %get-tuple-element.355), channel_id=1, source_target_pairs={{0,2},{2,4},{4,6},{6,8},{8,10},{10,12},{12,14},{14,16},{16,18},{18... | collective-permute-start | bytes 786440 | tf_op jit(solution)/shard_map/while/body/eval_jaxpr/ppermute | solution.py:22
  142.7 11.2 %collective-permute-start.1 = (bf16[256,2,256]{2,0,1:T(8,128)(2,1)S(1)}, bf16[256,2,256]{2,0,1:T(8,128)(2,1)S(1)}, u32[]{:S(2)}, u32[]{:S(2)}) collective-permute-start(bf16[256,2,256]{2,0,1:T(8,128)(2,1)S(1)} %get-tuple-element.356), channel_id=1, source_target_pairs={{0,2},{2,4},{4,6},{6,8},{8,10},{10,12},{12,14},{14,16},{16,18},{18... | collective-permute-start | bytes 786440 | tf_op jit(solution)/shard_map/while/body/eval_jaxpr/ppermute | solution.py:22
  154.5 8.8 %collective-permute-start = (bf16[256,2,256]{2,0,1:T(8,128)(2,1)}, bf16[256,2,256]{2,0,1:T(8,128)(2,1)S(1)}, u32[]{:S(2)}, u32[]{:S(2)}) collective-permute-start(bf16[256,2,256]{2,0,1:T(8,128)(2,1)} %get-tuple-element.355), channel_id=1, source_target_pairs={{0,2},{2,4},{4,6},{6,8},{8,10},{10,12},{12,14},{14,16},{16,18},{18... | collective-permute-start | bytes 786440 | tf_op jit(solution)/shard_map/while/body/eval_jaxpr/ppermute | solution.py:22
  156.4 9.7 %collective-permute-start.1 = (bf16[256,2,256]{2,0,1:T(8,128)(2,1)S(1)}, bf16[256,2,256]{2,0,1:T(8,128)(2,1)S(1)}, u32[]{:S(2)}, u32[]{:S(2)}) collective-permute-start(bf16[256,2,256]{2,0,1:T(8,128)(2,1)S(1)} %get-tuple-element.356), channel_id=1, source_target_pairs={{0,2},{2,4},{4,6},{6,8},{8,10},{10,12},{12,14},{14,16},{16,18},{18... | collective-permute-start | bytes 786440 | tf_op jit(solution)/shard_map/while/body/eval_jaxpr/ppermute | solution.py:22
  166.6 8.8 %collective-permute-start = (bf16[256,2,256]{2,0,1:T(8,128)(2,1)}, bf16[256,2,256]{2,0,1:T(8,128)(2,1)S(1)}, u32[]{:S(2)}, u32[]{:S(2)}) collective-permute-start(bf16[256,2,256]{2,0,1:T(8,128)(2,1)} %get-tuple-element.355), channel_id=1, source_target_pairs={{0,2},{2,4},{4,6},{6,8},{8,10},{10,12},{12,14},{14,16},{16,18},{18... | collective-permute-start | bytes 786440 | tf_op jit(solution)/shard_map/while/body/eval_jaxpr/ppermute | solution.py:22
  168.5 9.7 %collective-permute-start.1 = (bf16[256,2,256]{2,0,1:T(8,128)(2,1)S(1)}, bf16[256,2,256]{2,0,1:T(8,128)(2,1)S(1)}, u32[]{:S(2)}, u32[]{:S(2)}) collective-permute-start(bf16[256,2,256]{2,0,1:T(8,128)(2,1)S(1)} %get-tuple-element.356), channel_id=1, source_target_pairs={{0,2},{2,4},{4,6},{6,8},{8,10},{10,12},{12,14},{14,16},{16,18},{18... | collective-permute-start | bytes 786440 | tf_op jit(solution)/shard_map/while/body/eval_jaxpr/ppermute | solution.py:22
  178.7 8.8 %collective-permute-start = (bf16[256,2,256]{2,0,1:T(8,128)(2,1)}, bf16[256,2,256]{2,0,1:T(8,128)(2,1)S(1)}, u32[]{:S(2)}, u32[]{:S(2)}) collective-permute-start(bf16[256,2,256]{2,0,1:T(8,128)(2,1)} %get-tuple-element.355), channel_id=1, source_target_pairs={{0,2},{2,4},{4,6},{6,8},{8,10},{10,12},{12,14},{14,16},{16,18},{18... | collective-permute-start | bytes 786440 | tf_op jit(solution)/shard_map/while/body/eval_jaxpr/ppermute | solution.py:22
  180.7 9.7 %collective-permute-start.1 = (bf16[256,2,256]{2,0,1:T(8,128)(2,1)S(1)}, bf16[256,2,256]{2,0,1:T(8,128)(2,1)S(1)}, u32[]{:S(2)}, u32[]{:S(2)}) collective-permute-start(bf16[256,2,256]{2,0,1:T(8,128)(2,1)S(1)} %get-tuple-element.356), channel_id=1, source_target_pairs={{0,2},{2,4},{4,6},{6,8},{8,10},{10,12},{12,14},{14,16},{16,18},{18... | collective-permute-start | bytes 786440 | tf_op jit(solution)/shard_map/while/body/eval_jaxpr/ppermute | solution.py:22
  190.9 8.8 %collective-permute-start = (bf16[256,2,256]{2,0,1:T(8,128)(2,1)}, bf16[256,2,256]{2,0,1:T(8,128)(2,1)S(1)}, u32[]{:S(2)}, u32[]{:S(2)}) collective-permute-start(bf16[256,2,256]{2,0,1:T(8,128)(2,1)} %get-tuple-element.355), channel_id=1, source_target_pairs={{0,2},{2,4},{4,6},{6,8},{8,10},{10,12},{12,14},{14,16},{16,18},{18... | collective-permute-start | bytes 786440 | tf_op jit(solution)/shard_map/while/body/eval_jaxpr/ppermute | solution.py:22
  192.8 9.7 %collective-permute-start.1 = (bf16[256,2,256]{2,0,1:T(8,128)(2,1)S(1)}, bf16[256,2,256]{2,0,1:T(8,128)(2,1)S(1)}, u32[]{:S(2)}, u32[]{:S(2)}) collective-permute-start(bf16[256,2,256]{2,0,1:T(8,128)(2,1)S(1)} %get-tuple-element.356), channel_id=1, source_target_pairs={{0,2},{2,4},{4,6},{6,8},{8,10},{10,12},{12,14},{14,16},{16,18},{18... | collective-permute-start | bytes 786440 | tf_op jit(solution)/shard_map/while/body/eval_jaxpr/ppermute | solution.py:22
  203.0 8.8 %collective-permute-start = (bf16[256,2,256]{2,0,1:T(8,128)(2,1)}, bf16[256,2,256]{2,0,1:T(8,128)(2,1)S(1)}, u32[]{:S(2)}, u32[]{:S(2)}) collective-permute-start(bf16[256,2,256]{2,0,1:T(8,128)(2,1)} %get-tuple-element.355), channel_id=1, source_target_pairs={{0,2},{2,4},{4,6},{6,8},{8,10},{10,12},{12,14},{14,16},{16,18},{18... | collective-permute-start | bytes 786440 | tf_op jit(solution)/shard_map/while/body/eval_jaxpr/ppermute | solution.py:22
  205.0 9.7 %collective-permute-start.1 = (bf16[256,2,256]{2,0,1:T(8,128)(2,1)S(1)}, bf16[256,2,256]{2,0,1:T(8,128)(2,1)S(1)}, u32[]{:S(2)}, u32[]{:S(2)}) collective-permute-start(bf16[256,2,256]{2,0,1:T(8,128)(2,1)S(1)} %get-tuple-element.356), channel_id=1, source_target_pairs={{0,2},{2,4},{4,6},{6,8},{8,10},{10,12},{12,14},{14,16},{16,18},{18... | collective-permute-start | bytes 786440 | tf_op jit(solution)/shard_map/while/body/eval_jaxpr/ppermute | solution.py:22
  215.2 8.8 %collective-permute-start = (bf16[256,2,256]{2,0,1:T(8,128)(2,1)}, bf16[256,2,256]{2,0,1:T(8,128)(2,1)S(1)}, u32[]{:S(2)}, u32[]{:S(2)}) collective-permute-start(bf16[256,2,256]{2,0,1:T(8,128)(2,1)} %get-tuple-element.355), channel_id=1, source_target_pairs={{0,2},{2,4},{4,6},{6,8},{8,10},{10,12},{12,14},{14,16},{16,18},{18... | collective-permute-start | bytes 786440 | tf_op jit(solution)/shard_map/while/body/eval_jaxpr/ppermute | solution.py:22
  217.1 9.7 %collective-permute-start.1 = (bf16[256,2,256]{2,0,1:T(8,128)(2,1)S(1)}, bf16[256,2,256]{2,0,1:T(8,128)(2,1)S(1)}, u32[]{:S(2)}, u32[]{:S(2)}) collective-permute-start(bf16[256,2,256]{2,0,1:T(8,128)(2,1)S(1)} %get-tuple-element.356), channel_id=1, source_target_pairs={{0,2},{2,4},{4,6},{6,8},{8,10},{10,12},{12,14},{14,16},{16,18},{18... | collective-permute-start | bytes 786440 | tf_op jit(solution)/shard_map/while/body/eval_jaxpr/ppermute | solution.py:22
  227.3 8.8 %collective-permute-start = (bf16[256,2,256]{2,0,1:T(8,128)(2,1)}, bf16[256,2,256]{2,0,1:T(8,128)(2,1)S(1)}, u32[]{:S(2)}, u32[]{:S(2)}) collective-permute-start(bf16[256,2,256]{2,0,1:T(8,128)(2,1)} %get-tuple-element.355), channel_id=1, source_target_pairs={{0,2},{2,4},{4,6},{6,8},{8,10},{10,12},{12,14},{14,16},{16,18},{18... | collective-permute-start | bytes 786440 | tf_op jit(solution)/shard_map/while/body/eval_jaxpr/ppermute | solution.py:22
  229.2 9.7 %collective-permute-start.1 = (bf16[256,2,256]{2,0,1:T(8,128)(2,1)S(1)}, bf16[256,2,256]{2,0,1:T(8,128)(2,1)S(1)}, u32[]{:S(2)}, u32[]{:S(2)}) collective-permute-start(bf16[256,2,256]{2,0,1:T(8,128)(2,1)S(1)} %get-tuple-element.356), channel_id=1, source_target_pairs={{0,2},{2,4},{4,6},{6,8},{8,10},{10,12},{12,14},{14,16},{16,18},{18... | collective-permute-start | bytes 786440 | tf_op jit(solution)/shard_map/while/body/eval_jaxpr/ppermute | solution.py:22
  239.5 8.8 %collective-permute-start = (bf16[256,2,256]{2,0,1:T(8,128)(2,1)}, bf16[256,2,256]{2,0,1:T(8,128)(2,1)S(1)}, u32[]{:S(2)}, u32[]{:S(2)}) collective-permute-start(bf16[256,2,256]{2,0,1:T(8,128)(2,1)} %get-tuple-element.355), channel_id=1, source_target_pairs={{0,2},{2,4},{4,6},{6,8},{8,10},{10,12},{12,14},{14,16},{16,18},{18... | collective-permute-start | bytes 786440 | tf_op jit(solution)/shard_map/while/body/eval_jaxpr/ppermute | solution.py:22
  241.4 9.7 %collective-permute-start.1 = (bf16[256,2,256]{2,0,1:T(8,128)(2,1)S(1)}, bf16[256,2,256]{2,0,1:T(8,128)(2,1)S(1)}, u32[]{:S(2)}, u32[]{:S(2)}) collective-permute-start(bf16[256,2,256]{2,0,1:T(8,128)(2,1)S(1)} %get-tuple-element.356), channel_id=1, source_target_pairs={{0,2},{2,4},{4,6},{6,8},{8,10},{10,12},{12,14},{14,16},{16,18},{18... | collective-permute-start | bytes 786440 | tf_op jit(solution)/shard_map/while/body/eval_jaxpr/ppermute | solution.py:22
  251.6 8.8 %collective-permute-start = (bf16[256,2,256]{2,0,1:T(8,128)(2,1)}, bf16[256,2,256]{2,0,1:T(8,128)(2,1)S(1)}, u32[]{:S(2)}, u32[]{:S(2)}) collective-permute-start(bf16[256,2,256]{2,0,1:T(8,128)(2,1)} %get-tuple-element.355), channel_id=1, source_target_pairs={{0,2},{2,4},{4,6},{6,8},{8,10},{10,12},{12,14},{14,16},{16,18},{18... | collective-permute-start | bytes 786440 | tf_op jit(solution)/shard_map/while/body/eval_jaxpr/ppermute | solution.py:22
  253.5 9.7 %collective-permute-start.1 = (bf16[256,2,256]{2,0,1:T(8,128)(2,1)S(1)}, bf16[256,2,256]{2,0,1:T(8,128)(2,1)S(1)}, u32[]{:S(2)}, u32[]{:S(2)}) collective-permute-start(bf16[256,2,256]{2,0,1:T(8,128)(2,1)S(1)} %get-tuple-element.356), channel_id=1, source_target_pairs={{0,2},{2,4},{4,6},{6,8},{8,10},{10,12},{12,14},{14,16},{16,18},{18... | collective-permute-start | bytes 786440 | tf_op jit(solution)/shard_map/while/body/eval_jaxpr/ppermute | solution.py:22
  263.7 8.8 %collective-permute-start = (bf16[256,2,256]{2,0,1:T(8,128)(2,1)}, bf16[256,2,256]{2,0,1:T(8,128)(2,1)S(1)}, u32[]{:S(2)}, u32[]{:S(2)}) collective-permute-start(bf16[256,2,256]{2,0,1:T(8,128)(2,1)} %get-tuple-element.355), channel_id=1, source_target_pairs={{0,2},{2,4},{4,6},{6,8},{8,10},{10,12},{12,14},{14,16},{16,18},{18... | collective-permute-start | bytes 786440 | tf_op jit(solution)/shard_map/while/body/eval_jaxpr/ppermute | solution.py:22
  265.7 9.7 %collective-permute-start.1 = (bf16[256,2,256]{2,0,1:T(8,128)(2,1)S(1)}, bf16[256,2,256]{2,0,1:T(8,128)(2,1)S(1)}, u32[]{:S(2)}, u32[]{:S(2)}) collective-permute-start(bf16[256,2,256]{2,0,1:T(8,128)(2,1)S(1)} %get-tuple-element.356), channel_id=1, source_target_pairs={{0,2},{2,4},{4,6},{6,8},{8,10},{10,12},{12,14},{14,16},{16,18},{18... | collective-permute-start | bytes 786440 | tf_op jit(solution)/shard_map/while/body/eval_jaxpr/ppermute | solution.py:22
  275.9 8.8 %collective-permute-start = (bf16[256,2,256]{2,0,1:T(8,128)(2,1)}, bf16[256,2,256]{2,0,1:T(8,128)(2,1)S(1)}, u32[]{:S(2)}, u32[]{:S(2)}) collective-permute-start(bf16[256,2,256]{2,0,1:T(8,128)(2,1)} %get-tuple-element.355), channel_id=1, source_target_pairs={{0,2},{2,4},{4,6},{6,8},{8,10},{10,12},{12,14},{14,16},{16,18},{18... | collective-permute-start | bytes 786440 | tf_op jit(solution)/shard_map/while/body/eval_jaxpr/ppermute | solution.py:22
  277.8 9.7 %collective-permute-start.1 = (bf16[256,2,256]{2,0,1:T(8,128)(2,1)S(1)}, bf16[256,2,256]{2,0,1:T(8,128)(2,1)S(1)}, u32[]{:S(2)}, u32[]{:S(2)}) collective-permute-start(bf16[256,2,256]{2,0,1:T(8,128)(2,1)S(1)} %get-tuple-element.356), channel_id=1, source_target_pairs={{0,2},{2,4},{4,6},{6,8},{8,10},{10,12},{12,14},{14,16},{16,18},{18... | collective-permute-start | bytes 786440 | tf_op jit(solution)/shard_map/while/body/eval_jaxpr/ppermute | solution.py:22
  288.0 8.8 %collective-permute-start = (bf16[256,2,256]{2,0,1:T(8,128)(2,1)}, bf16[256,2,256]{2,0,1:T(8,128)(2,1)S(1)}, u32[]{:S(2)}, u32[]{:S(2)}) collective-permute-start(bf16[256,2,256]{2,0,1:T(8,128)(2,1)} %get-tuple-element.355), channel_id=1, source_target_pairs={{0,2},{2,4},{4,6},{6,8},{8,10},{10,12},{12,14},{14,16},{16,18},{18... | collective-permute-start | bytes 786440 | tf_op jit(solution)/shard_map/while/body/eval_jaxpr/ppermute | solution.py:22
  290.0 9.7 %collective-permute-start.1 = (bf16[256,2,256]{2,0,1:T(8,128)(2,1)S(1)}, bf16[256,2,256]{2,0,1:T(8,128)(2,1)S(1)}, u32[]{:S(2)}, u32[]{:S(2)}) collective-permute-start(bf16[256,2,256]{2,0,1:T(8,128)(2,1)S(1)} %get-tuple-element.356), channel_id=1, source_target_pairs={{0,2},{2,4},{4,6},{6,8},{8,10},{10,12},{12,14},{14,16},{16,18},{18... | collective-permute-start | bytes 786440 | tf_op jit(solution)/shard_map/while/body/eval_jaxpr/ppermute | solution.py:22
  (8 other events, 182.5 us)
Sparse Core Ops, SparseCore 0:
  9.6 81.5 all-gather.2
  93.5 57.7 all-gather.4
where the time goes:
time: 315 us; the launch traced here: 313 us
  waiting for transfers between devices  160 us (51%)
  starting transfers between devices  58.3 us (19%)
  matrix products  40.8 us (13%)
  local copies, waits for them, and re-layouts  15.9 us (5%)
  between operations  13.6 us (4%)
  other arithmetic  12 us (4%)
  blocking collectives  11.2 us (4%)
    ppermute x30, waiting for transfers between devices, from_behind(): return lax.ppermute(block, axis, route)  91.7 us
    all_gather x1, waiting for transfers between devices, per_device(): lax.all_gather(w_qkv, 'seq', axis=0, tiled=True)  66.8 us
    ppermute x30, starting transfers between devices, from_behind(): return lax.ppermute(block, axis, route)  58.2 us
    dot_general x16, matrix products, attend(): jnp.einsum('qhgd,khd->qhgk', queries, key_block, preferred_element_type=j...  24 us
    pmin x1, blocking collectives, per_device(): first_pos = lax.pmin(local_first, 'seq')  11.2 us
    while x30, local copies, waits for them, and re-layouts  10.8 us
    dot_general x16, matrix products, attend(): jnp.einsum('qhgk,khd->qhgd', weights.astype(jnp.bfloat16), value_block, p...  7.7 us
  transfers between devices with their start and end apart: 32, of which 31 were waited for; matrix products, arithmetic and copies ran while one was open for 20% of the time, Pallas kernels for 0%

commit v1 on v0

--- a/solution.py
+++ b/solution.py
@@ -105,7 +105,8 @@
         jnp.zeros((tok_rows, KV_HEADS, groups), jnp.float32),
     )
     states = attend(states, queries, key_rows, value_rows, positions, positions, starts)
-    hop_count = min(WINDOW // tok_rows, seq_count - 1)
+    longest = min(2 * seq_count * tok_rows // DOCS, WINDOW)
+    hop_count = min(-(-(longest - 1) // tok_rows), seq_count - 1)
 
     def relay_step(hop_index, carried):
         moving_keys, moving_values, running, totals = carried

time: 315 us -> 165 us (0.52)
  the two profiles are of different devices: /device:TPU:8 before, /device:TPU:0 now
where the time goes in v1:
time: 165 us
  waiting for transfers between devices  95.4 us (58%)
  blocking collectives  13.8 us (8%)
  starting transfers between devices  13.7 us (8%)
  between operations  13.6 us (8%)
  matrix products  12 us (7%)
  other arithmetic  8.59 us (5%)
  local copies, waits for them, and re-layouts  7.49 us (5%)
    all_gather x1, waiting for transfers between devices, per_device(): lax.all_gather(w_qkv, 'seq', axis=0, tiled=True)  67 us
    all_gather x1, waiting for transfers between devices, per_device(): lax.all_gather(w_out, 'seq', axis=0, tiled=True)  25.8 us
    pmin x1, blocking collectives, per_device(): first_pos = lax.pmin(local_first, 'seq')  13.8 us
    ppermute x4, starting transfers between devices, from_behind(): return lax.ppermute(block, axis, route)  13.6 us
    dot_general x1, matrix products, per_device(): jnp.dot(columns, lax.all_gather(w_qkv, 'seq', axis=0, tiled=True), prefer...  5.24 us
    dot_general x1, matrix products, per_device(): jnp.dot(columns, lax.all_gather(w_out, 'seq', axis=0, tiled=True), prefer...  3.88 us
  transfers between devices with their start and end apart: 6, of which 4 were waited for; matrix products, arithmetic and copies ran while one was open for 14% of the time, Pallas kernels for 0%

profile of v1, /device:TPU:0, one launch (start us, length us, event | category | flops | bytes accessed | tf_op | source)
XLA Modules:
  0.0 164.7 jit_solution(15084624760372904378)
XLA Ops:
  6.5 0.7 all-gather.3.cloned.1.call-update
  7.3 0.7 all-gather.5.cloned.1.call-update
  8.0 0.8 select_reduce_fusion.1
  8.8 13.8 %pmin.7 = s32[16]{0:T(128)S(1)} all-reduce(s32[16]{0:T(128)S(1)} %select_reduce_fusion.1), channel_id=1, replica_groups=mesh['seq'=16,'batch'=2] {'seq'}, use_global_device_ids=true, to_apply=%region_2.3 | all-reduce | flops 16 | bytes 128 | tf_op jit(solution)/shard_map/pmin | solution.py:101
  22.6 0.8 select_reduce_fusion
  23.4 1.6 fusion.13
  25.0 0.8 fusion.32
  25.7 0.5 multiply_cosine_fusion
  26.3 67.0 %all-gather.3.cloned.1.call-done = bf16[2304,2048]{1,0:T(8,128)(2,1)} async-done(((bf16[144,2048]{1,0:T(8,128)(2,1)}), bf16[2304,2048]{1,0:T(8,128)(2,1)}) %all-gather.3.cloned.1.call-update) | async-done | bytes 9437200 | tf_op jit(solution)/shard_map/all_gather | solution.py:80
  93.3 5.2 %fusion.23 = f32[256,2048]{1,0:T(8,128)S(1)} fusion(bf16[2304,2048]{1,0:T(8,128)(2,1)} %all-gather.3.cloned.1.call-done, bf16[1,256,2304]{2,1,0:T(8,128)(2,1)S(1)} %copy-done, f32[2304]{0:T(1024)S(1)} %copy-done.9, f32[256]{0:T(256)S(1)} %add_rsqrt_fusion.1), kind=kOutput, calls=%fused_computation.33 | convolution fusion | flops 2418278400 | bytes 12724224 | tf_op jit(solution)/shard_map/dot_general | solution.py:78
  98.7 1.1 reshape.306
  99.9 0.8 convert_element_type.46
  100.6 0.7 copy.60
  101.3 0.9 reshape.307
  102.2 1.1 fusion.36
  104.2 0.5 fusion.37
  105.5 1.0 pad_maximum_fusion.1
  106.5 1.0 pad_maximum_fusion
  107.5 18.7 %while.22 = (s32[]{:T(128)}, bf16[256,2,256]{2,0,1:T(8,128)(2,1)S(1)}, bf16[256,2,256]{2,0,1:T(8,128)(2,1)}, f32[256,2,2,256]{3,0,2,1:T(8,128)S(1)}, f32[256,2,2...) while((s32[]{:T(128)}, ...), condition=%wide.region_7.8_spmd.clone, body=%wide.region_5.7_spmd.clone.sunk | while | flops 270402048 | bytes 7492809 | solution.py:125
  107.5 2.2 %collective-permute-start = (bf16[256,2,256]{2,0,1:T(8,128)(2,1)S(1)}, bf16[256,2,256]{2,0,1:T(8,128)(2,1)S(1)}, u32[]{:S(2)}, u32[]{:S(2)}) collective-permute-start(bf16[256,2,256]{2,0,1:T(8,128)(2,1)S(1)} %get-tuple-element.355), channel_id=1, source_target_pairs={{0,2},{2,4},{4,6},{6,8},{8,10},{10,12},{12,14},{14,16},{16,18},{18... | collective-permute-start | bytes 786440 | tf_op jit(solution)/shard_map/while/body/eval_jaxpr/ppermute | solution.py:22
  109.7 2.3 %collective-permute-start.1 = (bf16[256,2,256]{2,0,1:T(8,128)(2,1)}, bf16[256,2,256]{2,0,1:T(8,128)(2,1)S(1)}, u32[]{:S(2)}, u32[]{:S(2)}) collective-permute-start(bf16[256,2,256]{2,0,1:T(8,128)(2,1)} %get-tuple-element.356), channel_id=1, source_target_pairs={{0,2},{2,4},{4,6},{6,8},{8,10},{10,12},{12,14},{14,16},{16,18},{18... | collective-permute-start | bytes 786440 | tf_op jit(solution)/shard_map/while/body/eval_jaxpr/ppermute | solution.py:22
  112.2 0.5 fusion.54
  112.8 0.6 collective-permute-done.1
  113.4 0.7 copy.73
  114.6 4.9 %collective-permute-start = (bf16[256,2,256]{2,0,1:T(8,128)(2,1)S(1)}, bf16[256,2,256]{2,0,1:T(8,128)(2,1)S(1)}, u32[]{:S(2)}, u32[]{:S(2)}) collective-permute-start(bf16[256,2,256]{2,0,1:T(8,128)(2,1)S(1)} %get-tuple-element.355), channel_id=1, source_target_pairs={{0,2},{2,4},{4,6},{6,8},{8,10},{10,12},{12,14},{14,16},{16,18},{18... | collective-permute-start | bytes 786440 | tf_op jit(solution)/shard_map/while/body/eval_jaxpr/ppermute | solution.py:22
  119.4 4.3 %collective-permute-start.1 = (bf16[256,2,256]{2,0,1:T(8,128)(2,1)}, bf16[256,2,256]{2,0,1:T(8,128)(2,1)S(1)}, u32[]{:S(2)}, u32[]{:S(2)}) collective-permute-start(bf16[256,2,256]{2,0,1:T(8,128)(2,1)} %get-tuple-element.356), channel_id=1, source_target_pairs={{0,2},{2,4},{4,6},{6,8},{8,10},{10,12},{12,14},{14,16},{16,18},{18... | collective-permute-start | bytes 786440 | tf_op jit(solution)/shard_map/while/body/eval_jaxpr/ppermute | solution.py:22
  123.9 0.5 fusion.54
  124.5 0.6 collective-permute-done.1
  125.1 0.7 copy.73
  126.7 25.8 %all-gather.5.cloned.1.call-done = bf16[1024,2304]{1,0:T(8,128)(2,1)} async-done(((bf16[64,2304]{1,0:T(8,128)(2,1)}), bf16[1024,2304]{1,0:T(8,128)(2,1)}) %all-gather.5.cloned.1.call-update) | async-done | bytes 4718608 | tf_op jit(solution)/shard_map/all_gather | solution.py:134
  152.5 3.9 %multiply_reduce_fusion = (f32[256]{0:T(256)S(1)}, f32[256,2304]{1,0:T(8,128)S(1)}) fusion(bf16[256,1024]{0,1:T(8,128)(2,1)S(1)} %bitcast.66, bf16[1024,2304]{1,0:T(8,128)(2,1)} %all-gather.5.cloned.1.call-done), kind=kOutput, calls=%fused_computation.24 | convolution fusion | flops 1209138944 | bytes 7603200 | tf_op jit(solution)/shard_map/dot_general | solution.py:132
  156.4 1.5 fusion.22
  (49 shorter events, 3.5 us)
Async XLA Ops:
  6.5 86.7 %copy-start = (bf16[1,256,2304]{2,1,0:T(8,128)(2,1)S(1)}, bf16[1,256,2304]{2,1,0:T(8,128)(2,1)}, u32[]{:S(2)}) copy-start(bf16[1,256,2304]{2,1,0:T(8,128)(2,1)} %param.8) | copy-start | bytes 3538948
  6.5 86.7 %copy-start.9 = (f32[2304]{0:T(1024)S(1)}, f32[2304]{0:T(1024)}, u32[]{:S(2)}) copy-start(f32[2304]{0:T(1024)} %param.10) | copy-start | bytes 27652
  6.5 86.7 %all-gather.3.cloned.1.call-start = ((), (), s32[]{:S(2)}) async-start(), calls=%async_computation | async-start | bytes 10027008 | tf_op jit(solution)/shard_map/all_gather | solution.py:80
  7.3 145.3 %all-gather.5.cloned.1.call-start = ((), (), s32[]{:S(2)}) async-start(), calls=%async_computation.1 | async-start | bytes 5013504 | tf_op jit(solution)/shard_map/all_gather | solution.py:134
  103.3 0.8 copy-start.7
  103.4 1.3 copy-start.6
  103.4 1.3 copy-start.5
  103.8 1.0 copy-start.1
  104.0 0.7 copy-start.2
  104.0 0.8 copy-start.4
  105.1 1.4 copy-start.3
  107.5 4.7 %collective-permute-start = (bf16[256,2,256]{2,0,1:T(8,128)(2,1)S(1)}, bf16[256,2,256]{2,0,1:T(8,128)(2,1)S(1)}, u32[]{:S(2)}, u32[]{:S(2)}) collective-permute-start(bf16[256,2,256]{2,0,1:T(8,128)(2,1)S(1)} %get-tuple-element.355), channel_id=1, source_target_pairs={{0,2},{2,4},{4,6},{6,8},{8,10},{10,12},{12,14},{14,16},{16,18},{18... | collective-permute-start | bytes 786440 | tf_op jit(solution)/shard_map/while/body/eval_jaxpr/ppermute | solution.py:22
  109.7 3.6 %collective-permute-start.1 = (bf16[256,2,256]{2,0,1:T(8,128)(2,1)}, bf16[256,2,256]{2,0,1:T(8,128)(2,1)S(1)}, u32[]{:S(2)}, u32[]{:S(2)}) collective-permute-start(bf16[256,2,256]{2,0,1:T(8,128)(2,1)} %get-tuple-element.356), channel_id=1, source_target_pairs={{0,2},{2,4},{4,6},{6,8},{8,10},{10,12},{12,14},{14,16},{16,18},{18... | collective-permute-start | bytes 786440 | tf_op jit(solution)/shard_map/while/body/eval_jaxpr/ppermute | solution.py:22
  114.6 9.3 %collective-permute-start = (bf16[256,2,256]{2,0,1:T(8,128)(2,1)S(1)}, bf16[256,2,256]{2,0,1:T(8,128)(2,1)S(1)}, u32[]{:S(2)}, u32[]{:S(2)}) collective-permute-start(bf16[256,2,256]{2,0,1:T(8,128)(2,1)S(1)} %get-tuple-element.355), channel_id=1, source_target_pairs={{0,2},{2,4},{4,6},{6,8},{8,10},{10,12},{12,14},{14,16},{16,18},{18... | collective-permute-start | bytes 786440 | tf_op jit(solution)/shard_map/while/body/eval_jaxpr/ppermute | solution.py:22
  119.4 5.6 %collective-permute-start.1 = (bf16[256,2,256]{2,0,1:T(8,128)(2,1)}, bf16[256,2,256]{2,0,1:T(8,128)(2,1)S(1)}, u32[]{:S(2)}, u32[]{:S(2)}) collective-permute-start(bf16[256,2,256]{2,0,1:T(8,128)(2,1)} %get-tuple-element.356), channel_id=1, source_target_pairs={{0,2},{2,4},{4,6},{6,8},{8,10},{10,12},{12,14},{14,16},{16,18},{18... | collective-permute-start | bytes 786440 | tf_op jit(solution)/shard_map/while/body/eval_jaxpr/ppermute | solution.py:22
  152.5 3.9 %copy-start.8 = (f32[2304]{0:T(1024)S(1)}, f32[2304]{0:T(1024)}, u32[]{:S(2)}) copy-start(f32[2304]{0:T(1024)} %param.13) | copy-start | bytes 27652
Sparse Core Ops, SparseCore 0:
  9.6 83.6 all-gather.2
  95.6 56.9 all-gather.4

commit v2 on v1

--- a/solution.py
+++ b/solution.py
@@ -1,8 +1,11 @@
+import functools
 import math
 
 import jax
 import jax.numpy as jnp
 from jax import lax
+from jax.experimental import pallas as pl
+from jax.experimental.pallas import tpu as pltpu
 from jax.sharding import PartitionSpec as P
 
 Q_HEADS = 4
@@ -10,20 +13,358 @@
 HEAD = 256
 WINDOW = 4096
 DOCS = 16
-
-
 EPS = 1e-06
 CAP = 50.0
+GROUPS = Q_HEADS // KV_HEADS
+
+
+def rms_scale(values, gain):
+    return values * lax.rsqrt(jnp.mean(values * values, axis=-1, keepdims=True) + EPS) * gain
+
+
+def rotary_tables(positions):
+    half_dim = HEAD // 2
+    inverse = 1.0 / 10000.0 ** (jnp.arange(half_dim, dtype=jnp.float32) * 2.0 / HEAD)
+    angles = positions.astype(jnp.float32)[:, None] * inverse[None, :]
+    return jnp.cos(angles), jnp.sin(angles)
+
+
+def swap_core(block):
+    return lax.ppermute(block, "seq", [(i, i ^ 1) for i in range(lax.axis_size("seq"))])
+
+
+def swap_pair(block):
+    return lax.ppermute(block, "seq", [(i, i ^ 2) for i in range(lax.axis_size("seq"))])
+
+
+def swap_batch(block):
+    return lax.ppermute(block, "batch", [(0, 1), (1, 0)])
+
+
+def along_line(block):
+    count = lax.axis_size("seq")
+    return lax.ppermute(block, "seq", [(i, (i + 4) % count) for i in range(count)])
+
+
+def from_chip_behind(block, distance):
+    count = lax.axis_size("seq")
+    return lax.ppermute(
+        block, "seq", [(i, i + 2 * distance) for i in range(count - 2 * distance)]
+    )
+
+
+def gather_wide(mine, rest, line_count):
+    own = jnp.stack([mine, rest])
+    pair_own = swap_pair(own)
+    pieces = [
+        (own, 0, (False, True), (False, False)),
+        (pair_own, 0, (False, True), (True, True)),
+    ]
+    unit = jnp.stack([mine, pair_own[0]])
+    for back in range(1, line_count):
+        unit = along_line(unit)
+        pieces.append((unit, back, (False, False), (False, True)))
+        pieces.append((swap_batch(unit), back, (True, True), (False, True)))
+    return pieces
+
+
+def gather_narrow(mine, rest, line_count):
+    own = jnp.stack([mine, rest])
+    pair_own = swap_pair(own)
+    pieces = [
+        (own, 0, (False, True), (False, False)),
+        (pair_own, 0, (False, True), (True, True)),
+    ]
+    unit = mine
+    for back in range(1, line_count):
+        unit = along_line(unit)
+        other = swap_batch(unit)
+        both = jnp.stack([unit, other])
+        pieces.append((both, back, (False, True), (False, False)))
+        pieces.append((swap_pair(both), back, (False, True), (True, True)))
+    return pieces
+
+
+def project_kernel(where, turned, spots, x_ref, cos_ref, sin_ref, *refs):
+    count = len(where)
+    pieces, out_ref, held, sems = refs[:count], refs[count], refs[count + 1], refs[count + 2]
+    rows = pieces[0].shape[1]
+    copies = []
+    for piece, blocks in zip(pieces, where):
+        for i in range(len(blocks)):
+            at = pl.multiple_of(spots[len(copies)] * rows, rows)
+            copies.append(
+                pltpu.make_async_copy(
+                    piece.at[i], held.at[pl.ds(at, rows), :], sems.at[len(copies)]
+                )
+            )
+            copies[-1].start()
+    for copy in copies:
+        copy.wait()
+    half = HEAD // 2
+    step = 256
+
+    def body(m, carry):
+        tokens = pl.ds(pl.multiple_of(m * step, step), step)
+        full = jnp.dot(x_ref[tokens, :], held[...], preferred_element_type=jnp.float32)
+        cosine, sine = cos_ref[tokens, :], sin_ref[tokens, :]
+        for h, turn in enumerate(turned):
+            a = full[:, h * HEAD : h * HEAD + half]
+            b = full[:, h * HEAD + half : (h + 1) * HEAD]
+            if turn:
+                a, b = a * cosine - b * sine, b * cosine + a * sine
+            out_ref[tokens, h * HEAD : h * HEAD + half] = a.astype(jnp.bfloat16)
+            out_ref[tokens, h * HEAD + half : (h + 1) * HEAD] = b.astype(jnp.bfloat16)
+        return carry
+
+    lax.fori_loop(0, x_ref.shape[0] // step, body, 0)
+
+
+def project(x, cosine, sine, arrays, where, spots, turned):
+    tokens, depth = x.shape
+    width = arrays[0].shape[2]
+    total = sum(len(blocks) for blocks in where)
+    vmem = pl.BlockSpec(memory_space=pltpu.VMEM)
+    return pl.pallas_call(
+        functools.partial(project_kernel, where, turned),
+        out_shape=jax.ShapeDtypeStruct((tokens, width), jnp.bfloat16),
+        in_specs=[pl.BlockSpec(memory_space=pltpu.SMEM), vmem, vmem, vmem]
+        + [pl.BlockSpec(memory_space=pl.ANY)] * len(arrays),
+        out_specs=vmem,
+        scratch_shapes=[
+            pltpu.VMEM((depth, width), jnp.bfloat16),
+            pltpu.SemaphoreType.DMA((total,)),
+        ],
+        compiler_params=pltpu.CompilerParams(vmem_limit_bytes=24 * 1024 * 1024),
+        cost_estimate=pl.CostEstimate(
+            flops=2 * tokens * depth * width, bytes_accessed=2 * depth * width, transcendentals=0
+        ),
+        name="project",
+    )(spots, x, cosine, sine, *arrays)
+
+
+def attend_kernel(behind, q_ref, kv_ref, old_ref, qseg_ref, kseg_ref, out_ref):
+    tokens = q_ref.shape[0]
+    step = out_ref.shape[2]
+    for m in range(tokens // step):
+        low = m * step
+        top = behind + (m + 1) * step
+        span = top - low
+        qpos = behind + m * step + lax.broadcasted_iota(jnp.int32, (step, span), 0)
+        kpos = low + lax.broadcasted_iota(jnp.int32, (step, span), 1)
+        same = qseg_ref[m * step : (m + 1) * step, :] == kseg_ref[:, low:top]
+        allowed = same & (kpos <= qpos) & (qpos - kpos < WINDOW)
+        keys = jnp.concatenate([old_ref[low:, :HEAD], kv_ref[: (m + 1) * step, :HEAD]], axis=0)
+        values = jnp.concatenate([old_ref[low:, HEAD:], kv_ref[: (m + 1) * step, HEAD:]], axis=0)
+        for h in range(GROUPS):
+            q = q_ref[m * step : (m + 1) * step, h * HEAD : (h + 1) * HEAD]
+            scores = lax.dot_general(
+                q, keys, (((1,), (1,)), ((), ())), preferred_element_type=jnp.float32
+            ) * (1.0 / math.sqrt(HEAD))
+            capped = CAP * jnp.tanh(scores / CAP)
+            weights = jnp.where(allowed, jnp.exp(capped), 0.0)
+            totals = jnp.sum(weights, axis=1, keepdims=True)
+            mixed = jnp.dot(
+                weights.astype(jnp.bfloat16), values, preferred_element_type=jnp.float32
+            )
+            out_ref[m, h] = (mixed / totals).astype(jnp.bfloat16)
+
+
+def attend(q, kv, old, qseg, kseg, blocks):
+    tokens = q.shape[0]
+    behind = old.shape[0]
+    work = GROUPS * tokens * (behind + tokens) * HEAD
+    return pl.pallas_call(
+        functools.partial(attend_kernel, behind),
+        out_shape=jax.ShapeDtypeStruct((blocks, GROUPS, tokens // blocks, HEAD), jnp.bfloat16),
+        in_specs=[pl.BlockSpec(memory_space=pltpu.VMEM)] * 5,
+        out_specs=pl.BlockSpec(memory_space=pltpu.VMEM),
+        compiler_params=pltpu.CompilerParams(vmem_limit_bytes=24 * 1024 * 1024),
+        cost_estimate=pl.CostEstimate(flops=4 * work, bytes_accessed=work // 256, transcendentals=0),
+        name="attend",
+    )(q, kv, old, qseg, kseg)
+
+
+def out_kernel(where, heads, last, marks, *refs):
+    refs = list(refs)
+    att_ref = refs.pop(0)
+    if last:
+        early_ref, hid_ref, gain_ref = refs.pop(0), refs.pop(0), refs.pop(0)
+    count = len(where)
+    pieces = refs[:count]
+    out_ref, held, sum_ref, sems = refs[count:]
+    rows = pieces[0].shape[1]
+    copies = []
+    for piece, blocks in zip(pieces, where):
+        for i, slot in enumerate(blocks):
+            at = pl.multiple_of(marks[heads + len(copies)], rows)
+            copies.append(
+                pltpu.make_async_copy(
+                    piece.at[i], held.at[slot, pl.ds(at, rows), :], sems.at[len(copies)]
+                )
+            )
+            copies[-1].start()
+    for copy in copies:
+        copy.wait()
+    width = out_ref.shape[1]
+    tile = next(t for t in (768, 512, 256, 128, width) if width % t == 0)
+    if not last:
+        for n in range(width // tile):
+            part = slice(n * tile, (n + 1) * tile)
+            total = jnp.zeros((out_ref.shape[0], tile), jnp.float32)
+            for s in range(heads):
+                total = total + jnp.dot(
+                    att_ref[marks[s]], held[s, :, part], preferred_element_type=jnp.float32
+                )
+            out_ref[:, part] = total
+        return
+    square = jnp.zeros((out_ref.shape[0], 1), jnp.float32)
+    for n in range(width // tile):
+        part = slice(n * tile, (n + 1) * tile)
+        total = early_ref[:, part]
+        for s in range(heads):
+            total = total + jnp.dot(
+                att_ref[marks[s]], held[s, :, part], preferred_element_type=jnp.float32
+            )
+        sum_ref[:, part] = total
+        square = square + jnp.sum(total * total, axis=1, keepdims=True)
+    scale = lax.rsqrt(square / width + EPS)
+    for n in range(width // tile):
+        part = slice(n * tile, (n + 1) * tile)
+        branch = sum_ref[:, part] * scale * gain_ref[:, part]
+        out_ref[:, part] = (hid_ref[:, part].astype(jnp.float32) + branch).astype(jnp.bfloat16)
+
+
+def out_project(att, arrays, where, marks, heads, rows, finish=None):
+    width = arrays[0].shape[2]
+    tokens = att.shape[1]
+    total = sum(len(blocks) for blocks in where)
+    vmem = pl.BlockSpec(memory_space=pltpu.VMEM)
+    extra = list(finish) if finish else []
+    return pl.pallas_call(
+        functools.partial(out_kernel, where, heads, bool(finish)),
+        out_shape=jax.ShapeDtypeStruct((tokens, width), jnp.bfloat16 if finish else jnp.float32),
+        in_specs=[pl.BlockSpec(memory_space=pltpu.SMEM)]
+        + [vmem] * (1 + len(extra))
+        + [pl.BlockSpec(memory_space=pl.ANY)] * len(arrays),
+        out_specs=vmem,
+        scratch_shapes=[
+            pltpu.VMEM((heads, rows, width), jnp.bfloat16),
+            pltpu.VMEM((tokens, width) if finish else (8, 128), jnp.float32),
+            pltpu.SemaphoreType.DMA((total,)),
+        ],
+        compiler_params=pltpu.CompilerParams(vmem_limit_bytes=24 * 1024 * 1024),
+        cost_estimate=pl.CostEstimate(
+            flops=2 * tokens * rows * heads * width, bytes_accessed=2 * rows * heads * width,
+            transcendentals=0,
+        ),
+        name="finish" if finish else "early",
+    )(marks, att, *extra, *arrays)
+
+
+def per_device(hidden_in, segment_ids, pre_gain, w_qkv, w_out, post_gain):
+    tok_rows, model = hidden_in.shape[1:]
+    seq_count = lax.axis_size("seq")
+    line_count = seq_count // 4
+    seq_index = lax.axis_index("seq")
+    plane = lax.axis_index("batch")
+    core, pair, line = seq_index % 2, (seq_index // 2) % 2, seq_index // 4
+    chip = seq_index // 2
+    chip_rows = 2 * tok_rows
+    on_plane = plane == core
+
+    att_w = Q_HEADS * HEAD
+    group_w = GROUPS * HEAD
+
+    def columns_of(c):
+        return jnp.concatenate(
+            [
+                lax.dynamic_slice_in_dim(w_qkv, att_w + c * HEAD, HEAD, 1),
+                lax.dynamic_slice_in_dim(w_qkv, att_w + (KV_HEADS + c) * HEAD, HEAD, 1),
+                lax.dynamic_slice_in_dim(w_qkv, c * group_w, group_w, 1),
+            ],
+            axis=1,
+        )
+
+    kept = columns_of(core)
+    came = swap_core(columns_of(1 - core))
+    mine = jnp.where(on_plane, kept, came)
+    rest = jnp.where(on_plane, came, kept)
+    kv_pieces = gather_narrow(mine[:, : 2 * HEAD], rest[:, : 2 * HEAD], line_count)
+
+    def by_core(own, other):
+        return jnp.where(
+            core == 0, jnp.concatenate([own, other]), jnp.concatenate([other, own])
+        )
+
+    hidden_chip = by_core(hidden_in[0], swap_core(hidden_in[0]))
+    normed = rms_scale(hidden_chip.astype(jnp.float32), pre_gain).astype(jnp.bfloat16)
+    ids = by_core(segment_ids[0], swap_core(segment_ids[0]))
+    longest = min(2 * seq_count * tok_rows // DOCS, WINDOW)
+    hops = min(-(-(longest - 1) // chip_rows), seq_count // 2 - 1)
+    key_ids = [
+        jnp.where(chip >= d, from_chip_behind(ids, d), -1) for d in range(hops, 0, -1)
+    ] + [ids]
+    cosine, sine = rotary_tables(chip * chip_rows + jnp.arange(chip_rows, dtype=jnp.int32))
+
+    def spot(back, other_half, other_pair):
+        layer = (line - back + line_count) % line_count
+        y = 1 - pair if other_pair else pair
+        h = 1 - plane if other_half else plane
+        return layer, y, h
+
+    def projected(pieces, turned):
+        spots, arrays, where = [], [], []
+        for block, back, halves, pairs in pieces:
+            arrays.append(block)
+            where.append(tuple(range(len(halves))))
+            for half, other in zip(halves, pairs):
+                layer, y, h = spot(back, half, other)
+                spots.append((layer * 2 + y) * 2 + h)
+        spots = jnp.stack(spots).astype(jnp.int32)
+        return project(normed, cosine, sine, arrays, tuple(where), spots, turned)
+
+    q_pieces = gather_wide(mine[:, 2 * HEAD :], rest[:, 2 * HEAD :], line_count)
+    kv = projected(kv_pieces, (True, False))
+    old = jnp.concatenate([from_chip_behind(kv, d) for d in range(hops, 0, -1)])
+
+    half_rows = w_out.shape[0] // 2
+    out_mine = lax.dynamic_slice_in_dim(w_out, plane * half_rows, half_rows, 0)
+    out_rest = lax.dynamic_slice_in_dim(w_out, (1 - plane) * half_rows, half_rows, 0)
+    out_pieces = gather_wide(out_mine, out_rest, line_count)
+
+    q = projected(q_pieces, (True, True))
+    att = attend(q, kv, old, ids[:, None], jnp.concatenate(key_ids)[None, :], 2)
+    att_own = lax.dynamic_index_in_dim(att, core, 0, keepdims=False)
+    att_other = swap_core(lax.dynamic_index_in_dim(att, 1 - core, 0, keepdims=False))
+    att = by_core(att_own, att_other)
+
+    def out_part(backs, finish=None):
+        heads = [(line - back + line_count) % line_count for back in backs]
+        offsets, arrays, where = [], [], []
+        for block, back, halves, pairs in out_pieces:
+            if back not in backs:
+                continue
+            for array, c in ((block, core), (swap_core(block), 1 - core)):
+                arrays.append(array)
+                where.append((backs.index(back),) * len(halves))
+                for half, other in zip(halves, pairs):
+                    _, y, h = spot(back, half, other)
+                    offsets.append(((y * 2 + c) * 2 + h) * half_rows)
+        marks = jnp.stack(heads + offsets).astype(jnp.int32)
+        return out_project(
+            att, arrays, tuple(where), marks, len(backs), 8 * half_rows, finish
+        )
+
+    early = out_part(list(range(line_count - 1)))
+    done = out_part([line_count - 1], (early, hidden_in[0], post_gain[None, :]))
+    return done[None]
 
 
 def from_behind(block, axis, distance):
     devices = range(lax.axis_size(axis))
     route = [(i - distance, i) for i in devices if i - distance in devices]
     return lax.ppermute(block, axis, route)
-
-
-def rms_scale(values, gain):
-    return values * lax.rsqrt(jnp.mean(values * values, axis=-1, keepdims=True) + EPS) * gain
 
 
 def rotary(values, positions, leading):
@@ -44,7 +385,7 @@
     )
 
 
-def attend(states, queries, key_block, value_block, query_pos, key_pos, starts):
+def attend_block(states, queries, key_block, value_block, query_pos, key_pos, starts):
     running, totals = states
     scores = jnp.einsum(
         "qhgd,khd->qhgk", queries, key_block, preferred_element_type=jnp.float32
@@ -66,7 +407,7 @@
     return (running, totals)
 
 
-def per_device(hidden_in, segment_ids, pre_gain, w_qkv, w_out, post_gain):
+def per_device_general(hidden_in, segment_ids, pre_gain, w_qkv, w_out, post_gain):
     tok_rows = hidden_in.shape[1]
     seq_count = lax.axis_size("seq")
     seq_index = lax.axis_index("seq")
@@ -104,14 +445,14 @@
         jnp.zeros((tok_rows, KV_HEADS, groups, HEAD), jnp.float32),
         jnp.zeros((tok_rows, KV_HEADS, groups), jnp.float32),
     )
-    states = attend(states, queries, key_rows, value_rows, positions, positions, starts)
+    states = attend_block(states, queries, key_rows, value_rows, positions, positions, starts)
     longest = min(2 * seq_count * tok_rows // DOCS, WINDOW)
     hop_count = min(-(-(longest - 1) // tok_rows), seq_count - 1)
 
     def relay_step(hop_index, carried):
         moving_keys, moving_values, running, totals = carried
         moving_keys, moving_values = from_behind((moving_keys, moving_values), "seq", 1)
-        running, totals = attend(
+        running, totals = attend_block(
             (running, totals),
             queries,
             moving_keys,
@@ -138,7 +479,13 @@
 
 
 def solution(mesh):
+    seq_count, planes = mesh.shape["seq"], mesh.shape["batch"]
+    special = seq_count == 4 * Q_HEADS and planes == 2 and KV_HEADS == 2
     placed = (P("batch", "seq", None), P("batch", "seq"), P(), P("seq", None), P("seq", None), P())
     return jax.shard_map(
-        per_device, mesh=mesh, in_specs=placed, out_specs=P("batch", "seq", None), check_vma=False
-    )
+        per_device if special else per_device_general,
+        mesh=mesh,
+        in_specs=placed,
+        out_specs=P("batch", "seq", None),
+        check_vma=False,
+    )

time: 165 us -> 119 us (0.72)
  waiting for transfers between devices: 95.4 us -> 47.2 us
  Pallas kernels: 0 us -> 22.5 us
  starting transfers between devices: 13.7 us -> 30.7 us
  blocking collectives: 13.8 us -> 0 us
  between operations: 13.6 us -> 0.58 us
  matrix products: 12 us -> 0 us
  local copies, waits for them, and re-layouts: 7.49 us -> 10.3 us
    all_gather x2 -> x0, waiting for transfers between devices: 92.8 us -> none  [the longest x1 67 us: per_device(): lax.all_gather(w_qkv, 'seq', axis=0, tiled=True)]
    ppermute x4 -> x38, waiting for transfers between devices: 1.18 us -> 47.2 us  [the longest x9 27.2 us: swap_batch(): return lax.ppermute(block, 'batch', [(0, 1), (1, 0)])]
    pallas_call x0 -> x5, Pallas kernels: none -> 22.5 us  [the longest x2 10.8 us: project(): pl.pallas_call(functools.partial(project_kernel, where, turned), out_shap...]
    ppermute x4 -> x38, starting transfers between devices: 13.6 us -> 30.7 us  [the longest x9 11.8 us: swap_batch(): return lax.ppermute(block, 'batch', [(0, 1), (1, 0)])]
    pmin x1 -> x0, blocking collectives: 13.8 us -> none  [per_device(): first_pos = lax.pmin(local_first, 'seq')]
    dot_general x8 -> x0, matrix products: 12 us -> none  [the longest x1 5.24 us: per_device(): jnp.dot(columns, lax.all_gather(w_qkv, 'seq', axis=0, tiled=True), prefer...]
    unnamed x21 -> x22, local copies, waits for them, and re-layouts: 0.58 us -> 5.05 us
    convert_element_type x2, other arithmetic: 0.1 us -> 2.22 us  [the longest x1 2.21 us: per_device(): rms_scale(hidden_chip.astype(jnp.float32), pre_gain).astype(jnp.bfloat16)]
  transfers between devices with their start and end apart: 6 -> 38, of which waited for: 4 -> 14; matrix products, arithmetic and copies ran while one was open for 14% -> 10% of each run, Pallas kernels for 0% -> 15%
where the time goes in v2:
time: 119 us; the launch traced here: 118 us
  waiting for transfers between devices  47.2 us (40%)
  starting transfers between devices  30.7 us (26%)
  Pallas kernels  22.5 us (19%)
  local copies, waits for them, and re-layouts  10.3 us (9%)
  other arithmetic  7.17 us (6%)
    ppermute x9, waiting for transfers between devices, swap_batch(): return lax.ppermute(block, 'batch', [(0, 1), (1, 0)])  27.2 us
    ppermute x9, waiting for transfers between devices, along_line(): lax.ppermute(block, 'seq', [(i, (i + 4) % count) for i in range(count)])  13.1 us
    ppermute x9, starting transfers between devices, swap_batch(): return lax.ppermute(block, 'batch', [(0, 1), (1, 0)])  11.8 us
    pallas_call x2, Pallas kernels, project(): pl.pallas_call(functools.partial(project_kernel, where, turned), out_shap...  10.8 us
    pallas_call x2, Pallas kernels, out_project(): pl.pallas_call(functools.partial(out_kernel, where, heads, bool(finish)),...  10.3 us
    ppermute x6, starting transfers between devices, swap_pair(): lax.ppermute(block, 'seq', [(i, i ^ 2) for i in range(lax.axis_size('seq'...  7.83 us
    ppermute x6, waiting for transfers between devices, swap_pair(): lax.ppermute(block, 'seq', [(i, i ^ 2) for i in range(lax.axis_size('seq'...  6.81 us
    unnamed x22, local copies, waits for them, and re-layouts  5.05 us
  transfers between devices with their start and end apart: 38, of which 14 were waited for; matrix products, arithmetic and copies ran while one was open for 10% of the time, Pallas kernels for 15%

profile of v2, /device:TPU:0, one launch (start us, length us, event | category | flops | bytes accessed | tf_op | source)
XLA Modules:
  0.0 118.4 jit_solution(11505803084586798740)
XLA Ops:
  4.2 2.6 %collective-permute-start.24 = (bf16[2,32,2304]{2,1,0:T(8,128)(2,1)S(1)}, bf16[2,32,2304]{2,1,0:T(8,128)(2,1)S(1)}, u32[]{:S(2)}, u32[]{:S(2)}) collective-permute-start(bf16[2,32,2304]{2,1,0:T(8,128)(2,1)S(1)} %pad_maximum_fusion.3.refs_1_), channel_id=1, source_target_pairs={{0,4},{2,6},{4,0},{6,2},{8,12},{10,14},{12,8},{14,10},{16,20},{18,... | collective-permute-start | bytes 884744 | tf_op jit(solution)/shard_map/ppermute | solution.py:37
  9.4 1.6 %collective-permute-start.10 = (bf16[144,512]{1,0:T(8,128)(2,1)S(1)}, bf16[144,512]{1,0:T(8,128)(2,1)S(1)}, u32[]{:S(2)}, u32[]{:S(2)}) collective-permute-start(bf16[144,512]{1,0:T(8,128)(2,1)S(1)} %get-tuple-element.17), channel_id=1, source_target_pairs={{0,8},{2,10},{4,12},{6,14},{8,16},{10,18},{12,20},{14,22},{16,24},... | collective-permute-start | bytes 442376 | tf_op jit(solution)/shard_map/ppermute | solution.py:46
  11.1 6.2 %collective-permute-done.10 = bf16[144,512]{1,0:T(8,128)(2,1)S(1)} collective-permute-done((bf16[144,512]{1,0:T(8,128)(2,1)S(1)}, bf16[144,512]{1,0:T(8,128)(2,1)S(1)}, u32[]{:S(2)}, u32[]{:S(2)}) %collective-permute-start.10) | collective-permute-done | bytes 147488 | tf_op jit(solution)/shard_map/ppermute | solution.py:46
  17.9 1.6 %collective-permute-start.9 = (bf16[2,144,512]{2,1,0:T(8,128)(2,1)S(1)}, bf16[2,144,512]{2,1,0:T(8,128)(2,1)S(1)}, u32[]{:S(2)}, u32[]{:S(2)}) collective-permute-start(bf16[2,144,512]{2,1,0:T(8,128)(2,1)S(1)} %pad_maximum_fusion.6.refs_0_), channel_id=1, source_target_pairs={{0,4},{2,6},{4,0},{6,2},{8,12},{10,14},{12,8},{14,10},{16,20},{18,... | collective-permute-start | bytes 884744 | tf_op jit(solution)/shard_map/ppermute | solution.py:37
  19.5 1.6 %collective-permute-start.11 = (bf16[144,512]{1,0:T(8,128)(2,1)S(1)}, bf16[144,512]{1,0:T(8,128)(2,1)S(1)}, u32[]{:S(2)}, u32[]{:S(2)}) collective-permute-start(bf16[144,512]{1,0:T(8,128)(2,1)S(1)} %collective-permute-done.10), channel_id=1, source_target_pairs={{0,1},{1,0},{2,3},{3,2},{4,5},{5,4},{6,7},{7,6},{8,9},{9,8},{10,11... | collective-permute-start | bytes 442376 | tf_op jit(solution)/shard_map/ppermute | solution.py:41
  21.1 3.1 %collective-permute-done.13 = bf16[144,512]{1,0:T(8,128)(2,1)S(1)} collective-permute-done((bf16[144,512]{1,0:T(8,128)(2,1)S(1)}, bf16[144,512]{1,0:T(8,128)(2,1)S(1)}, u32[]{:S(2)}, u32[]{:S(2)}) %collective-permute-start.13) | collective-permute-done | bytes 147488 | tf_op jit(solution)/shard_map/ppermute | solution.py:46
  24.2 3.0 %collective-permute-done.2.refs_1_ = bf16[2,144,512]{2,1,0:T(8,128)(2,1)S(1)} collective-permute-done((bf16[2,144,512]{2,1,0:T(8,128)(2,1)S(1)}, bf16[2,144,512]{2,1,0:T(8,128)(2,1)S(1)}, u32[]{:S(2)}, u32[]{:S(2)}) %collective-permute-start.2) | collective-permute-done | bytes 294944 | tf_op jit(solution)/shard_map/ppermute | solution.py:37
  27.2 1.5 %collective-permute-start.14 = (bf16[144,512]{1,0:T(8,128)(2,1)S(1)}, bf16[144,512]{1,0:T(8,128)(2,1)S(1)}, u32[]{:S(2)}, u32[]{:S(2)}) collective-permute-start(bf16[144,512]{1,0:T(8,128)(2,1)S(1)} %collective-permute-done.13), channel_id=1, source_target_pairs={{0,1},{1,0},{2,3},{3,2},{4,5},{5,4},{6,7},{7,6},{8,9},{9,8},{10,11... | collective-permute-start | bytes 442376 | tf_op jit(solution)/shard_map/ppermute | solution.py:41
  28.8 1.3 %collective-permute-start.26 = (bf16[2,32,2304]{2,1,0:T(8,128)(2,1)S(1)}, bf16[2,32,2304]{2,1,0:T(8,128)(2,1)S(1)}, u32[]{:S(2)}, u32[]{:S(2)}) collective-permute-start(bf16[2,32,2304]{2,1,0:T(8,128)(2,1)S(1)} %pad_maximum_fusion.2), channel_id=1, source_target_pairs={{0,8},{2,10},{4,12},{6,14},{8,16},{10,18},{12,20},{14,22},{16,24},... | collective-permute-start | bytes 884744 | tf_op jit(solution)/shard_map/ppermute | solution.py:46
  30.1 2.3 %collective-permute-done.16 = bf16[144,512]{1,0:T(8,128)(2,1)S(1)} collective-permute-done((bf16[144,512]{1,0:T(8,128)(2,1)S(1)}, bf16[144,512]{1,0:T(8,128)(2,1)S(1)}, u32[]{:S(2)}, u32[]{:S(2)}) %collective-permute-start.16) | collective-permute-done | bytes 147488 | tf_op jit(solution)/shard_map/ppermute | solution.py:46
  32.4 1.8 %collective-permute-start.17 = (bf16[144,512]{1,0:T(8,128)(2,1)S(1)}, bf16[144,512]{1,0:T(8,128)(2,1)S(1)}, u32[]{:S(2)}, u32[]{:S(2)}) collective-permute-start(bf16[144,512]{1,0:T(8,128)(2,1)S(1)} %collective-permute-done.16), channel_id=1, source_target_pairs={{0,1},{1,0},{2,3},{3,2},{4,5},{5,4},{6,7},{7,6},{8,9},{9,8},{10,11... | collective-permute-start | bytes 442376 | tf_op jit(solution)/shard_map/ppermute | solution.py:41
  34.4 3.2 %collective-permute-done.17 = bf16[144,512]{1,0:T(8,128)(2,1)S(1)} collective-permute-done((bf16[144,512]{1,0:T(8,128)(2,1)S(1)}, bf16[144,512]{1,0:T(8,128)(2,1)S(1)}, u32[]{:S(2)}, u32[]{:S(2)}) %collective-permute-start.17) | collective-permute-done | bytes 147488 | tf_op jit(solution)/shard_map/ppermute | solution.py:41
  38.5 1.2 %collective-permute-start.15 = (bf16[2,144,512]{2,1,0:T(8,128)(2,1)S(1)}, bf16[2,144,512]{2,1,0:T(8,128)(2,1)S(1)}, u32[]{:S(2)}, u32[]{:S(2)}) collective-permute-start(bf16[2,144,512]{2,1,0:T(8,128)(2,1)S(1)} %pad_maximum_fusion.8.refs_4_), channel_id=1, source_target_pairs={{0,4},{2,6},{4,0},{6,2},{8,12},{10,14},{12,8},{14,10},{16,20},{18,... | collective-permute-start | bytes 884744 | tf_op jit(solution)/shard_map/ppermute | solution.py:37
  39.7 2.2 %fusion = f32[512]{0:T(512)S(1)} fusion(bf16[256,2304]{1,0:T(8,128)(2,1)S(1)} %bitcast.57, bf16[256,2304]{1,0:T(8,128)(2,1)} %collective-permute-done, pred[]{:T(512)S(6)} %eq.47), kind=kLoop, calls=%fused_computation.2 | loop fusion | flops 14155264 | bytes 2361345 | tf_op jit(solution)/shard_map/reduce_sum | solution.py:22
  43.8 2.2 %fusion.2.x_ref = bf16[512,2304]{1,0:T(8,128)(2,1)S(1)} fusion(f32[2304]{0:T(1024)S(1)} %copy-done.9, f32[512]{0:T(512)S(1)} %add_rsqrt_fusion, bf16[256,2304]{1,0:T(8,128)(2,1)S(1)} %bitcast.58, bf16[256,2304]{1,0:T(8,128)(2,1)} %collective-permute-done, pred[]{:T(512)S(6)} %eq.47), kind=kLoop, calls=%fused_computation.4 | loop fusion | flops 15335424 | bytes 4729857 | tf_op jit(solution)/shard_map/convert_element_type | solution.py:301
  46.0 2.6 %collective-permute-start.21 = (s32[512]{0:T(512)S(1)}, s32[512]{0:T(512)S(1)}, u32[]{:S(2)}, u32[]{:S(2)}) collective-permute-start(s32[512]{0:T(512)S(1)} %add_select_fusion), channel_id=1, source_target_pairs={{0,4},{2,6},{4,8},{6,10},{8,12},{10,14},{12,16},{14,18},{16,20},{1... | collective-permute-start | bytes 6152 | tf_op jit(solution)/shard_map/ppermute | solution.py:51
  49.7 2.8 %collective-permute-done.15.refs_5_ = bf16[2,144,512]{2,1,0:T(8,128)(2,1)S(1)} collective-permute-done((bf16[2,144,512]{2,1,0:T(8,128)(2,1)S(1)}, bf16[2,144,512]{2,1,0:T(8,128)(2,1)S(1)}, u32[]{:S(2)}, u32[]{:S(2)}) %collective-permute-start.15) | collective-permute-done | bytes 294944 | tf_op jit(solution)/shard_map/ppermute | solution.py:37
  52.4 1.5 %collective-permute-start.4 = (bf16[2,144,512]{2,1,0:T(8,128)(2,1)S(1)}, bf16[2,144,512]{2,1,0:T(8,128)(2,1)S(1)}, u32[]{:S(2)}, u32[]{:S(2)}) collective-permute-start(bf16[2,144,512]{2,1,0:T(8,128)(2,1)S(1)} %collective-permute-done.3.refs_2_), channel_id=1, source_target_pairs={{0,1},{1,0},{2,3},{3,2},{4,5},{5,4},{6,7},{7,6},{8,9},{9,8},{10,11... | collective-permute-start | bytes 884744 | tf_op jit(solution)/shard_map/ppermute | solution.py:41
  55.6 5.4 %project.3.kv_ref = bf16[512,512]{1,0:T(8,128)(2,1)S(1)} custom-call(s32[16]{0:T(128)S(1)} %stack.229.spots, bf16[512,2304]{1,0:T(8,128)(2,1)S(1)} %fusion.2.x_ref, f32[512,128]{1,0:T(8,128)S(1)} %get-tuple-element.23.cos_ref, f32[512,128]{1,0:T(8,128)S(1)} %get-tuple-element.22.sin_ref, bf16[2,144,512]{2,1,0:T(8,128)(2,1)S(1)} %pad_maximum_fusion.6.refs_0_, ...), custom_call_target="tpu_custom_call" | custom-call | flops 1207959552 | bytes 2359296 | tf_op jit(solution)/shard_map/project/pallas_call | solution.py:128
  61.0 2.2 %collective-permute-start.19 = (bf16[512,512]{1,0:T(8,128)(2,1)S(1)}, bf16[512,512]{1,0:T(8,128)(2,1)S(1)}, u32[]{:S(2)}, u32[]{:S(2)}) collective-permute-start(bf16[512,512]{1,0:T(8,128)(2,1)S(1)} %project.3.kv_ref), channel_id=1, source_target_pairs={{0,4},{2,6},{4,8},{6,10},{8,12},{10,14},{12,16},{14,18},{16,20},{1... | collective-permute-start | bytes 1572872 | tf_op jit(solution)/shard_map/ppermute | solution.py:51
  63.3 1.8 %collective-permute-start.6 = (bf16[2,144,512]{2,1,0:T(8,128)(2,1)S(1)}, bf16[2,144,512]{2,1,0:T(8,128)(2,1)S(1)}, u32[]{:S(2)}, u32[]{:S(2)}) collective-permute-start(bf16[2,144,512]{2,1,0:T(8,128)(2,1)S(1)} %collective-permute-done.5.refs_4_), channel_id=1, source_target_pairs={{0,1},{1,0},{2,3},{3,2},{4,5},{5,4},{6,7},{7,6},{8,9},{9,8},{10,11... | collective-permute-start | bytes 884744 | tf_op jit(solution)/shard_map/ppermute | solution.py:41
  65.9 5.8 %collective-permute-done.6.refs_5_ = bf16[2,144,512]{2,1,0:T(8,128)(2,1)S(1)} collective-permute-done((bf16[2,144,512]{2,1,0:T(8,128)(2,1)S(1)}, bf16[2,144,512]{2,1,0:T(8,128)(2,1)S(1)}, u32[]{:S(2)}, u32[]{:S(2)}) %collective-permute-start.6) | collective-permute-done | bytes 294944 | tf_op jit(solution)/shard_map/ppermute | solution.py:41
  71.7 3.2 %collective-permute-done.8.refs_7_ = bf16[2,144,512]{2,1,0:T(8,128)(2,1)S(1)} collective-permute-done((bf16[2,144,512]{2,1,0:T(8,128)(2,1)S(1)}, bf16[2,144,512]{2,1,0:T(8,128)(2,1)S(1)}, u32[]{:S(2)}, u32[]{:S(2)}) %collective-permute-start.8) | collective-permute-done | bytes 294944 | tf_op jit(solution)/shard_map/ppermute | solution.py:41
  74.8 5.4 %project.2.q_ref = bf16[512,512]{1,0:T(8,128)(2,1)S(1)} custom-call(s32[16]{0:T(128)S(1)} %stack.224.spots, bf16[512,2304]{1,0:T(8,128)(2,1)S(1)} %fusion.2.x_ref, f32[512,128]{1,0:T(8,128)S(1)} %get-tuple-element.23.cos_ref, f32[512,128]{1,0:T(8,128)S(1)} %get-tuple-element.22.sin_ref, bf16[2,144,512]{2,1,0:T(8,128)(2,1)S(1)} %pad_maximum_fusion.1.refs_0_, ...), custom_call_target="tpu_custom_call" | custom-call | flops 1207959552 | bytes 2359296 | tf_op jit(solution)/shard_map/project/pallas_call | solution.py:128
  81.2 1.4 %attend.1 = bf16[2,2,256,256]{3,2,1,0:T(8,128)(2,1)S(1)} custom-call(bf16[512,512]{1,0:T(8,128)(2,1)S(1)} %project.2.q_ref, bf16[512,512]{1,0:T(8,128)(2,1)S(1)} %project.3.kv_ref, bf16[512,512]{1,0:T(8,128)(2,1)S(1)} %collective-permute-done.19.old_ref, s32[512,1]{1,0:T(8,128)S(1)} %broadcast_select_fusion.2.qseg_ref, s32[1,1024]{1,0:T(1,128)S(1)} %bitcast.60), custom_call_target="tpu_custom_call" | custom-call | flops 1073741824 | bytes 1048576 | tf_op jit(solution)/shard_map/attend/pallas_call | solution.py:177
  82.6 1.2 %collective-permute-start.32 = (bf16[2,32,2304]{2,1,0:T(8,128)(2,1)S(1)}, bf16[2,32,2304]{2,1,0:T(8,128)(2,1)}, u32[]{:S(2)}, u32[]{:S(2)}) collective-permute-start(bf16[2,32,2304]{2,1,0:T(8,128)(2,1)S(1)} %collective-permute-done.30.refs_9_), channel_id=1, source_target_pairs={{0,1},{1,0},{2,3},{3,2},{4,5},{5,4},{6,7},{7,6},{8,9},{9,8},{10,11... | collective-permute-start | bytes 884744 | tf_op jit(solution)/shard_map/ppermute | solution.py:41
  87.4 2.9 %collective-permute-done.28.refs_7_ = bf16[2,32,2304]{2,1,0:T(8,128)(2,1)} collective-permute-done((bf16[2,32,2304]{2,1,0:T(8,128)(2,1)S(1)}, bf16[2,32,2304]{2,1,0:T(8,128)(2,1)}, u32[]{:S(2)}, u32[]{:S(2)}) %collective-permute-start.28) | collective-permute-done | bytes 294944 | tf_op jit(solution)/shard_map/ppermute | solution.py:41
  90.3 6.3 %collective-permute-done.32.refs_11_ = bf16[2,32,2304]{2,1,0:T(8,128)(2,1)} collective-permute-done((bf16[2,32,2304]{2,1,0:T(8,128)(2,1)S(1)}, bf16[2,32,2304]{2,1,0:T(8,128)(2,1)}, u32[]{:S(2)}, u32[]{:S(2)}) %collective-permute-start.32) | collective-permute-done | bytes 294944 | tf_op jit(solution)/shard_map/ppermute | solution.py:41
  96.6 5.9 %collective-permute-done.36.refs_6_ = bf16[2,32,2304]{2,1,0:T(8,128)(2,1)} collective-permute-done((bf16[2,32,2304]{2,1,0:T(8,128)(2,1)S(1)}, bf16[2,32,2304]{2,1,0:T(8,128)(2,1)}, u32[]{:S(2)}, u32[]{:S(2)}) %collective-permute-start.36) | collective-permute-done | bytes 294944 | tf_op jit(solution)/shard_map/ppermute | solution.py:41
  103.2 1.3 %maximum_select_fusion.1.refs_0_ = bf16[4,256,256]{2,1,0:T(8,128)(2,1)S(1)} fusion(bf16[2,256,256]{2,1,0:T(8,128)(2,1)} %collective-permute-done.22, bf16[2,256,256]{2,1,0:T(8,128)(2,1)} %get-tuple-element.13, pred[]{:T(512)S(6)} %eq.47), kind=kLoop, calls=%fused_computation.6 | loop fusion | flops 786432 | bytes 1048577 | tf_op jit(solution)/shard_map/jit(_where)/select_n | solution.py:296
  108.1 6.1 %early.1.refs_1_ = f32[256,2304]{1,0:T(8,128)S(1)} custom-call(s32[27]{0:T(128)S(1)} %stack.245.marks, bf16[4,256,256]{2,1,0:T(8,128)(2,1)S(1)} %maximum_select_fusion.1.refs_0_, bf16[2,32,2304]{2,1,0:T(8,128)(2,1)S(1)} %pad_maximum_fusion.3.refs_1_, bf16[2,32,2304]{2,1,0:T(8,128)(2,1)S(1)} %collective-permute-done.23.refs_2_, ...), custom_call_target="tpu_custom_call" | custom-call | flops 905969664 | bytes 3538944 | tf_op jit(solution)/shard_map/early/pallas_call | solution.py:244
  114.2 4.2 %finish.1 = bf16[256,2304]{1,0:T(8,128)(2,1)} custom-call(s32[9]{0:T(128)S(1)} %stack.207.marks, bf16[4,256,256]{2,1,0:T(8,128)(2,1)S(1)} %maximum_select_fusion.1.refs_0_, f32[256,2304]{1,0:T(8,128)S(1)} %early.1.refs_1_, bf16[256,2304]{1,0:T(8,128)(2,1)S(1)} %bitcast.59, f32[1,2304]{1,0:T(1,128)S(1)} %broadcast_in_dim.20.refs_3_, ...), custom_call_target="tpu_custom_call" | custom-call | flops 301989888 | bytes 1179648 | tf_op jit(solution)/shard_map/finish/pallas_call | solution.py:244
  (108 shorter events, 22.4 us)
Async XLA Ops:
  0.0 38.5 %collective-permute-start = (bf16[256,2304]{1,0:T(8,128)(2,1)}, bf16[256,2304]{1,0:T(8,128)(2,1)}, u32[]{:S(2)}, u32[]{:S(2)}) collective-permute-start(bf16[256,2304]{1,0:T(8,128)(2,1)} %bitcast.56), channel_id=1, source_target_pairs={{0,2},{2,0},{4,6},{6,4},{8,10},{10,8},{12,14},{14,12},{16,18},{18,... | collective-permute-start | bytes 3538952 | tf_op jit(solution)/shard_map/ppermute | solution.py:33
  4.2 15.3 %collective-permute-start.24 = (bf16[2,32,2304]{2,1,0:T(8,128)(2,1)S(1)}, bf16[2,32,2304]{2,1,0:T(8,128)(2,1)S(1)}, u32[]{:S(2)}, u32[]{:S(2)}) collective-permute-start(bf16[2,32,2304]{2,1,0:T(8,128)(2,1)S(1)} %pad_maximum_fusion.3.refs_1_), channel_id=1, source_target_pairs={{0,4},{2,6},{4,0},{6,2},{8,12},{10,14},{12,8},{14,10},{16,20},{18,... | collective-permute-start | bytes 884744 | tf_op jit(solution)/shard_map/ppermute | solution.py:37
  17.3 9.9 %collective-permute-start.2 = (bf16[2,144,512]{2,1,0:T(8,128)(2,1)S(1)}, bf16[2,144,512]{2,1,0:T(8,128)(2,1)S(1)}, u32[]{:S(2)}, u32[]{:S(2)}) collective-permute-start(bf16[2,144,512]{2,1,0:T(8,128)(2,1)S(1)} %pad_maximum_fusion.1.refs_0_), channel_id=1, source_target_pairs={{0,4},{2,6},{4,0},{6,2},{8,12},{10,14},{12,8},{14,10},{16,20},{18,... | collective-permute-start | bytes 884744 | tf_op jit(solution)/shard_map/ppermute | solution.py:37
  17.9 24.0 %collective-permute-start.9 = (bf16[2,144,512]{2,1,0:T(8,128)(2,1)S(1)}, bf16[2,144,512]{2,1,0:T(8,128)(2,1)S(1)}, u32[]{:S(2)}, u32[]{:S(2)}) collective-permute-start(bf16[2,144,512]{2,1,0:T(8,128)(2,1)S(1)} %pad_maximum_fusion.6.refs_0_), channel_id=1, source_target_pairs={{0,4},{2,6},{4,0},{6,2},{8,12},{10,14},{12,8},{14,10},{16,20},{18,... | collective-permute-start | bytes 884744 | tf_op jit(solution)/shard_map/ppermute | solution.py:37
  19.5 9.3 %collective-permute-start.11 = (bf16[144,512]{1,0:T(8,128)(2,1)S(1)}, bf16[144,512]{1,0:T(8,128)(2,1)S(1)}, u32[]{:S(2)}, u32[]{:S(2)}) collective-permute-start(bf16[144,512]{1,0:T(8,128)(2,1)S(1)} %collective-permute-done.10), channel_id=1, source_target_pairs={{0,1},{1,0},{2,3},{3,2},{4,5},{5,4},{6,7},{7,6},{8,9},{9,8},{10,11... | collective-permute-start | bytes 442376 | tf_op jit(solution)/shard_map/ppermute | solution.py:41
  24.2 8.2 %collective-permute-start.16 = (bf16[144,512]{1,0:T(8,128)(2,1)S(1)}, bf16[144,512]{1,0:T(8,128)(2,1)S(1)}, u32[]{:S(2)}, u32[]{:S(2)}) collective-permute-start(bf16[144,512]{1,0:T(8,128)(2,1)S(1)} %collective-permute-done.13), channel_id=1, source_target_pairs={{0,8},{2,10},{4,12},{6,14},{8,16},{10,18},{12,20},{14,22},{16,24},... | collective-permute-start | bytes 442376 | tf_op jit(solution)/shard_map/ppermute | solution.py:46
  28.8 17.2 %collective-permute-start.26 = (bf16[2,32,2304]{2,1,0:T(8,128)(2,1)S(1)}, bf16[2,32,2304]{2,1,0:T(8,128)(2,1)S(1)}, u32[]{:S(2)}, u32[]{:S(2)}) collective-permute-start(bf16[2,32,2304]{2,1,0:T(8,128)(2,1)S(1)} %pad_maximum_fusion.2), channel_id=1, source_target_pairs={{0,8},{2,10},{4,12},{6,14},{8,16},{10,18},{12,20},{14,22},{16,24},... | collective-permute-start | bytes 884744 | tf_op jit(solution)/shard_map/ppermute | solution.py:46
  34.2 9.5 %collective-permute-start.3 = (bf16[2,144,512]{2,1,0:T(8,128)(2,1)S(1)}, bf16[2,144,512]{2,1,0:T(8,128)(2,1)S(1)}, u32[]{:S(2)}, u32[]{:S(2)}) collective-permute-start(bf16[2,144,512]{2,1,0:T(8,128)(2,1)S(1)} %pad_maximum_fusion), channel_id=1, source_target_pairs={{0,8},{2,10},{4,12},{6,14},{8,16},{10,18},{12,20},{14,22},{16,24},... | collective-permute-start | bytes 884744 | tf_op jit(solution)/shard_map/ppermute | solution.py:46
  37.6 11.1 %collective-permute-start.12 = (bf16[2,144,512]{2,1,0:T(8,128)(2,1)S(1)}, bf16[2,144,512]{2,1,0:T(8,128)(2,1)S(1)}, u32[]{:S(2)}, u32[]{:S(2)}) collective-permute-start(bf16[2,144,512]{2,1,0:T(8,128)(2,1)S(1)} %pad_maximum_fusion.7.refs_2_), channel_id=1, source_target_pairs={{0,4},{2,6},{4,0},{6,2},{8,12},{10,14},{12,8},{14,10},{16,20},{18,... | collective-permute-start | bytes 884744 | tf_op jit(solution)/shard_map/ppermute | solution.py:37
  38.5 14.0 %collective-permute-start.15 = (bf16[2,144,512]{2,1,0:T(8,128)(2,1)S(1)}, bf16[2,144,512]{2,1,0:T(8,128)(2,1)S(1)}, u32[]{:S(2)}, u32[]{:S(2)}) collective-permute-start(bf16[2,144,512]{2,1,0:T(8,128)(2,1)S(1)} %pad_maximum_fusion.8.refs_4_), channel_id=1, source_target_pairs={{0,4},{2,6},{4,0},{6,2},{8,12},{10,14},{12,8},{14,10},{16,20},{18,... | collective-permute-start | bytes 884744 | tf_op jit(solution)/shard_map/ppermute | solution.py:37
  42.0 13.6 %collective-permute-start.18 = (bf16[2,144,512]{2,1,0:T(8,128)(2,1)S(1)}, bf16[2,144,512]{2,1,0:T(8,128)(2,1)S(1)}, u32[]{:S(2)}, u32[]{:S(2)}) collective-permute-start(bf16[2,144,512]{2,1,0:T(8,128)(2,1)S(1)} %pad_maximum_fusion.9.refs_6_), channel_id=1, source_target_pairs={{0,4},{2,6},{4,0},{6,2},{8,12},{10,14},{12,8},{14,10},{16,20},{18,... | collective-permute-start | bytes 884744 | tf_op jit(solution)/shard_map/ppermute | solution.py:37
  43.8 10.8 %collective-permute-start.5 = (bf16[2,144,512]{2,1,0:T(8,128)(2,1)S(1)}, bf16[2,144,512]{2,1,0:T(8,128)(2,1)S(1)}, u32[]{:S(2)}, u32[]{:S(2)}) collective-permute-start(bf16[2,144,512]{2,1,0:T(8,128)(2,1)S(1)} %collective-permute-done.3.refs_2_), channel_id=1, source_target_pairs={{0,8},{2,10},{4,12},{6,14},{8,16},{10,18},{12,20},{14,22},{16,24},... | collective-permute-start | bytes 884744 | tf_op jit(solution)/shard_map/ppermute | solution.py:46
  46.0 17.3 %collective-permute-start.21 = (s32[512]{0:T(512)S(1)}, s32[512]{0:T(512)S(1)}, u32[]{:S(2)}, u32[]{:S(2)}) collective-permute-start(s32[512]{0:T(512)S(1)} %add_select_fusion), channel_id=1, source_target_pairs={{0,4},{2,6},{4,8},{6,10},{8,12},{10,14},{12,16},{14,18},{16,20},{1... | collective-permute-start | bytes 6152 | tf_op jit(solution)/shard_map/ppermute | solution.py:51
  48.6 17.2 %collective-permute-start.30 = (bf16[2,32,2304]{2,1,0:T(8,128)(2,1)S(1)}, bf16[2,32,2304]{2,1,0:T(8,128)(2,1)S(1)}, u32[]{:S(2)}, u32[]{:S(2)}) collective-permute-start(bf16[2,32,2304]{2,1,0:T(8,128)(2,1)S(1)} %collective-permute-done.26.refs_5_), channel_id=1, source_target_pairs={{0,8},{2,10},{4,12},{6,14},{8,16},{10,18},{12,20},{14,22},{16,24},... | collective-permute-start | bytes 884744 | tf_op jit(solution)/shard_map/ppermute | solution.py:46
  52.4 13.4 %collective-permute-start.4 = (bf16[2,144,512]{2,1,0:T(8,128)(2,1)S(1)}, bf16[2,144,512]{2,1,0:T(8,128)(2,1)S(1)}, u32[]{:S(2)}, u32[]{:S(2)}) collective-permute-start(bf16[2,144,512]{2,1,0:T(8,128)(2,1)S(1)} %collective-permute-done.3.refs_2_), channel_id=1, source_target_pairs={{0,1},{1,0},{2,3},{3,2},{4,5},{5,4},{6,7},{7,6},{8,9},{9,8},{10,11... | collective-permute-start | bytes 884744 | tf_op jit(solution)/shard_map/ppermute | solution.py:41
  54.6 10.5 %collective-permute-start.7 = (bf16[2,144,512]{2,1,0:T(8,128)(2,1)S(1)}, bf16[2,144,512]{2,1,0:T(8,128)(2,1)S(1)}, u32[]{:S(2)}, u32[]{:S(2)}) collective-permute-start(bf16[2,144,512]{2,1,0:T(8,128)(2,1)S(1)} %collective-permute-done.5.refs_4_), channel_id=1, source_target_pairs={{0,8},{2,10},{4,12},{6,14},{8,16},{10,18},{12,20},{14,22},{16,24},... | collective-permute-start | bytes 884744 | tf_op jit(solution)/shard_map/ppermute | solution.py:46
  61.0 19.3 %collective-permute-start.19 = (bf16[512,512]{1,0:T(8,128)(2,1)S(1)}, bf16[512,512]{1,0:T(8,128)(2,1)S(1)}, u32[]{:S(2)}, u32[]{:S(2)}) collective-permute-start(bf16[512,512]{1,0:T(8,128)(2,1)S(1)} %project.3.kv_ref), channel_id=1, source_target_pairs={{0,4},{2,6},{4,8},{6,10},{8,12},{10,14},{12,16},{14,18},{16,20},{1... | collective-permute-start | bytes 1572872 | tf_op jit(solution)/shard_map/ppermute | solution.py:51
  63.3 8.4 %collective-permute-start.6 = (bf16[2,144,512]{2,1,0:T(8,128)(2,1)S(1)}, bf16[2,144,512]{2,1,0:T(8,128)(2,1)S(1)}, u32[]{:S(2)}, u32[]{:S(2)}) collective-permute-start(bf16[2,144,512]{2,1,0:T(8,128)(2,1)S(1)} %collective-permute-done.5.refs_4_), channel_id=1, source_target_pairs={{0,1},{1,0},{2,3},{3,2},{4,5},{5,4},{6,7},{7,6},{8,9},{9,8},{10,11... | collective-permute-start | bytes 884744 | tf_op jit(solution)/shard_map/ppermute | solution.py:41
  65.1 9.8 %collective-permute-start.8 = (bf16[2,144,512]{2,1,0:T(8,128)(2,1)S(1)}, bf16[2,144,512]{2,1,0:T(8,128)(2,1)S(1)}, u32[]{:S(2)}, u32[]{:S(2)}) collective-permute-start(bf16[2,144,512]{2,1,0:T(8,128)(2,1)S(1)} %collective-permute-done.7.refs_6_), channel_id=1, source_target_pairs={{0,1},{1,0},{2,3},{3,2},{4,5},{5,4},{6,7},{7,6},{8,9},{9,8},{10,11... | collective-permute-start | bytes 884744 | tf_op jit(solution)/shard_map/ppermute | solution.py:41
  65.8 16.8 %collective-permute-start.23 = (bf16[2,32,2304]{2,1,0:T(8,128)(2,1)S(1)}, bf16[2,32,2304]{2,1,0:T(8,128)(2,1)S(1)}, u32[]{:S(2)}, u32[]{:S(2)}) collective-permute-start(bf16[2,32,2304]{2,1,0:T(8,128)(2,1)S(1)} %pad_maximum_fusion.3.refs_1_), channel_id=1, source_target_pairs={{0,2},{2,0},{4,6},{6,4},{8,10},{10,8},{12,14},{14,12},{16,18},{18,... | collective-permute-start | bytes 884744 | tf_op jit(solution)/shard_map/ppermute | solution.py:33
  65.8 18.1 %collective-permute-start.34 = (bf16[2,32,2304]{2,1,0:T(8,128)(2,1)S(1)}, bf16[2,32,2304]{2,1,0:T(8,128)(2,1)S(1)}, u32[]{:S(2)}, u32[]{:S(2)}) collective-permute-start(bf16[2,32,2304]{2,1,0:T(8,128)(2,1)S(1)} %collective-permute-done.30.refs_9_), channel_id=1, source_target_pairs={{0,8},{2,10},{4,12},{6,14},{8,16},{10,18},{12,20},{14,22},{16,24},... | collective-permute-start | bytes 884744 | tf_op jit(solution)/shard_map/ppermute | solution.py:46
  71.7 13.8 %collective-permute-start.25 = (bf16[2,32,2304]{2,1,0:T(8,128)(2,1)S(1)}, bf16[2,32,2304]{2,1,0:T(8,128)(2,1)S(1)}, u32[]{:S(2)}, u32[]{:S(2)}) collective-permute-start(bf16[2,32,2304]{2,1,0:T(8,128)(2,1)S(1)} %collective-permute-done.24.refs_3_), channel_id=1, source_target_pairs={{0,2},{2,0},{4,6},{6,4},{8,10},{10,8},{12,14},{14,12},{16,18},{18,... | collective-permute-start | bytes 884744 | tf_op jit(solution)/shard_map/ppermute | solution.py:33
  74.8 11.3 %collective-permute-start.27 = (bf16[2,32,2304]{2,1,0:T(8,128)(2,1)S(1)}, bf16[2,32,2304]{2,1,0:T(8,128)(2,1)S(1)}, u32[]{:S(2)}, u32[]{:S(2)}) collective-permute-start(bf16[2,32,2304]{2,1,0:T(8,128)(2,1)S(1)} %collective-permute-done.26.refs_5_), channel_id=1, source_target_pairs={{0,2},{2,0},{4,6},{6,4},{8,10},{10,8},{12,14},{14,12},{16,18},{18,... | collective-permute-start | bytes 884744 | tf_op jit(solution)/shard_map/ppermute | solution.py:33
  80.2 10.1 %collective-permute-start.28 = (bf16[2,32,2304]{2,1,0:T(8,128)(2,1)S(1)}, bf16[2,32,2304]{2,1,0:T(8,128)(2,1)}, u32[]{:S(2)}, u32[]{:S(2)}) collective-permute-start(bf16[2,32,2304]{2,1,0:T(8,128)(2,1)S(1)} %collective-permute-done.26.refs_5_), channel_id=1, source_target_pairs={{0,1},{1,0},{2,3},{3,2},{4,5},{5,4},{6,7},{7,6},{8,9},{9,8},{10,11... | collective-permute-start | bytes 884744 | tf_op jit(solution)/shard_map/ppermute | solution.py:41
  82.6 14.0 %collective-permute-start.32 = (bf16[2,32,2304]{2,1,0:T(8,128)(2,1)S(1)}, bf16[2,32,2304]{2,1,0:T(8,128)(2,1)}, u32[]{:S(2)}, u32[]{:S(2)}) collective-permute-start(bf16[2,32,2304]{2,1,0:T(8,128)(2,1)S(1)} %collective-permute-done.30.refs_9_), channel_id=1, source_target_pairs={{0,1},{1,0},{2,3},{3,2},{4,5},{5,4},{6,7},{7,6},{8,9},{9,8},{10,11... | collective-permute-start | bytes 884744 | tf_op jit(solution)/shard_map/ppermute | solution.py:41
  83.9 18.6 %collective-permute-start.36 = (bf16[2,32,2304]{2,1,0:T(8,128)(2,1)S(1)}, bf16[2,32,2304]{2,1,0:T(8,128)(2,1)}, u32[]{:S(2)}, u32[]{:S(2)}) collective-permute-start(bf16[2,32,2304]{2,1,0:T(8,128)(2,1)S(1)} %collective-permute-done.34.refs_4_), channel_id=1, source_target_pairs={{0,1},{1,0},{2,3},{3,2},{4,5},{5,4},{6,7},{7,6},{8,9},{9,8},{10,11... | collective-permute-start | bytes 884744 | tf_op jit(solution)/shard_map/ppermute | solution.py:41
  86.2 16.3 %collective-permute-start.22 = (bf16[2,256,256]{2,1,0:T(8,128)(2,1)S(1)}, bf16[2,256,256]{2,1,0:T(8,128)(2,1)}, u32[]{:S(2)}, u32[]{:S(2)}) collective-permute-start(bf16[2,256,256]{2,1,0:T(8,128)(2,1)S(1)} %get-tuple-element.14), channel_id=1, source_target_pairs={{0,2},{2,0},{4,6},{6,4},{8,10},{10,8},{12,14},{14,12},{16,18},{18,... | collective-permute-start | bytes 786440 | tf_op jit(solution)/shard_map/ppermute | solution.py:33
  86.9 17.6 %collective-permute-start.31 = (bf16[2,32,2304]{2,1,0:T(8,128)(2,1)S(1)}, bf16[2,32,2304]{2,1,0:T(8,128)(2,1)S(1)}, u32[]{:S(2)}, u32[]{:S(2)}) collective-permute-start(bf16[2,32,2304]{2,1,0:T(8,128)(2,1)S(1)} %collective-permute-done.30.refs_9_), channel_id=1, source_target_pairs={{0,2},{2,0},{4,6},{6,4},{8,10},{10,8},{12,14},{14,12},{16,18},{18,... | collective-permute-start | bytes 884744 | tf_op jit(solution)/shard_map/ppermute | solution.py:33
  90.3 14.2 %collective-permute-start.29 = (bf16[2,32,2304]{2,1,0:T(8,128)(2,1)}, bf16[2,32,2304]{2,1,0:T(8,128)(2,1)}, u32[]{:S(2)}, u32[]{:S(2)}) collective-permute-start(bf16[2,32,2304]{2,1,0:T(8,128)(2,1)} %collective-permute-done.28.refs_7_), channel_id=1, source_target_pairs={{0,2},{2,0},{4,6},{6,4},{8,10},{10,8},{12,14},{14,12},{16,18},{18,... | collective-permute-start | bytes 884744 | tf_op jit(solution)/shard_map/ppermute | solution.py:33
  96.6 8.6 %collective-permute-start.33 = (bf16[2,32,2304]{2,1,0:T(8,128)(2,1)}, bf16[2,32,2304]{2,1,0:T(8,128)(2,1)}, u32[]{:S(2)}, u32[]{:S(2)}) collective-permute-start(bf16[2,32,2304]{2,1,0:T(8,128)(2,1)} %collective-permute-done.32.refs_11_), channel_id=1, source_target_pairs={{0,2},{2,0},{4,6},{6,4},{8,10},{10,8},{12,14},{14,12},{16,18},{18,... | collective-permute-start | bytes 884744 | tf_op jit(solution)/shard_map/ppermute | solution.py:33
  102.5 11.7 %collective-permute-start.35 = (bf16[2,32,2304]{2,1,0:T(8,128)(2,1)S(1)}, bf16[2,32,2304]{2,1,0:T(8,128)(2,1)}, u32[]{:S(2)}, u32[]{:S(2)}) collective-permute-start(bf16[2,32,2304]{2,1,0:T(8,128)(2,1)S(1)} %collective-permute-done.34.refs_4_), channel_id=1, source_target_pairs={{0,2},{2,0},{4,6},{6,4},{8,10},{10,8},{12,14},{14,12},{16,18},{18,... | collective-permute-start | bytes 884744 | tf_op jit(solution)/shard_map/ppermute | solution.py:33
  102.5 11.7 %collective-permute-start.37 = (bf16[2,32,2304]{2,1,0:T(8,128)(2,1)}, bf16[2,32,2304]{2,1,0:T(8,128)(2,1)}, u32[]{:S(2)}, u32[]{:S(2)}) collective-permute-start(bf16[2,32,2304]{2,1,0:T(8,128)(2,1)} %collective-permute-done.36.refs_6_), channel_id=1, source_target_pairs={{0,2},{2,0},{4,6},{6,4},{8,10},{10,8},{12,14},{14,12},{16,18},{18,... | collective-permute-start | bytes 884744 | tf_op jit(solution)/shard_map/ppermute | solution.py:33
  (17 other events, 119.3 us)

commit v3 on v1

--- a/solution.py
+++ b/solution.py
@@ -1,29 +1,608 @@
+import functools
 import math
 
 import jax
 import jax.numpy as jnp
 from jax import lax
+from jax.experimental import pallas as pl
+from jax.experimental.pallas import tpu as pltpu
 from jax.sharding import PartitionSpec as P
+
 
 Q_HEADS = 4
 KV_HEADS = 2
 HEAD = 256
 WINDOW = 4096
 DOCS = 16
-
-
 EPS = 1e-06
 CAP = 50.0
+TAIL = 16
+GROUPS = Q_HEADS // KV_HEADS
+
+
+def rms_scale(values, gain):
+    return values * lax.rsqrt(jnp.mean(values * values, axis=-1, keepdims=True) + EPS) * gain
+
+
+def rotary_tables(positions):
+    half_dim = HEAD // 2
+    inverse = 1.0 / 10000.0 ** (jnp.arange(half_dim, dtype=jnp.float32) * 2.0 / HEAD)
+    angles = positions.astype(jnp.float32)[:, None] * inverse[None, :]
+    return jnp.cos(angles), jnp.sin(angles)
+
+
+def swap_core(block):
+    return lax.ppermute(block, "seq", [(i, i ^ 1) for i in range(lax.axis_size("seq"))])
+
+
+def swap_pair(block):
+    return lax.ppermute(block, "seq", [(i, i ^ 2) for i in range(lax.axis_size("seq"))])
+
+
+def swap_batch(block):
+    return lax.ppermute(block, "batch", [(0, 1), (1, 0)])
+
+
+def along_line(block, steps):
+    count = lax.axis_size("seq")
+    return lax.ppermute(block, "seq", [(i, (i + 4 * steps) % count) for i in range(count)])
+
+
+def from_chip_behind(block, distance):
+    count = lax.axis_size("seq")
+    return lax.ppermute(block, "seq", [(i, (i + 2 * distance) % count) for i in range(count)])
+
+
+def line_gather(unit, line_count):
+    units = []
+    for _ in range(1, line_count):
+        unit = along_line(unit, 1)
+        units.append(unit)
+    return units
+
+
+def gather_near(own, unit, plane, pair, line_count, tag):
+    pair_own = swap_pair(own)
+    pieces = [(own, [(0, pair, 0), (0, pair, 1)]), (pair_own, [(0, 1 - pair, 0), (0, 1 - pair, 1)])]
+    first, second, third = line_gather(unit, line_count)
+    near = pack(first, second[None], 0)
+    for name, block, backs in (("n", near, (1, 2)), ("f", third[None], (3,))):
+        pieces.append((block, [(k, pair, plane) for k in backs]))
+        beside = swap_batch(block)
+        pieces.append((beside, [(k, pair, 1 - plane) for k in backs]))
+        across = swap_pair(block)
+        pieces.append((across, [(k, 1 - pair, plane) for k in backs]))
+        if tag + name in BY_BATCH:
+            corner = swap_batch(across)
+        else:
+            corner = swap_pair(beside)
+        pieces.append((corner, [(k, 1 - pair, 1 - plane) for k in backs]))
+    return pieces
+
+
+def gather_wide(own, mine, plane, pair, line_count):
+    pair_own = swap_pair(own)
+    pieces = [(own, [(0, pair, 0), (0, pair, 1)]), (pair_own, [(0, 1 - pair, 0), (0, 1 - pair, 1)])]
+    unit = pack(mine, pair_own, plane)
+    for back, block in enumerate(line_gather(unit, line_count), 1):
+        pieces.append((block, [(back, pair, plane), (back, 1 - pair, plane)]))
+        other = swap_batch(block)
+        pieces.append((other, [(back, pair, 1 - plane), (back, 1 - pair, 1 - plane)]))
+    return pieces
+
+
+def in_hbm(arrays):
+    return [pltpu.with_memory_space_constraint(array, pltpu.HBM) for array in arrays]
+
+
+def pack_kernel(place, first_ref, second_ref, out_ref):
+    out_ref[0] = first_ref[...]
+    out_ref[1] = second_ref[place[0]]
+
+
+def pack(first, second, index):
+    vmem = pl.BlockSpec(memory_space=pltpu.VMEM)
+    return pl.pallas_call(
+        pack_kernel,
+        out_shape=jax.ShapeDtypeStruct((2,) + first.shape, first.dtype),
+        in_specs=[pl.BlockSpec(memory_space=pltpu.SMEM)] + [vmem] * 2,
+        out_specs=vmem,
+        compiler_params=pltpu.CompilerParams(vmem_limit_bytes=4 * 1024 * 1024),
+        cost_estimate=pl.CostEstimate(flops=1000000, bytes_accessed=6 * first.size, transcendentals=0),
+        name="pack",
+    )(jnp.asarray(index, jnp.int32)[None], first, second)
+
+
+def prepare_kernel(place, w_ref, came_ref, out_ref, kv_ref, q_ref, kv_unit, q_unit, out_unit):
+    core, plane = place[0], place[1]
+    rows = out_ref.shape[0] // 2
+    at_q = pl.multiple_of(core * GROUPS * HEAD, 128)
+    at_k = pl.multiple_of((Q_HEADS + core) * HEAD, 128)
+    at_v = pl.multiple_of((Q_HEADS + KV_HEADS + core) * HEAD, 128)
+    out_unit[...] = out_ref[pl.ds(pl.multiple_of(plane * rows, rows), rows), :]
+    for ref, half in ((w_ref, core), (came_ref, 1 - core)):
+        for target, low, at, width in (
+            (kv_ref, 0, at_k, HEAD),
+            (kv_ref, HEAD, at_v, HEAD),
+            (q_ref, 0, at_q, GROUPS * HEAD),
+        ):
+            block = ref[:, pl.ds(at, width)]
+            target[half, :, low : low + width] = block
+            unit = kv_unit if target is kv_ref else q_unit
+
+            @pl.when(half == plane)
+            def _():
+                unit[:, low : low + width] = block
+
+
+def prepare(w_qkv, came, w_out, core, plane):
+    rows = w_qkv.shape[0]
+    vmem = pl.BlockSpec(memory_space=pltpu.VMEM)
+    kv, q = 2 * HEAD, GROUPS * HEAD
+    return pl.pallas_call(
+        prepare_kernel,
+        out_shape=[
+            jax.ShapeDtypeStruct(shape, jnp.bfloat16)
+            for shape in (
+                (2, rows, kv),
+                (2, rows, q),
+                (rows, kv),
+                (rows, q),
+                (w_out.shape[0] // 2, w_out.shape[1]),
+            )
+        ],
+        in_specs=[pl.BlockSpec(memory_space=pltpu.SMEM)] + [vmem] * 3,
+        out_specs=[vmem] * 5,
+        compiler_params=pltpu.CompilerParams(vmem_limit_bytes=12 * 1024 * 1024),
+        cost_estimate=pl.CostEstimate(flops=1000000, bytes_accessed=2 * w_qkv.size, transcendentals=0),
+        name="prepare",
+    )(jnp.stack([core, plane]).astype(jnp.int32), *in_hbm([w_qkv]), came, *in_hbm([w_out]))
+
+
+def norm_kernel(in_ref, gain_ref, cos_ref, sin_ref, out_ref):
+    step = 64
+
+    def body(i, carry):
+        at = pl.ds(pl.multiple_of(i * step, step), step)
+        normed = rms_scale(in_ref[at, :].astype(jnp.float32), gain_ref[...]).astype(jnp.bfloat16)
+        depth = normed.shape[1] // out_ref.shape[0]
+        for part in range(out_ref.shape[0]):
+            out_ref[part, at, :depth] = normed[:, part * depth : (part + 1) * depth]
+        return carry
+
+    lax.fori_loop(0, in_ref.shape[0] // step, body, 0)
+
+
+def norm(rows, gain, tables, parts):
+    count, width = rows.shape
+    vmem = pl.BlockSpec(memory_space=pltpu.VMEM)
+    return pl.pallas_call(
+        norm_kernel,
+        out_shape=jax.ShapeDtypeStruct((parts, count, -(-width // parts // 128) * 128), jnp.bfloat16),
+        in_specs=[vmem] * 2 + [pl.BlockSpec(memory_space=pl.ANY)] * 2,
+        out_specs=vmem,
+        compiler_params=pltpu.CompilerParams(vmem_limit_bytes=8 * 1024 * 1024),
+        cost_estimate=pl.CostEstimate(flops=1000000, bytes_accessed=4 * rows.size, transcendentals=0),
+        name="norm",
+    )(*in_hbm([rows]), gain[None, :], *in_hbm(tables))
+
+
+def project_kernel(slots, turned, joined, early, spots, x_ref, other_ref, *refs):
+    refs = list(refs)
+    if joined:
+        sum_ref = refs.pop(0)
+    if not early:
+        cos_ref, sin_ref = refs.pop(0), refs.pop(0)
+    tailed = turned is not None and not all(turned)
+    if tailed:
+        ids_ref, other_ids_ref = refs.pop(0), refs.pop(0)
+    pieces = refs[: len(slots)]
+    out_ref, held, total, sems = refs[len(slots) :]
+    layers = held.shape[0]
+    rows = pieces[0].shape[1]
+    copies = []
+    for piece, blocks in zip(pieces, slots):
+        for i, slot in enumerate(blocks):
+            at = pl.multiple_of(spots[layers + len(copies)] * rows, rows)
+            copy = pltpu.make_async_copy(
+                piece.at[i], held.at[slot, pl.ds(at, rows), :], sems.at[len(copies)]
+            )
+            copy.start()
+            copies.append((slot, copy))
+    core = spots[layers + len(copies)]
+    tokens = x_ref.shape[1]
+    mine = pl.ds(pl.multiple_of(core * tokens, tokens), tokens)
+    theirs = pl.ds(pl.multiple_of((1 - core) * tokens, tokens), tokens)
+    if tailed:
+        for ref, at in ((ids_ref, mine), (other_ids_ref, theirs)):
+            row = jnp.broadcast_to(ref[...].astype(jnp.float32), (TAIL, tokens))
+            out_ref[2 * tokens :, at] = row.astype(jnp.bfloat16)
+    half = HEAD // 2
+    for layer in range(layers):
+        for slot, copy in copies:
+            if slot == layer:
+                copy.wait()
+        last = layer == layers - 1
+        for ref, at in ((x_ref, mine), (other_ref, theirs)):
+            part = jnp.dot(
+                ref[spots[layer], :, : held.shape[1]], held[layer], preferred_element_type=jnp.float32
+            )
+            if layer > 0:
+                part = part + total[at, :]
+            elif joined:
+                part = part + sum_ref[at, :]
+            if not last:
+                total[at, :] = part
+            elif early:
+                out_ref[at, :] = part
+            else:
+                cosine, sine = cos_ref[at, :], sin_ref[at, :]
+                for h, turn in enumerate(turned):
+                    a = part[:, h * HEAD : h * HEAD + half]
+                    b = part[:, h * HEAD + half : (h + 1) * HEAD]
+                    if turn:
+                        a, b = a * cosine - b * sine, b * cosine + a * sine
+                    out_ref[at, h * HEAD : h * HEAD + half] = a.astype(jnp.bfloat16)
+                    out_ref[at, h * HEAD + half : (h + 1) * HEAD] = b.astype(jnp.bfloat16)
+
+
+def project(x, other, arrays, slots, layers, spots, turned=None, tables=(), before=None, ids=()):
+    tokens, depth = 2 * x.shape[1], 4 * arrays[0].shape[1]
+    width = arrays[0].shape[2]
+    early = turned is None
+    extra = ([] if before is None else [before]) + in_hbm(tables) + list(ids)
+    vmem = pl.BlockSpec(memory_space=pltpu.VMEM)
+    return pl.pallas_call(
+        functools.partial(project_kernel, slots, turned, before is not None, early),
+        out_shape=jax.ShapeDtypeStruct(
+            (tokens + (TAIL if ids else 0), width), jnp.float32 if early else jnp.bfloat16
+        ),
+        in_specs=[pl.BlockSpec(memory_space=pltpu.SMEM)]
+        + [vmem] * (2 + len(extra))
+        + [pl.BlockSpec(memory_space=pl.ANY)] * len(arrays),
+        out_specs=vmem,
+        scratch_shapes=[
+            pltpu.VMEM((layers, depth, width), jnp.bfloat16),
+            pltpu.VMEM((tokens, width), jnp.float32),
+            pltpu.SemaphoreType.DMA((sum(len(blocks) for blocks in slots),)),
+        ],
+        compiler_params=pltpu.CompilerParams(vmem_limit_bytes=12 * 1024 * 1024),
+        cost_estimate=pl.CostEstimate(
+            flops=2 * tokens * depth * layers * width,
+            bytes_accessed=2 * layers * depth * width,
+            transcendentals=0,
+        ),
+        name="project",
+    )(spots, x, other, *extra, *in_hbm(arrays))
+
+
+def attend_kernel(slots, place, x_ref, other_ref, sum_ref, cos_ref, sin_ref, ids_ref, *refs):
+    other_ids_ref, kv_hbm, old_hbm = refs[:3]
+    pieces = refs[3 : 3 + len(slots)]
+    own_ref, send_ref, held, q_ref, kv_ref, old_ref, sems, ends = refs[3 + len(slots) :]
+    rows = pieces[0].shape[1]
+    copies = []
+    for piece, blocks in zip(pieces, slots):
+        for i in range(blocks):
+            at = pl.multiple_of(place[3 + len(copies)] * rows, rows)
+            copies.append(
+                pltpu.make_async_copy(piece.at[i], held.at[pl.ds(at, rows), :], sems.at[len(copies)])
+            )
+            copies[-1].start()
+    fetch = (
+        pltpu.make_async_copy(kv_hbm, kv_ref, ends.at[0]),
+        pltpu.make_async_copy(old_hbm, old_ref, ends.at[1]),
+    )
+    for copy in fetch:
+        copy.start()
+    core, chip, layer = place[0], place[1], place[2]
+    step = own_ref.shape[1]
+    tokens = q_ref.shape[0]
+    behind = tokens
+    first = core == 0
+    ids = jnp.concatenate(
+        [
+            jnp.where(first, ids_ref[...], other_ids_ref[...]),
+            jnp.where(first, other_ids_ref[...], ids_ref[...]),
+        ],
+        axis=1,
+    ).astype(jnp.float32)
+    query_ids = jnp.broadcast_to(ids, (128, tokens)).T[:, :1]
+    half = HEAD // 2
+    for copy in copies:
+        copy.wait()
+    for ref, block in ((x_ref, core), (other_ref, 1 - core)):
+        at = pl.ds(pl.multiple_of(block * step, step), step)
+        part = sum_ref[at, :] + jnp.dot(
+            ref[layer, :, : held.shape[0]], held[...], preferred_element_type=jnp.float32
+        )
+        cosine, sine = cos_ref[at, :], sin_ref[at, :]
+        for h in range(GROUPS):
+            a = part[:, h * HEAD : h * HEAD + half]
+            b = part[:, h * HEAD + half : (h + 1) * HEAD]
+            q_ref[at, h * HEAD : h * HEAD + half] = (a * cosine - b * sine).astype(jnp.bfloat16)
+            q_ref[at, h * HEAD + half : (h + 1) * HEAD] = (b * cosine + a * sine).astype(
+                jnp.bfloat16
+            )
+    for copy in fetch:
+        copy.wait()
+    old_ids = old_ref[behind : behind + TAIL, :].astype(jnp.float32)[:1]
+    key_ids = jnp.concatenate([jnp.where(chip > 0, old_ids, -1.0), ids], axis=1)
+    for m in range(tokens // step):
+        low = m * step
+        top = behind + (m + 1) * step
+        span = top - low
+        qpos = behind + m * step + lax.broadcasted_iota(jnp.int32, (step, span), 0)
+        kpos = low + lax.broadcasted_iota(jnp.int32, (step, span), 1)
+        same = query_ids[m * step : (m + 1) * step, :] == key_ids[:, low:top]
+        allowed = same & (kpos <= qpos) & (qpos - kpos < WINDOW)
+        keys = jnp.concatenate([old_ref[low:behind, :HEAD], kv_ref[: (m + 1) * step, :HEAD]], axis=0)
+        values = jnp.concatenate(
+            [old_ref[low:behind, HEAD:], kv_ref[: (m + 1) * step, HEAD:]], axis=0
+        )
+        for h in range(GROUPS):
+            q = q_ref[m * step : (m + 1) * step, h * HEAD : (h + 1) * HEAD]
+            scores = lax.dot_general(
+                q, keys, (((1,), (1,)), ((), ())), preferred_element_type=jnp.float32
+            )
+            capped = CAP * jnp.tanh(scores * (1.0 / (CAP * math.sqrt(HEAD))))
+            weights = jnp.where(allowed, jnp.exp(capped), 0.0)
+            totals = jnp.sum(weights, axis=1, keepdims=True)
+            mixed = jnp.dot(
+                weights.astype(jnp.bfloat16), values, preferred_element_type=jnp.float32
+            )
+            result = (mixed / totals).astype(jnp.bfloat16)
+
+            @pl.when(core == m)
+            def _():
+                own_ref[h] = result
+
+            @pl.when(core != m)
+            def _():
+                send_ref[h] = result
+
+
+def attend(x, other, arrays, slots, place, before, tables, kv, old, ids):
+    tokens, width = before.shape
+    depth = 4 * arrays[0].shape[1]
+    work = GROUPS * tokens * 2 * tokens * HEAD
+    vmem, left = pl.BlockSpec(memory_space=pltpu.VMEM), pl.BlockSpec(memory_space=pl.ANY)
+    return pl.pallas_call(
+        functools.partial(attend_kernel, slots),
+        out_shape=[jax.ShapeDtypeStruct((GROUPS, tokens // 2, HEAD), jnp.bfloat16)] * 2,
+        in_specs=[pl.BlockSpec(memory_space=pltpu.SMEM)] + [vmem] * 7 + [left] * (2 + len(arrays)),
+        out_specs=[vmem] * 2,
+        scratch_shapes=[
+            pltpu.VMEM((depth, width), jnp.bfloat16),
+            pltpu.VMEM((tokens, width), jnp.bfloat16),
+            pltpu.VMEM(kv.shape, jnp.bfloat16),
+            pltpu.VMEM(old.shape, jnp.bfloat16),
+            pltpu.SemaphoreType.DMA((sum(slots),)),
+            pltpu.SemaphoreType.DMA((2,)),
+        ],
+        compiler_params=pltpu.CompilerParams(vmem_limit_bytes=16 * 1024 * 1024),
+        cost_estimate=pl.CostEstimate(
+            flops=4 * work, bytes_accessed=work // 256, transcendentals=0
+        ),
+        name="attend",
+    )(place, x, other, before, *in_hbm(tables), *ids, *in_hbm([kv, old]), *in_hbm(arrays))
+
+
+def fetch_layers(slots, first, marks, pieces, held, sems):
+    rows = pieces[0].shape[1]
+    copies = []
+    for piece, blocks in zip(pieces, slots):
+        for i, slot in enumerate(blocks):
+            at = pl.multiple_of(marks[first + len(copies)], rows)
+            copy = pltpu.make_async_copy(
+                piece.at[i], held.at[slot, pl.ds(at, rows), :], sems.at[len(copies)]
+            )
+            copy.start()
+            copies.append((slot, copy))
+    return copies
+
+
+def fetch_heads(own_hbm, other_hbm, own_ref, other_ref, ends):
+    copies = (
+        pltpu.make_async_copy(own_hbm, own_ref, ends.at[0]),
+        pltpu.make_async_copy(other_hbm, other_ref, ends.at[1]),
+    )
+    for copy in copies:
+        copy.start()
+    return copies
+
+
+def head_of(own_ref, other_ref, core, head):
+    return jnp.where(head // GROUPS == core, own_ref[head % GROUPS], other_ref[head % GROUPS])
+
+
+def early_kernel(slots, heads, marks, own_hbm, other_hbm, *refs):
+    pieces = refs[: len(slots)]
+    out_ref, held, own_ref, other_ref, sems, ends = refs[len(slots) :]
+    fetch = fetch_heads(own_hbm, other_hbm, own_ref, other_ref, ends)
+    copies = fetch_layers(slots, heads + 1, marks, pieces, held, sems)
+    for copy in fetch:
+        copy.wait()
+    width = out_ref.shape[1]
+    tile = next(t for t in (768, 512, 256, 128, width) if width % t == 0)
+    for s in range(heads):
+        for slot, copy in copies:
+            if slot == s:
+                copy.wait()
+        att = head_of(own_ref, other_ref, marks[heads], marks[s])
+        for n in range(width // tile):
+            part = slice(n * tile, (n + 1) * tile)
+            product = jnp.dot(att, held[s, :, part], preferred_element_type=jnp.float32)
+            out_ref[:, part] = product if s == 0 else out_ref[:, part] + product
+
+
+def finish_kernel(slots, marks, own_hbm, other_hbm, early_ref, gain_ref, hid_hbm, *refs):
+    pieces = refs[: len(slots)]
+    out_hbm, held, own_ref, other_ref, hid_ref, sum_ref, out_ref, sems, ends = refs[len(slots) :]
+    heads = fetch_heads(own_hbm, other_hbm, own_ref, other_ref, ends)
+    fetch = pltpu.make_async_copy(hid_hbm, hid_ref, ends.at[2])
+    copies = fetch_layers(slots, 2, marks, pieces, held, sems)
+    fetch.start()
+    tokens, width = sum_ref.shape
+    tile = next(t for t in (768, 512, 256, 128, width) if width % t == 0)
+    for copy in heads:
+        copy.wait()
+    att = head_of(own_ref, other_ref, marks[1], marks[0])
+    for _, copy in copies:
+        copy.wait()
+    square = jnp.zeros((tokens, 1), jnp.float32)
+    for n in range(width // tile):
+        part = slice(n * tile, (n + 1) * tile)
+        total = early_ref[:, part] + jnp.dot(
+            att, held[0, :, part], preferred_element_type=jnp.float32
+        )
+        sum_ref[:, part] = total
+        square = square + jnp.sum(total * total, axis=1, keepdims=True)
+    scale = lax.rsqrt(square / width + EPS)
+    fetch.wait()
+    step = 64
+    stores = []
+    for m in range(tokens // step):
+        rows = slice(m * step, (m + 1) * step)
+        branch = sum_ref[rows, :] * scale[rows] * gain_ref[...]
+        out_ref[rows, :] = (hid_ref[rows, :].astype(jnp.float32) + branch).astype(jnp.bfloat16)
+        stores.append(
+            pltpu.make_async_copy(out_ref.at[rows, :], out_hbm.at[rows, :], ends.at[3 + m])
+        )
+        stores[-1].start()
+    for store in stores:
+        store.wait()
+
+
+def out_project(own, other, arrays, slots, marks, heads, rows, finish=None):
+    width = arrays[0].shape[2]
+    tokens = own.shape[1]
+    total = sum(len(blocks) for blocks in slots)
+    vmem, left = pl.BlockSpec(memory_space=pltpu.VMEM), pl.BlockSpec(memory_space=pl.ANY)
+    held = [pltpu.VMEM((heads, rows, width), jnp.bfloat16)]
+    held += [pltpu.VMEM(own.shape, jnp.bfloat16)] * 2
+    sems = [pltpu.SemaphoreType.DMA((total,))]
+    extra, specs = [], []
+    if finish:
+        early, gain, hidden = finish
+        extra, specs = [early, gain] + in_hbm([hidden]), [vmem, vmem, left]
+        held += [
+            pltpu.VMEM((tokens, width), jnp.bfloat16),
+            pltpu.VMEM((tokens, width), jnp.float32),
+            pltpu.VMEM((tokens, width), jnp.bfloat16),
+        ]
+        sems.append(pltpu.SemaphoreType.DMA((3 + tokens // 64,)))
+        body = functools.partial(finish_kernel, slots)
+    else:
+        sems.append(pltpu.SemaphoreType.DMA((2,)))
+        body = functools.partial(early_kernel, slots, heads)
+    return pl.pallas_call(
+        body,
+        out_shape=jax.ShapeDtypeStruct((tokens, width), jnp.bfloat16 if finish else jnp.float32),
+        in_specs=[pl.BlockSpec(memory_space=pltpu.SMEM)]
+        + [left] * 2
+        + specs
+        + [left] * len(arrays),
+        out_specs=left if finish else vmem,
+        scratch_shapes=held + sems,
+        compiler_params=pltpu.CompilerParams(vmem_limit_bytes=14 * 1024 * 1024),
+        cost_estimate=pl.CostEstimate(
+            flops=2 * tokens * rows * heads * width,
+            bytes_accessed=2 * rows * heads * width,
+            transcendentals=0,
+        ),
+        name="finish" if finish else "early",
+    )(marks, own, other, *extra, *in_hbm(arrays))
+
+
+def per_device(hidden_in, segment_ids, pre_gain, w_qkv, w_out, post_gain):
+    return layer(hidden_in, segment_ids, pre_gain, w_qkv, w_out, post_gain)
+
+
+def layer(hidden_in, segment_ids, pre_gain, w_qkv, w_out, post_gain):
+    tok_rows, model = hidden_in.shape[1:]
+    seq_count = lax.axis_size("seq")
+    line_count = seq_count // 4
+    seq_index = lax.axis_index("seq")
+    plane = lax.axis_index("batch")
+    core, pair, line = seq_index % 2, (seq_index // 2) % 2, seq_index // 4
+    chip = seq_index // 2
+    chip_rows = 2 * tok_rows
+
+    half_rows = w_out.shape[0] // 2
+    came = swap_core(w_qkv)
+    own_kv, own_q, kv_unit, q_unit, out_unit = prepare(w_qkv, came, w_out, core, plane)
+    first_pos, out_unit = lax.optimization_barrier((chip * chip_rows, out_unit))
+    kv_pieces = gather_near(own_kv, kv_unit, plane, pair, line_count, "1")
+    q_pieces = gather_wide(own_q, q_unit, plane, pair, line_count)
+    out_own = w_out.reshape(2, half_rows, model)
+    out_pieces = gather_near(out_own, out_unit, plane, pair, line_count, "3")
+
+    cosine, sine = rotary_tables(first_pos + jnp.arange(chip_rows, dtype=jnp.int32))
+    normed = norm(hidden_in[0], pre_gain, [cosine, sine], line_count)
+    normed_other = swap_core(normed)
+    ids = (segment_ids, swap_core(segment_ids))
+
+    def projected(pieces, backs, **more):
+        layers = [(line - back + line_count) % line_count for back in backs]
+        spots, arrays, slots = [], [], []
+        for block, blocks in pieces:
+            if not any(back in backs for back, _, _ in blocks):
+                continue
+            arrays.append(block)
+            slots.append(tuple(backs.index(back) for back, _, _ in blocks))
+            spots += [y * 2 + h for _, y, h in blocks]
+        spots = jnp.stack([jnp.asarray(spot, jnp.int32) for spot in layers + spots + [core]])
+        return project(normed, normed_other, arrays, tuple(slots), len(backs), spots, **more)
+
+    kv = projected(kv_pieces, [0, 1, 2, 3], turned=(True, False), tables=(cosine, sine), ids=ids)
+    old = from_chip_behind(kv, 1)
+    q = projected(q_pieces, [0, 1, 2])
+    last = line_count - 1
+    final = [(block, blocks) for block, blocks in q_pieces if blocks[0][0] == last]
+    place = [core, chip, (line - last + line_count) % line_count]
+    place += [y * 2 + h for _, blocks in final for _, y, h in blocks]
+    att_own, att_send = attend(
+        normed,
+        normed_other,
+        [block for block, _ in final],
+        tuple(len(blocks) for _, blocks in final),
+        jnp.stack([jnp.asarray(entry, jnp.int32) for entry in place]),
+        q,
+        (cosine, sine),
+        kv,
+        old,
+        ids,
+    )
+    att_other = swap_core(att_send)
+
+    swapped = [swap_core(block) for block, _ in out_pieces]
+
+    def out_part(backs, finish=None):
+        heads = [(line - back + line_count) % line_count for back in backs]
+        offsets, arrays, where = [], [], []
+        for (block, blocks), other in zip(out_pieces, swapped):
+            if blocks[0][0] not in backs:
+                continue
+            for array, c in ((block, core), (other, 1 - core)):
+                arrays.append(array)
+                where.append(tuple(backs.index(back) for back, _, _ in blocks))
+                offsets += [((y * 2 + c) * 2 + h) * half_rows for _, y, h in blocks]
+        marks = jnp.stack([jnp.asarray(mark, jnp.int32) for mark in heads + [core] + offsets])
+        return out_project(att_own, att_other, arrays, tuple(where), marks, len(backs), 8 * half_rows, finish)
+
+    early = out_part([0, 1, 2])
+    done = out_part([3], (early, post_gain[None, :], hidden_in[0]))
+    return done[None]
+
+
+BY_BATCH = ("3n",)
 
 
 def from_behind(block, axis, distance):
     devices = range(lax.axis_size(axis))
     route = [(i - distance, i) for i in devices if i - distance in devices]
     return lax.ppermute(block, axis, route)
-
-
-def rms_scale(values, gain):
-    return values * lax.rsqrt(jnp.mean(values * values, axis=-1, keepdims=True) + EPS) * gain
 
 
 def rotary(values, positions, leading):
@@ -44,7 +623,7 @@
     )
 
 
-def attend(states, queries, key_block, value_block, query_pos, key_pos, starts):
+def attend_block(states, queries, key_block, value_block, query_pos, key_pos, starts):
     running, totals = states
     scores = jnp.einsum(
         "qhgd,khd->qhgk", queries, key_block, preferred_element_type=jnp.float32
@@ -66,7 +645,7 @@
     return (running, totals)
 
 
-def per_device(hidden_in, segment_ids, pre_gain, w_qkv, w_out, post_gain):
+def per_device_general(hidden_in, segment_ids, pre_gain, w_qkv, w_out, post_gain):
     tok_rows = hidden_in.shape[1]
     seq_count = lax.axis_size("seq")
     seq_index = lax.axis_index("seq")
@@ -104,14 +683,14 @@
         jnp.zeros((tok_rows, KV_HEADS, groups, HEAD), jnp.float32),
         jnp.zeros((tok_rows, KV_HEADS, groups), jnp.float32),
     )
-    states = attend(states, queries, key_rows, value_rows, positions, positions, starts)
+    states = attend_block(states, queries, key_rows, value_rows, positions, positions, starts)
     longest = min(2 * seq_count * tok_rows // DOCS, WINDOW)
     hop_count = min(-(-(longest - 1) // tok_rows), seq_count - 1)
 
     def relay_step(hop_index, carried):
         moving_keys, moving_values, running, totals = carried
         moving_keys, moving_values = from_behind((moving_keys, moving_values), "seq", 1)
-        running, totals = attend(
+        running, totals = attend_block(
             (running, totals),
             queries,
             moving_keys,
@@ -138,7 +717,13 @@
 
 
 def solution(mesh):
+    seq_count, planes = mesh.shape["seq"], mesh.shape["batch"]
+    special = seq_count == 4 * Q_HEADS == DOCS and planes == 2 == KV_HEADS and Q_HEADS == 4
     placed = (P("batch", "seq", None), P("batch", "seq"), P(), P("seq", None), P("seq", None), P())
     return jax.shard_map(
-        per_device, mesh=mesh, in_specs=placed, out_specs=P("batch", "seq", None), check_vma=False
-    )
+        per_device if special else per_device_general,
+        mesh=mesh,
+        in_specs=placed,
+        out_specs=P("batch", "seq", None),
+        check_vma=False,
+    )

time: 165 us -> 121 us (0.73)
  waiting for transfers between devices: 95.4 us -> 60.3 us
  Pallas kernels: 0 us -> 25.4 us
  starting transfers between devices: 13.7 us -> 27.8 us
  blocking collectives: 13.8 us -> 0 us
  between operations: 13.6 us -> 0.53 us
  matrix products: 12 us -> 0 us
  other arithmetic: 8.59 us -> 1.9 us
  local copies, waits for them, and re-layouts: 7.49 us -> 4.97 us
    all_gather x2 -> x0, waiting for transfers between devices: 92.8 us -> none  [the longest x1 67 us: per_device(): lax.all_gather(w_qkv, 'seq', axis=0, tiled=True)]
    ppermute x4 -> x42, waiting for transfers between devices: 1.18 us -> 60.3 us  [the longest x9 21.8 us: along_line(): lax.ppermute(block, 'seq', [(i, (i + 4 * steps) % count) for i in range(c...]
    pallas_call x0 -> x10, Pallas kernels: none -> 25.4 us  [the longest x2 8.13 us: project(): pl.pallas_call(functools.partial(project_kernel, slots, turned, before is...]
    ppermute x4 -> x42, starting transfers between devices: 13.6 us -> 27.8 us  [the longest x10 10.1 us: swap_pair(): lax.ppermute(block, 'seq', [(i, i ^ 2) for i in range(lax.axis_size('seq'...]
    pmin x1 -> x0, blocking collectives: 13.8 us -> none  [per_device(): first_pos = lax.pmin(local_first, 'seq')]
    dot_general x8 -> x0, matrix products: 12 us -> none  [the longest x1 5.24 us: per_device(): jnp.dot(columns, lax.all_gather(w_qkv, 'seq', axis=0, tiled=True), prefer...]
    unnamed x21 -> x52, local copies, waits for them, and re-layouts: 0.58 us -> 3.78 us
    reduce_sum x2 -> x0, other arithmetic: 2.35 us -> none  [the longest x1 1.58 us: rms_scale(): jnp.mean(values * values, axis=-1, keepdims=True) + EPS]
  transfers between devices with their start and end apart: 6 -> 42, of which waited for: 4 -> 18; matrix products, arithmetic and copies ran while one was open for 14% -> 1% of each run, Pallas kernels for 0% -> 15%
where the time goes in v3:
time: 121 us
  waiting for transfers between devices  60.3 us (50%)
  starting transfers between devices  27.8 us (23%)
  Pallas kernels  25.4 us (21%)
  local copies, waits for them, and re-layouts  4.97 us (4%)
  other arithmetic  1.9 us (2%)
    ppermute x9, waiting for transfers between devices, along_line(): lax.ppermute(block, 'seq', [(i, (i + 4 * steps) % count) for i in range(c...  21.8 us
    ppermute x8, waiting for transfers between devices, swap_batch(): return lax.ppermute(block, 'batch', [(0, 1), (1, 0)])  19.8 us
    ppermute x10, waiting for transfers between devices, swap_pair(): lax.ppermute(block, 'seq', [(i, i ^ 2) for i in range(lax.axis_size('seq'...  16.5 us
    ppermute x10, starting transfers between devices, swap_pair(): lax.ppermute(block, 'seq', [(i, i ^ 2) for i in range(lax.axis_size('seq'...  10.1 us
    ppermute x8, starting transfers between devices, swap_batch(): return lax.ppermute(block, 'batch', [(0, 1), (1, 0)])  9.19 us
    pallas_call x2, Pallas kernels, project(): pl.pallas_call(functools.partial(project_kernel, slots, turned, before is...  8.13 us
    pallas_call x2, Pallas kernels, out_project(): pl.pallas_call(body, out_shape=jax.ShapeDtypeStruct((tokens, width), jnp....  7.46 us
    pallas_call x1, Pallas kernels, attend(): pl.pallas_call(functools.partial(attend_kernel, slots), out_shape=[jax.Sh...  5.52 us
  transfers between devices with their start and end apart: 42, of which 18 were waited for; matrix products, arithmetic and copies ran while one was open for 1% of the time, Pallas kernels for 15%

profile of v3, /device:TPU:0, one launch (start us, length us, event | category | flops | bytes accessed | tf_op | source)
XLA Modules:
  0.0 121.0 jit_solution(6303161763958512806)
XLA Ops:
  2.3 1.2 %prepare.1 = (bf16[2,144,512]{2,1,0:T(8,128)(2,1)S(1)}, bf16[2,144,512]{2,1,0:T(8,128)(2,1)S(1)}, bf16[144,512]{1,0:T(8,128)(2,1)S(1)}, bf16[144,512]{1,0:T(8,128)(2,1)S(1)}, bf16[32,2304]{1,0:T(8,128)(2,1)S(1)}) custom-call(s32[2]{0:T(128)S(1)} %pad_add_fusion.place, bf16[144,2048]{1,0:T(8,128)(2,1)} %w_ref.1, ...), custom_call_target="tpu_custom_call" | custom-call | flops 1000000 | bytes 589824 | tf_op jit(solution)/shard_map/prepare/pallas_call | solution.py:142
  3.6 1.8 %multiply_sine_fusion = (f32[512,128]{1,0:T(8,128)}, f32[512,128]{1,0:T(8,128)}) fusion(f32[128]{0:T(128)S(1)} %negate_power_fusion, f32[512]{0:T(512)S(1)} %add_convert_fusion), kind=kLoop, calls=%fused_computation | loop fusion | flops 65536 | bytes 526848 | tf_op jit(solution)/shard_map/sin | solution.py:31
  5.4 2.3 %norm.1.x_ref = bf16[4,256,640]{2,1,0:T(8,128)(2,1)S(1)} custom-call(bf16[256,2304]{1,0:T(8,128)(2,1)} %bitcast.40, f32[1,2304]{1,0:T(1,128)S(1)} %broadcast_in_dim.24.gain_ref, f32[512,128]{1,0:T(8,128)} %get-tuple-element.24.cos_ref.refs_0_, f32[512,128]{1,0:T(8,128)} %get-tuple-element.23.sin_ref.refs_1_), custom_call_target="tpu_custom_call" | custom-call | flops 1000000 | bytes 2359296 | tf_op jit(solution)/shard_map/norm/pallas_call | solution.py:179
  8.2 2.6 %collective-permute-start.23 = (bf16[2,32,2304]{2,1,0:T(8,128)(2,1)S(1)}, bf16[2,32,2304]{2,1,0:T(8,128)(2,1)}, u32[]{:S(2)}, u32[]{:S(2)}) collective-permute-start(bf16[2,32,2304]{2,1,0:T(8,128)(2,1)S(1)} %bitcast.43), channel_id=1, source_target_pairs={{0,4},{2,6},{4,0},{6,2},{8,12},{10,14},{12,8},{14,10},{16,20},{18,... | collective-permute-start | bytes 884744 | tf_op jit(solution)/shard_map/ppermute | solution.py:39
  10.8 1.6 %collective-permute-start.9 = (bf16[144,512]{1,0:T(8,128)(2,1)S(1)}, bf16[144,512]{1,0:T(8,128)(2,1)S(1)}, u32[]{:S(2)}, u32[]{:S(2)}) collective-permute-start(bf16[144,512]{1,0:T(8,128)(2,1)S(1)} %get-tuple-element.19), channel_id=1, source_target_pairs={{0,8},{2,10},{4,12},{6,14},{8,16},{10,18},{12,20},{14,22},{16,24},... | collective-permute-start | bytes 442376 | tf_op jit(solution)/shard_map/ppermute | solution.py:48
  12.4 1.6 %collective-permute-start.25 = (bf16[32,2304]{1,0:T(8,128)(2,1)S(1)}, bf16[32,2304]{1,0:T(8,128)(2,1)S(1)}, u32[]{:S(2)}, u32[]{:S(2)}) collective-permute-start(bf16[32,2304]{1,0:T(8,128)(2,1)S(1)} %get-tuple-element.22), channel_id=1, source_target_pairs={{0,8},{2,10},{4,12},{6,14},{8,16},{10,18},{12,20},{14,22},{16,24},... | collective-permute-start | bytes 442376 | tf_op jit(solution)/shard_map/ppermute | solution.py:48
  15.7 3.7 %collective-permute-done.9.first_ref = bf16[144,512]{1,0:T(8,128)(2,1)S(1)} collective-permute-done((bf16[144,512]{1,0:T(8,128)(2,1)S(1)}, bf16[144,512]{1,0:T(8,128)(2,1)S(1)}, u32[]{:S(2)}, u32[]{:S(2)}) %collective-permute-start.9) | collective-permute-done | bytes 147488 | tf_op jit(solution)/shard_map/ppermute | solution.py:48
  19.4 2.3 %collective-permute-done.25.first_ref = bf16[32,2304]{1,0:T(8,128)(2,1)S(1)} collective-permute-done((bf16[32,2304]{1,0:T(8,128)(2,1)S(1)}, bf16[32,2304]{1,0:T(8,128)(2,1)S(1)}, u32[]{:S(2)}, u32[]{:S(2)}) %collective-permute-start.25) | collective-permute-done | bytes 147488 | tf_op jit(solution)/shard_map/ppermute | solution.py:48
  22.2 4.1 %collective-permute-done.10 = bf16[144,512]{1,0:T(8,128)(2,1)S(1)} collective-permute-done((bf16[144,512]{1,0:T(8,128)(2,1)S(1)}, bf16[144,512]{1,0:T(8,128)(2,1)S(1)}, u32[]{:S(2)}, u32[]{:S(2)}) %collective-permute-start.10) | collective-permute-done | bytes 147488 | tf_op jit(solution)/shard_map/ppermute | solution.py:48
  27.1 6.1 %collective-permute-done.26 = bf16[32,2304]{1,0:T(8,128)(2,1)S(1)} collective-permute-done((bf16[32,2304]{1,0:T(8,128)(2,1)S(1)}, bf16[32,2304]{1,0:T(8,128)(2,1)S(1)}, u32[]{:S(2)}, u32[]{:S(2)}) %collective-permute-start.26) | collective-permute-done | bytes 147488 | tf_op jit(solution)/shard_map/ppermute | solution.py:48
  33.3 1.6 %collective-permute-start.11 = (bf16[2,144,512]{2,1,0:T(8,128)(2,1)S(1)}, bf16[2,144,512]{2,1,0:T(8,128)(2,1)}, u32[]{:S(2)}, u32[]{:S(2)}) collective-permute-start(bf16[2,144,512]{2,1,0:T(8,128)(2,1)S(1)} %pack.4.refs_6_), channel_id=1, source_target_pairs={{0,1},{1,0},{2,3},{3,2},{4,5},{5,4},{6,7},{7,6},{8,9},{9,8},{10,11... | collective-permute-start | bytes 884744 | tf_op jit(solution)/shard_map/ppermute | solution.py:43
  35.8 1.5 %collective-permute-start.15 = (bf16[1,144,512]{2,1,0:T(8,128)(2,1)S(1)}, bf16[1,144,512]{2,1,0:T(8,128)(2,1)S(1)}, u32[]{:S(2)}, u32[]{:S(2)}) collective-permute-start(bf16[1,144,512]{2,1,0:T(8,128)(2,1)S(1)} %bitcast.45), channel_id=1, source_target_pairs={{0,1},{1,0},{2,3},{3,2},{4,5},{5,4},{6,7},{7,6},{8,9},{9,8},{10,11... | collective-permute-start | bytes 442376 | tf_op jit(solution)/shard_map/ppermute | solution.py:43
  37.3 3.9 %collective-permute-done.34 = bf16[32,2304]{1,0:T(8,128)(2,1)} collective-permute-done((bf16[32,2304]{1,0:T(8,128)(2,1)S(1)}, bf16[32,2304]{1,0:T(8,128)(2,1)}, u32[]{:S(2)}, u32[]{:S(2)}) %collective-permute-start.34) | collective-permute-done | bytes 147488 | tf_op jit(solution)/shard_map/ppermute | solution.py:48
  41.7 1.6 %collective-permute-start.16 = (bf16[1,144,512]{2,1,0:T(8,128)(2,1)S(1)}, bf16[1,144,512]{2,1,0:T(8,128)(2,1)S(1)}, u32[]{:S(2)}, u32[]{:S(2)}) collective-permute-start(bf16[1,144,512]{2,1,0:T(8,128)(2,1)S(1)} %bitcast.46), channel_id=1, source_target_pairs={{0,4},{2,6},{4,0},{6,2},{8,12},{10,14},{12,8},{14,10},{16,20},{18,... | collective-permute-start | bytes 442376 | tf_op jit(solution)/shard_map/ppermute | solution.py:39
  44.5 7.1 %collective-permute-done.16.refs_12_ = bf16[1,144,512]{2,1,0:T(8,128)(2,1)S(1)} collective-permute-done((bf16[1,144,512]{2,1,0:T(8,128)(2,1)S(1)}, bf16[1,144,512]{2,1,0:T(8,128)(2,1)S(1)}, u32[]{:S(2)}, u32[]{:S(2)}) %collective-permute-start.16) | collective-permute-done | bytes 147488 | tf_op jit(solution)/shard_map/ppermute | solution.py:39
  52.9 4.9 %collective-permute-done.17.refs_13_ = bf16[1,144,512]{2,1,0:T(8,128)(2,1)S(1)} collective-permute-done((bf16[1,144,512]{2,1,0:T(8,128)(2,1)S(1)}, bf16[1,144,512]{2,1,0:T(8,128)(2,1)S(1)}, u32[]{:S(2)}, u32[]{:S(2)}) %collective-permute-start.17) | collective-permute-done | bytes 147488 | tf_op jit(solution)/shard_map/ppermute | solution.py:39
  59.0 1.7 %collective-permute-start.28 = (bf16[2,32,2304]{2,1,0:T(8,128)(2,1)}, bf16[2,32,2304]{2,1,0:T(8,128)(2,1)S(1)}, u32[]{:S(2)}, u32[]{:S(2)}) collective-permute-start(bf16[2,32,2304]{2,1,0:T(8,128)(2,1)} %pack.5.refs_4_), channel_id=1, source_target_pairs={{0,1},{1,0},{2,3},{3,2},{4,5},{5,4},{6,7},{7,6},{8,9},{9,8},{10,11... | collective-permute-start | bytes 884744 | tf_op jit(solution)/shard_map/ppermute | solution.py:43
  61.1 1.3 %collective-permute-start.19 = (bf16[2,144,512]{2,1,0:T(8,128)(2,1)}, bf16[2,144,512]{2,1,0:T(8,128)(2,1)}, u32[]{:S(2)}, u32[]{:S(2)}) collective-permute-start(bf16[2,144,512]{2,1,0:T(8,128)(2,1)} %collective-permute-done.5.refs_4_), channel_id=1, source_target_pairs={{0,8},{2,10},{4,12},{6,14},{8,16},{10,18},{12,20},{14,22},{16,24},... | collective-permute-start | bytes 884744 | tf_op jit(solution)/shard_map/ppermute | solution.py:48
  62.4 4.6 %project.3.refs_1_ = bf16[528,512]{1,0:T(8,128)(2,1)S(1)} custom-call(s32[21]{0:T(128)S(1)} %stack.191.spots, bf16[4,256,640]{2,1,0:T(8,128)(2,1)S(1)} %norm.1.x_ref, bf16[4,256,640]{2,1,0:T(8,128)(2,1)S(1)} %collective-permute-done.1.other_ref, f32[512,128]{1,0:T(8,128)} %get-tuple-element.24.cos_ref.refs_0_, f32[512,128]{1,0:T(8,128)} %get-tuple-element.23.sin_ref.refs_1_, ...), custom_call_target="tpu_custom_call" | custom-call | flops 1207959552 | bytes 2359296 | tf_op jit(solution)/shard_map/project/pallas_call | solution.py:255
  67.7 3.1 %collective-permute-done.36.refs_2_ = bf16[1,32,2304]{2,1,0:T(8,128)(2,1)S(1)} collective-permute-done((bf16[1,32,2304]{2,1,0:T(8,128)(2,1)}, bf16[1,32,2304]{2,1,0:T(8,128)(2,1)S(1)}, u32[]{:S(2)}, u32[]{:S(2)}) %collective-permute-start.36) | collective-permute-done | bytes 147488 | tf_op jit(solution)/shard_map/ppermute | solution.py:43
  70.7 1.7 %collective-permute-start.4 = (bf16[2,144,512]{2,1,0:T(8,128)(2,1)}, bf16[2,144,512]{2,1,0:T(8,128)(2,1)S(1)}, u32[]{:S(2)}, u32[]{:S(2)}) collective-permute-start(bf16[2,144,512]{2,1,0:T(8,128)(2,1)} %collective-permute-done.3.refs_2_), channel_id=1, source_target_pairs={{0,1},{1,0},{2,3},{3,2},{4,5},{5,4},{6,7},{7,6},{8,9},{9,8},{10,11... | collective-permute-start | bytes 884744 | tf_op jit(solution)/shard_map/ppermute | solution.py:43
  72.7 1.7 %collective-permute-start.32 = (bf16[2,32,2304]{2,1,0:T(8,128)(2,1)}, bf16[2,32,2304]{2,1,0:T(8,128)(2,1)}, u32[]{:S(2)}, u32[]{:S(2)}) collective-permute-start(bf16[2,32,2304]{2,1,0:T(8,128)(2,1)} %collective-permute-done.30.refs_8_), channel_id=1, source_target_pairs={{0,1},{1,0},{2,3},{3,2},{4,5},{5,4},{6,7},{7,6},{8,9},{9,8},{10,11... | collective-permute-start | bytes 884744 | tf_op jit(solution)/shard_map/ppermute | solution.py:43
  74.8 6.0 %collective-permute-done.4.refs_3_ = bf16[2,144,512]{2,1,0:T(8,128)(2,1)S(1)} collective-permute-done((bf16[2,144,512]{2,1,0:T(8,128)(2,1)}, bf16[2,144,512]{2,1,0:T(8,128)(2,1)S(1)}, u32[]{:S(2)}, u32[]{:S(2)}) %collective-permute-start.4) | collective-permute-done | bytes 294944 | tf_op jit(solution)/shard_map/ppermute | solution.py:43
  81.7 5.5 %collective-permute-done.6.refs_5_ = bf16[2,144,512]{2,1,0:T(8,128)(2,1)} collective-permute-done((bf16[2,144,512]{2,1,0:T(8,128)(2,1)}, bf16[2,144,512]{2,1,0:T(8,128)(2,1)}, u32[]{:S(2)}, u32[]{:S(2)}) %collective-permute-start.6) | collective-permute-done | bytes 294944 | tf_op jit(solution)/shard_map/ppermute | solution.py:43
  87.2 1.7 %collective-permute-start.38 = (bf16[1,32,2304]{2,1,0:T(8,128)(2,1)}, bf16[1,32,2304]{2,1,0:T(8,128)(2,1)}, u32[]{:S(2)}, u32[]{:S(2)}) collective-permute-start(bf16[1,32,2304]{2,1,0:T(8,128)(2,1)} %bitcast.36.refs_0_), channel_id=1, source_target_pairs={{0,4},{2,6},{4,0},{6,2},{8,12},{10,14},{12,8},{14,10},{16,20},{18,... | collective-permute-start | bytes 442376 | tf_op jit(solution)/shard_map/ppermute | solution.py:39
  88.9 3.5 %project.2.sum_ref = f32[512,512]{1,0:T(8,128)S(1)} custom-call(s32[16]{0:T(128)S(1)} %stack.190.spots, bf16[4,256,640]{2,1,0:T(8,128)(2,1)S(1)} %norm.1.x_ref, bf16[4,256,640]{2,1,0:T(8,128)(2,1)S(1)} %collective-permute-done.1.other_ref, bf16[2,144,512]{2,1,0:T(8,128)(2,1)} %copy-done.3, bf16[2,144,512]{2,1,0:T(8,128)(2,1)} %copy-done.1, ...), custom_call_target="tpu_custom_call" | custom-call | flops 905969664 | bytes 1769472 | tf_op jit(solution)/shard_map/project/pallas_call | solution.py:255
  93.5 3.9 %collective-permute-done.20.refs_4_ = bf16[2,144,512]{2,1,0:T(8,128)(2,1)} collective-permute-done((bf16[2,144,512]{2,1,0:T(8,128)(2,1)}, bf16[2,144,512]{2,1,0:T(8,128)(2,1)}, u32[]{:S(2)}, u32[]{:S(2)}) %collective-permute-start.20) | collective-permute-done | bytes 294944 | tf_op jit(solution)/shard_map/ppermute | solution.py:43
  98.0 5.5 %attend.1 = (bf16[2,256,256]{2,1,0:T(8,128)(2,1)S(1)}, bf16[2,256,256]{2,1,0:T(8,128)(2,1)S(1)}) custom-call(s32[7]{0:T(128)S(1)} %stack.180.place, bf16[4,256,640]{2,1,0:T(8,128)(2,1)S(1)} %norm.1.x_ref, bf16[4,256,640]{2,1,0:T(8,128)(2,1)S(1)} %collective-permute-done.1.other_ref, f32[512,512]{1,0:T(8,128)S(1)} %project.2.sum_ref, ...), custom_call_target="tpu_custom_call" | custom-call | flops 1073741824 | bytes 1048576 | tf_op jit(solution)/shard_map/attend/pallas_call | solution.py:370
  103.7 1.7 %collective-permute-start.40 = (bf16[1,32,2304]{2,1,0:T(8,128)(2,1)S(1)}, bf16[1,32,2304]{2,1,0:T(8,128)(2,1)S(1)}, u32[]{:S(2)}, u32[]{:S(2)}) collective-permute-start(bf16[1,32,2304]{2,1,0:T(8,128)(2,1)S(1)} %copy-done.15), channel_id=1, source_target_pairs={{0,4},{2,6},{4,0},{6,2},{8,12},{10,14},{12,8},{14,10},{16,20},{18,... | collective-permute-start | bytes 442376 | tf_op jit(solution)/shard_map/ppermute | solution.py:39
  105.4 4.5 %collective-permute-done.40.refs_6_ = bf16[1,32,2304]{2,1,0:T(8,128)(2,1)S(1)} collective-permute-done((bf16[1,32,2304]{2,1,0:T(8,128)(2,1)S(1)}, bf16[1,32,2304]{2,1,0:T(8,128)(2,1)S(1)}, u32[]{:S(2)}, u32[]{:S(2)}) %collective-permute-start.40) | collective-permute-done | bytes 147488 | tf_op jit(solution)/shard_map/ppermute | solution.py:39
  111.9 3.7 %early.1.early_ref = f32[256,2304]{1,0:T(8,128)S(1)} custom-call(s32[28]{0:T(128)S(1)} %stack.200.marks, bf16[2,256,256]{2,1,0:T(8,128)(2,1)S(1)} %get-tuple-element.20.own_hbm, bf16[2,256,256]{2,1,0:T(8,128)(2,1)S(1)} %collective-permute-done.21.other_hbm, bf16[2,32,2304]{2,1,0:T(8,128)(2,1)} %bitcast.42, bf16[2,32,2304]{2,1,0:T(8,128)(2,1)} %copy-done.7, ...), custom_call_target="tpu_custom_call" | custom-call | flops 905969664 | bytes 3538944 | tf_op jit(solution)/shard_map/early/pallas_call | solution.py:499
  117.1 3.7 %finish.1 = bf16[256,2304]{1,0:T(8,128)(2,1)} custom-call(s32[10]{0:T(128)S(1)} %stack.84.marks, bf16[2,256,256]{2,1,0:T(8,128)(2,1)S(1)} %get-tuple-element.20.own_hbm, bf16[2,256,256]{2,1,0:T(8,128)(2,1)S(1)} %collective-permute-done.21.other_hbm, f32[256,2304]{1,0:T(8,128)S(1)} %early.1.early_ref, f32[1,2304]{1,0:T(1,128)S(1)} %broadcast_in_dim.28.gain_ref, ...), custom_call_target="tpu_custom_call" | custom-call | flops 301989888 | bytes 1179648 | tf_op jit(solution)/shard_map/finish/pallas_call | solution.py:499
  (125 shorter events, 18.5 us)
Async XLA Ops:
  7.8 53.3 %collective-permute-start.1 = (bf16[4,256,640]{2,1,0:T(8,128)(2,1)S(1)}, bf16[4,256,640]{2,1,0:T(8,128)(2,1)S(1)}, u32[]{:S(2)}, u32[]{:S(2)}) collective-permute-start(bf16[4,256,640]{2,1,0:T(8,128)(2,1)S(1)} %norm.1.x_ref), channel_id=1, source_target_pairs={{0,2},{2,0},{4,6},{6,4},{8,10},{10,8},{12,14},{14,12},{16,18},{18,... | collective-permute-start | bytes 3932168 | tf_op jit(solution)/shard_map/ppermute | solution.py:35
  8.2 11.2 %collective-permute-start.23 = (bf16[2,32,2304]{2,1,0:T(8,128)(2,1)S(1)}, bf16[2,32,2304]{2,1,0:T(8,128)(2,1)}, u32[]{:S(2)}, u32[]{:S(2)}) collective-permute-start(bf16[2,32,2304]{2,1,0:T(8,128)(2,1)S(1)} %bitcast.43), channel_id=1, source_target_pairs={{0,4},{2,6},{4,0},{6,2},{8,12},{10,14},{12,8},{14,10},{16,20},{18,... | collective-permute-start | bytes 884744 | tf_op jit(solution)/shard_map/ppermute | solution.py:39
  10.8 8.5 %collective-permute-start.9 = (bf16[144,512]{1,0:T(8,128)(2,1)S(1)}, bf16[144,512]{1,0:T(8,128)(2,1)S(1)}, u32[]{:S(2)}, u32[]{:S(2)}) collective-permute-start(bf16[144,512]{1,0:T(8,128)(2,1)S(1)} %get-tuple-element.19), channel_id=1, source_target_pairs={{0,8},{2,10},{4,12},{6,14},{8,16},{10,18},{12,20},{14,22},{16,24},... | collective-permute-start | bytes 442376 | tf_op jit(solution)/shard_map/ppermute | solution.py:48
  12.4 9.3 %collective-permute-start.25 = (bf16[32,2304]{1,0:T(8,128)(2,1)S(1)}, bf16[32,2304]{1,0:T(8,128)(2,1)S(1)}, u32[]{:S(2)}, u32[]{:S(2)}) collective-permute-start(bf16[32,2304]{1,0:T(8,128)(2,1)S(1)} %get-tuple-element.22), channel_id=1, source_target_pairs={{0,8},{2,10},{4,12},{6,14},{8,16},{10,18},{12,20},{14,22},{16,24},... | collective-permute-start | bytes 442376 | tf_op jit(solution)/shard_map/ppermute | solution.py:48
  15.2 11.1 %collective-permute-start.2 = (bf16[2,144,512]{2,1,0:T(8,128)(2,1)S(1)}, bf16[2,144,512]{2,1,0:T(8,128)(2,1)S(1)}, u32[]{:S(2)}, u32[]{:S(2)}) collective-permute-start(bf16[2,144,512]{2,1,0:T(8,128)(2,1)S(1)} %get-tuple-element.16.refs_0_), channel_id=1, source_target_pairs={{0,4},{2,6},{4,0},{6,2},{8,12},{10,14},{12,8},{14,10},{16,20},{18,... | collective-permute-start | bytes 884744 | tf_op jit(solution)/shard_map/ppermute | solution.py:39
  19.4 6.9 %collective-permute-start.10 = (bf16[144,512]{1,0:T(8,128)(2,1)S(1)}, bf16[144,512]{1,0:T(8,128)(2,1)S(1)}, u32[]{:S(2)}, u32[]{:S(2)}) collective-permute-start(bf16[144,512]{1,0:T(8,128)(2,1)S(1)} %collective-permute-done.9.first_ref), channel_id=1, source_target_pairs={{0,8},{2,10},{4,12},{6,14},{8,16},{10,18},{12,20},{14,22},{16,24},... | collective-permute-start | bytes 442376 | tf_op jit(solution)/shard_map/ppermute | solution.py:48
  19.4 13.9 %collective-permute-start.22 = (bf16[2,32,2304]{2,1,0:T(8,128)(2,1)S(1)}, bf16[2,32,2304]{2,1,0:T(8,128)(2,1)S(1)}, u32[]{:S(2)}, u32[]{:S(2)}) collective-permute-start(bf16[2,32,2304]{2,1,0:T(8,128)(2,1)S(1)} %bitcast.44), channel_id=1, source_target_pairs={{0,2},{2,0},{4,6},{6,4},{8,10},{10,8},{12,14},{14,12},{16,18},{18,... | collective-permute-start | bytes 884744 | tf_op jit(solution)/shard_map/ppermute | solution.py:35
  21.7 13.2 %collective-permute-start.8 = (bf16[2,144,512]{2,1,0:T(8,128)(2,1)S(1)}, bf16[2,144,512]{2,1,0:T(8,128)(2,1)S(1)}, u32[]{:S(2)}, u32[]{:S(2)}) collective-permute-start(bf16[2,144,512]{2,1,0:T(8,128)(2,1)S(1)} %get-tuple-element.18.refs_4_), channel_id=1, source_target_pairs={{0,4},{2,6},{4,0},{6,2},{8,12},{10,14},{12,8},{14,10},{16,20},{18,... | collective-permute-start | bytes 884744 | tf_op jit(solution)/shard_map/ppermute | solution.py:39
  26.3 9.5 %collective-permute-start.14 = (bf16[144,512]{1,0:T(8,128)(2,1)S(1)}, bf16[144,512]{1,0:T(8,128)(2,1)S(1)}, u32[]{:S(2)}, u32[]{:S(2)}) collective-permute-start(bf16[144,512]{1,0:T(8,128)(2,1)S(1)} %collective-permute-done.10), channel_id=1, source_target_pairs={{0,8},{2,10},{4,12},{6,14},{8,16},{10,18},{12,20},{14,22},{16,24},... | collective-permute-start | bytes 442376 | tf_op jit(solution)/shard_map/ppermute | solution.py:48
  33.2 8.0 %collective-permute-start.34 = (bf16[32,2304]{1,0:T(8,128)(2,1)S(1)}, bf16[32,2304]{1,0:T(8,128)(2,1)}, u32[]{:S(2)}, u32[]{:S(2)}) collective-permute-start(bf16[32,2304]{1,0:T(8,128)(2,1)S(1)} %collective-permute-done.26), channel_id=1, source_target_pairs={{0,8},{2,10},{4,12},{6,14},{8,16},{10,18},{12,20},{14,22},{16,24},... | collective-permute-start | bytes 442376 | tf_op jit(solution)/shard_map/ppermute | solution.py:48
  33.3 10.0 %collective-permute-start.11 = (bf16[2,144,512]{2,1,0:T(8,128)(2,1)S(1)}, bf16[2,144,512]{2,1,0:T(8,128)(2,1)}, u32[]{:S(2)}, u32[]{:S(2)}) collective-permute-start(bf16[2,144,512]{2,1,0:T(8,128)(2,1)S(1)} %pack.4.refs_6_), channel_id=1, source_target_pairs={{0,1},{1,0},{2,3},{3,2},{4,5},{5,4},{6,7},{7,6},{8,9},{9,8},{10,11... | collective-permute-start | bytes 884744 | tf_op jit(solution)/shard_map/ppermute | solution.py:43
  34.9 9.5 %collective-permute-start.3 = (bf16[2,144,512]{2,1,0:T(8,128)(2,1)S(1)}, bf16[2,144,512]{2,1,0:T(8,128)(2,1)}, u32[]{:S(2)}, u32[]{:S(2)}) collective-permute-start(bf16[2,144,512]{2,1,0:T(8,128)(2,1)S(1)} %pack.3), channel_id=1, source_target_pairs={{0,8},{2,10},{4,12},{6,14},{8,16},{10,18},{12,20},{14,22},{16,24},... | collective-permute-start | bytes 884744 | tf_op jit(solution)/shard_map/ppermute | solution.py:48
  41.2 10.3 %collective-permute-start.12 = (bf16[2,144,512]{2,1,0:T(8,128)(2,1)S(1)}, bf16[2,144,512]{2,1,0:T(8,128)(2,1)S(1)}, u32[]{:S(2)}, u32[]{:S(2)}) collective-permute-start(bf16[2,144,512]{2,1,0:T(8,128)(2,1)S(1)} %pack.4.refs_6_), channel_id=1, source_target_pairs={{0,4},{2,6},{4,0},{6,2},{8,12},{10,14},{12,8},{14,10},{16,20},{18,... | collective-permute-start | bytes 884744 | tf_op jit(solution)/shard_map/ppermute | solution.py:39
  41.7 9.9 %collective-permute-start.16 = (bf16[1,144,512]{2,1,0:T(8,128)(2,1)S(1)}, bf16[1,144,512]{2,1,0:T(8,128)(2,1)S(1)}, u32[]{:S(2)}, u32[]{:S(2)}) collective-permute-start(bf16[1,144,512]{2,1,0:T(8,128)(2,1)S(1)} %bitcast.46), channel_id=1, source_target_pairs={{0,4},{2,6},{4,0},{6,2},{8,12},{10,14},{12,8},{14,10},{16,20},{18,... | collective-permute-start | bytes 442376 | tf_op jit(solution)/shard_map/ppermute | solution.py:39
  43.3 15.7 %collective-permute-start.13 = (bf16[2,144,512]{2,1,0:T(8,128)(2,1)}, bf16[2,144,512]{2,1,0:T(8,128)(2,1)}, u32[]{:S(2)}, u32[]{:S(2)}) collective-permute-start(bf16[2,144,512]{2,1,0:T(8,128)(2,1)} %collective-permute-done.11.refs_7_), channel_id=1, source_target_pairs={{0,4},{2,6},{4,0},{6,2},{8,12},{10,14},{12,8},{14,10},{16,20},{18,... | collective-permute-start | bytes 884744 | tf_op jit(solution)/shard_map/ppermute | solution.py:39
  44.4 16.3 %collective-permute-start.5 = (bf16[2,144,512]{2,1,0:T(8,128)(2,1)}, bf16[2,144,512]{2,1,0:T(8,128)(2,1)}, u32[]{:S(2)}, u32[]{:S(2)}) collective-permute-start(bf16[2,144,512]{2,1,0:T(8,128)(2,1)} %collective-permute-done.3.refs_2_), channel_id=1, source_target_pairs={{0,8},{2,10},{4,12},{6,14},{8,16},{10,18},{12,20},{14,22},{16,24},... | collective-permute-start | bytes 884744 | tf_op jit(solution)/shard_map/ppermute | solution.py:48
  51.6 15.5 %collective-permute-start.24 = (bf16[2,32,2304]{2,1,0:T(8,128)(2,1)}, bf16[2,32,2304]{2,1,0:T(8,128)(2,1)}, u32[]{:S(2)}, u32[]{:S(2)}) collective-permute-start(bf16[2,32,2304]{2,1,0:T(8,128)(2,1)} %collective-permute-done.23.refs_2_), channel_id=1, source_target_pairs={{0,2},{2,0},{4,6},{6,4},{8,10},{10,8},{12,14},{14,12},{16,18},{18,... | collective-permute-start | bytes 884744 | tf_op jit(solution)/shard_map/ppermute | solution.py:35
  58.6 13.8 %collective-permute-start.30 = (bf16[2,32,2304]{2,1,0:T(8,128)(2,1)}, bf16[2,32,2304]{2,1,0:T(8,128)(2,1)}, u32[]{:S(2)}, u32[]{:S(2)}) collective-permute-start(bf16[2,32,2304]{2,1,0:T(8,128)(2,1)} %pack.5.refs_4_), channel_id=1, source_target_pairs={{0,4},{2,6},{4,0},{6,2},{8,12},{10,14},{12,8},{14,10},{16,20},{18,... | collective-permute-start | bytes 884744 | tf_op jit(solution)/shard_map/ppermute | solution.py:39
  59.0 13.7 %collective-permute-start.28 = (bf16[2,32,2304]{2,1,0:T(8,128)(2,1)}, bf16[2,32,2304]{2,1,0:T(8,128)(2,1)S(1)}, u32[]{:S(2)}, u32[]{:S(2)}) collective-permute-start(bf16[2,32,2304]{2,1,0:T(8,128)(2,1)} %pack.5.refs_4_), channel_id=1, source_target_pairs={{0,1},{1,0},{2,3},{3,2},{4,5},{5,4},{6,7},{7,6},{8,9},{9,8},{10,11... | collective-permute-start | bytes 884744 | tf_op jit(solution)/shard_map/ppermute | solution.py:43
  60.7 10.0 %collective-permute-start.36 = (bf16[1,32,2304]{2,1,0:T(8,128)(2,1)}, bf16[1,32,2304]{2,1,0:T(8,128)(2,1)S(1)}, u32[]{:S(2)}, u32[]{:S(2)}) collective-permute-start(bf16[1,32,2304]{2,1,0:T(8,128)(2,1)} %bitcast.36.refs_0_), channel_id=1, source_target_pairs={{0,1},{1,0},{2,3},{3,2},{4,5},{5,4},{6,7},{7,6},{8,9},{9,8},{10,11... | collective-permute-start | bytes 442376 | tf_op jit(solution)/shard_map/ppermute | solution.py:43
  61.1 13.3 %collective-permute-start.19 = (bf16[2,144,512]{2,1,0:T(8,128)(2,1)}, bf16[2,144,512]{2,1,0:T(8,128)(2,1)}, u32[]{:S(2)}, u32[]{:S(2)}) collective-permute-start(bf16[2,144,512]{2,1,0:T(8,128)(2,1)} %collective-permute-done.5.refs_4_), channel_id=1, source_target_pairs={{0,8},{2,10},{4,12},{6,14},{8,16},{10,18},{12,20},{14,22},{16,24},... | collective-permute-start | bytes 884744 | tf_op jit(solution)/shard_map/ppermute | solution.py:48
  67.1 30.4 %collective-permute-start.18 = (bf16[528,512]{1,0:T(8,128)(2,1)S(1)}, bf16[528,512]{1,0:T(8,128)(2,1)}, u32[]{:S(2)}, u32[]{:S(2)}) collective-permute-start(bf16[528,512]{1,0:T(8,128)(2,1)S(1)} %project.3.refs_1_), channel_id=1, source_target_pairs={{0,4},{2,6},{4,8},{6,10},{8,12},{10,14},{12,16},{14,18},{16,20},{1... | collective-permute-start | bytes 1622024 | tf_op jit(solution)/shard_map/ppermute | solution.py:53
  70.7 10.1 %collective-permute-start.4 = (bf16[2,144,512]{2,1,0:T(8,128)(2,1)}, bf16[2,144,512]{2,1,0:T(8,128)(2,1)S(1)}, u32[]{:S(2)}, u32[]{:S(2)}) collective-permute-start(bf16[2,144,512]{2,1,0:T(8,128)(2,1)} %collective-permute-done.3.refs_2_), channel_id=1, source_target_pairs={{0,1},{1,0},{2,3},{3,2},{4,5},{5,4},{6,7},{7,6},{8,9},{9,8},{10,11... | collective-permute-start | bytes 884744 | tf_op jit(solution)/shard_map/ppermute | solution.py:43
  72.4 14.9 %collective-permute-start.6 = (bf16[2,144,512]{2,1,0:T(8,128)(2,1)}, bf16[2,144,512]{2,1,0:T(8,128)(2,1)}, u32[]{:S(2)}, u32[]{:S(2)}) collective-permute-start(bf16[2,144,512]{2,1,0:T(8,128)(2,1)} %collective-permute-done.5.refs_4_), channel_id=1, source_target_pairs={{0,1},{1,0},{2,3},{3,2},{4,5},{5,4},{6,7},{7,6},{8,9},{9,8},{10,11... | collective-permute-start | bytes 884744 | tf_op jit(solution)/shard_map/ppermute | solution.py:43
  72.7 20.8 %collective-permute-start.32 = (bf16[2,32,2304]{2,1,0:T(8,128)(2,1)}, bf16[2,32,2304]{2,1,0:T(8,128)(2,1)}, u32[]{:S(2)}, u32[]{:S(2)}) collective-permute-start(bf16[2,32,2304]{2,1,0:T(8,128)(2,1)} %collective-permute-done.30.refs_8_), channel_id=1, source_target_pairs={{0,1},{1,0},{2,3},{3,2},{4,5},{5,4},{6,7},{7,6},{8,9},{9,8},{10,11... | collective-permute-start | bytes 884744 | tf_op jit(solution)/shard_map/ppermute | solution.py:43
  74.4 23.1 %collective-permute-start.20 = (bf16[2,144,512]{2,1,0:T(8,128)(2,1)}, bf16[2,144,512]{2,1,0:T(8,128)(2,1)}, u32[]{:S(2)}, u32[]{:S(2)}) collective-permute-start(bf16[2,144,512]{2,1,0:T(8,128)(2,1)} %collective-permute-done.19.refs_3_), channel_id=1, source_target_pairs={{0,1},{1,0},{2,3},{3,2},{4,5},{5,4},{6,7},{7,6},{8,9},{9,8},{10,11... | collective-permute-start | bytes 884744 | tf_op jit(solution)/shard_map/ppermute | solution.py:43
  81.5 22.2 %collective-permute-start.27 = (bf16[2,32,2304]{2,1,0:T(8,128)(2,1)}, bf16[2,32,2304]{2,1,0:T(8,128)(2,1)}, u32[]{:S(2)}, u32[]{:S(2)}) collective-permute-start(bf16[2,32,2304]{2,1,0:T(8,128)(2,1)} %pack.5.refs_4_), channel_id=1, source_target_pairs={{0,2},{2,0},{4,6},{6,4},{8,10},{10,8},{12,14},{14,12},{16,18},{18,... | collective-permute-start | bytes 884744 | tf_op jit(solution)/shard_map/ppermute | solution.py:35
  87.2 16.3 %collective-permute-start.38 = (bf16[1,32,2304]{2,1,0:T(8,128)(2,1)}, bf16[1,32,2304]{2,1,0:T(8,128)(2,1)}, u32[]{:S(2)}, u32[]{:S(2)}) collective-permute-start(bf16[1,32,2304]{2,1,0:T(8,128)(2,1)} %bitcast.36.refs_0_), channel_id=1, source_target_pairs={{0,4},{2,6},{4,0},{6,2},{8,12},{10,14},{12,8},{14,10},{16,20},{18,... | collective-permute-start | bytes 442376 | tf_op jit(solution)/shard_map/ppermute | solution.py:39
  93.5 17.6 %collective-permute-start.31 = (bf16[2,32,2304]{2,1,0:T(8,128)(2,1)}, bf16[2,32,2304]{2,1,0:T(8,128)(2,1)}, u32[]{:S(2)}, u32[]{:S(2)}) collective-permute-start(bf16[2,32,2304]{2,1,0:T(8,128)(2,1)} %collective-permute-done.30.refs_8_), channel_id=1, source_target_pairs={{0,2},{2,0},{4,6},{6,4},{8,10},{10,8},{12,14},{14,12},{16,18},{18,... | collective-permute-start | bytes 884744 | tf_op jit(solution)/shard_map/ppermute | solution.py:35
  97.5 12.4 %collective-permute-start.29 = (bf16[2,32,2304]{2,1,0:T(8,128)(2,1)S(1)}, bf16[2,32,2304]{2,1,0:T(8,128)(2,1)S(1)}, u32[]{:S(2)}, u32[]{:S(2)}) collective-permute-start(bf16[2,32,2304]{2,1,0:T(8,128)(2,1)S(1)} %copy-done.10), channel_id=1, source_target_pairs={{0,2},{2,0},{4,6},{6,4},{8,10},{10,8},{12,14},{14,12},{16,18},{18,... | collective-permute-start | bytes 884744 | tf_op jit(solution)/shard_map/ppermute | solution.py:35
  97.5 13.7 %collective-permute-start.33 = (bf16[2,32,2304]{2,1,0:T(8,128)(2,1)}, bf16[2,32,2304]{2,1,0:T(8,128)(2,1)}, u32[]{:S(2)}, u32[]{:S(2)}) collective-permute-start(bf16[2,32,2304]{2,1,0:T(8,128)(2,1)} %collective-permute-done.32.refs_10_), channel_id=1, source_target_pairs={{0,2},{2,0},{4,6},{6,4},{8,10},{10,8},{12,14},{14,12},{16,18},{18,... | collective-permute-start | bytes 884744 | tf_op jit(solution)/shard_map/ppermute | solution.py:35
  103.5 8.3 %collective-permute-start.21 = (bf16[2,256,256]{2,1,0:T(8,128)(2,1)S(1)}, bf16[2,256,256]{2,1,0:T(8,128)(2,1)S(1)}, u32[]{:S(2)}, u32[]{:S(2)}) collective-permute-start(bf16[2,256,256]{2,1,0:T(8,128)(2,1)S(1)} %get-tuple-element.21), channel_id=1, source_target_pairs={{0,2},{2,0},{4,6},{6,4},{8,10},{10,8},{12,14},{14,12},{16,18},{18,... | collective-permute-start | bytes 786440 | tf_op jit(solution)/shard_map/ppermute | solution.py:35
  (36 other events, 340.2 us)

commit v4 on v3

--- a/solution.py
+++ b/solution.py
@@ -187,84 +187,88 @@
     )(*in_hbm([rows]), gain[None, :], *in_hbm(tables))
 
 
-def project_kernel(slots, turned, joined, early, spots, x_ref, other_ref, *refs):
-    refs = list(refs)
-    if joined:
-        sum_ref = refs.pop(0)
-    if not early:
-        cos_ref, sin_ref = refs.pop(0), refs.pop(0)
-    tailed = turned is not None and not all(turned)
-    if tailed:
-        ids_ref, other_ids_ref = refs.pop(0), refs.pop(0)
-    pieces = refs[: len(slots)]
-    out_ref, held, total, sems = refs[len(slots) :]
-    layers = held.shape[0]
+def fetch_layers(slots, first, marks, pieces, held, sems):
     rows = pieces[0].shape[1]
     copies = []
     for piece, blocks in zip(pieces, slots):
         for i, slot in enumerate(blocks):
-            at = pl.multiple_of(spots[layers + len(copies)] * rows, rows)
+            at = pl.multiple_of(marks[first + len(copies)], rows)
             copy = pltpu.make_async_copy(
                 piece.at[i], held.at[slot, pl.ds(at, rows), :], sems.at[len(copies)]
             )
             copy.start()
             copies.append((slot, copy))
+    return copies
+
+
+def fetch_pair(first_hbm, second_hbm, first_ref, second_ref, sems):
+    copies = (
+        pltpu.make_async_copy(first_hbm, first_ref, sems.at[0]),
+        pltpu.make_async_copy(second_hbm, second_ref, sems.at[1]),
+    )
+    for copy in copies:
+        copy.start()
+    return copies
+
+
+def project_kernel(slots, turned, spots, x_ref, other_ref, cos_hbm, sin_hbm, ids_ref, other_ids_ref, *refs):
+    pieces = refs[: len(slots)]
+    out_ref, held, total, cos_ref, sin_ref, sems, ends = refs[len(slots) :]
+    layers = held.shape[0]
+    copies = fetch_layers(slots, layers, spots, pieces, held, sems)
+    tables = fetch_pair(cos_hbm, sin_hbm, cos_ref, sin_ref, ends)
     core = spots[layers + len(copies)]
     tokens = x_ref.shape[1]
     mine = pl.ds(pl.multiple_of(core * tokens, tokens), tokens)
     theirs = pl.ds(pl.multiple_of((1 - core) * tokens, tokens), tokens)
-    if tailed:
-        for ref, at in ((ids_ref, mine), (other_ids_ref, theirs)):
-            row = jnp.broadcast_to(ref[...].astype(jnp.float32), (TAIL, tokens))
-            out_ref[2 * tokens :, at] = row.astype(jnp.bfloat16)
+    for ref, at in ((ids_ref, mine), (other_ids_ref, theirs)):
+        row = jnp.broadcast_to(ref[...].astype(jnp.float32), (TAIL, tokens))
+        out_ref[2 * tokens :, at] = row.astype(jnp.bfloat16)
     half = HEAD // 2
     for layer in range(layers):
         for slot, copy in copies:
             if slot == layer:
                 copy.wait()
         last = layer == layers - 1
+        if last:
+            for copy in tables:
+                copy.wait()
         for ref, at in ((x_ref, mine), (other_ref, theirs)):
             part = jnp.dot(
                 ref[spots[layer], :, : held.shape[1]], held[layer], preferred_element_type=jnp.float32
             )
             if layer > 0:
                 part = part + total[at, :]
-            elif joined:
-                part = part + sum_ref[at, :]
             if not last:
                 total[at, :] = part
-            elif early:
-                out_ref[at, :] = part
-            else:
-                cosine, sine = cos_ref[at, :], sin_ref[at, :]
-                for h, turn in enumerate(turned):
-                    a = part[:, h * HEAD : h * HEAD + half]
-                    b = part[:, h * HEAD + half : (h + 1) * HEAD]
-                    if turn:
-                        a, b = a * cosine - b * sine, b * cosine + a * sine
-                    out_ref[at, h * HEAD : h * HEAD + half] = a.astype(jnp.bfloat16)
-                    out_ref[at, h * HEAD + half : (h + 1) * HEAD] = b.astype(jnp.bfloat16)
-
-
-def project(x, other, arrays, slots, layers, spots, turned=None, tables=(), before=None, ids=()):
-    tokens, depth = 2 * x.shape[1], 4 * arrays[0].shape[1]
-    width = arrays[0].shape[2]
-    early = turned is None
-    extra = ([] if before is None else [before]) + in_hbm(tables) + list(ids)
-    vmem = pl.BlockSpec(memory_space=pltpu.VMEM)
+                continue
+            cosine, sine = cos_ref[at, :], sin_ref[at, :]
+            for h, turn in enumerate(turned):
+                a = part[:, h * HEAD : h * HEAD + half]
+                b = part[:, h * HEAD + half : (h + 1) * HEAD]
+                if turn:
+                    a, b = a * cosine - b * sine, b * cosine + a * sine
+                out_ref[at, h * HEAD : h * HEAD + half] = a.astype(jnp.bfloat16)
+                out_ref[at, h * HEAD + half : (h + 1) * HEAD] = b.astype(jnp.bfloat16)
+
+
+def project(x, other, arrays, slots, layers, spots, turned, tables, ids):
+    tokens, depth, width = 2 * x.shape[1], 4 * arrays[0].shape[1], arrays[0].shape[2]
+    vmem, left = pl.BlockSpec(memory_space=pltpu.VMEM), pl.BlockSpec(memory_space=pl.ANY)
     return pl.pallas_call(
-        functools.partial(project_kernel, slots, turned, before is not None, early),
-        out_shape=jax.ShapeDtypeStruct(
-            (tokens + (TAIL if ids else 0), width), jnp.float32 if early else jnp.bfloat16
-        ),
+        functools.partial(project_kernel, slots, turned),
+        out_shape=jax.ShapeDtypeStruct((tokens + TAIL, width), jnp.bfloat16),
         in_specs=[pl.BlockSpec(memory_space=pltpu.SMEM)]
-        + [vmem] * (2 + len(extra))
-        + [pl.BlockSpec(memory_space=pl.ANY)] * len(arrays),
+        + [vmem, vmem, left, left, vmem, vmem]
+        + [left] * len(arrays),
         out_specs=vmem,
         scratch_shapes=[
             pltpu.VMEM((layers, depth, width), jnp.bfloat16),
             pltpu.VMEM((tokens, width), jnp.float32),
+            pltpu.VMEM((tokens, HEAD // 2), jnp.float32),
+            pltpu.VMEM((tokens, HEAD // 2), jnp.float32),
             pltpu.SemaphoreType.DMA((sum(len(blocks) for blocks in slots),)),
+            pltpu.SemaphoreType.DMA((2,)),
         ],
         compiler_params=pltpu.CompilerParams(vmem_limit_bytes=12 * 1024 * 1024),
         cost_estimate=pl.CostEstimate(
@@ -273,29 +277,17 @@
             transcendentals=0,
         ),
         name="project",
-    )(spots, x, other, *extra, *in_hbm(arrays))
-
-
-def attend_kernel(slots, place, x_ref, other_ref, sum_ref, cos_ref, sin_ref, ids_ref, *refs):
-    other_ids_ref, kv_hbm, old_hbm = refs[:3]
-    pieces = refs[3 : 3 + len(slots)]
-    own_ref, send_ref, held, q_ref, kv_ref, old_ref, sems, ends = refs[3 + len(slots) :]
-    rows = pieces[0].shape[1]
-    copies = []
-    for piece, blocks in zip(pieces, slots):
-        for i in range(blocks):
-            at = pl.multiple_of(place[3 + len(copies)] * rows, rows)
-            copies.append(
-                pltpu.make_async_copy(piece.at[i], held.at[pl.ds(at, rows), :], sems.at[len(copies)])
-            )
-            copies[-1].start()
-    fetch = (
-        pltpu.make_async_copy(kv_hbm, kv_ref, ends.at[0]),
-        pltpu.make_async_copy(old_hbm, old_ref, ends.at[1]),
-    )
-    for copy in fetch:
-        copy.start()
-    core, chip, layer = place[0], place[1], place[2]
+    )(spots, x, other, *in_hbm(tables), *ids, *in_hbm(arrays))
+
+
+def attend_kernel(slots, layers, place, x_ref, other_ref, ids_ref, *refs):
+    other_ids_ref, cos_hbm, sin_hbm, kv_hbm, old_hbm = refs[:5]
+    pieces, refs = refs[5 : 5 + len(slots)], refs[5 + len(slots) :]
+    own_ref, send_ref, held, total, q_ref, cos_ref, sin_ref, kv_ref, old_ref, sems, turns, ends = refs
+    copies = fetch_layers(slots, 2 + layers, place, pieces, held, sems)
+    tables = fetch_pair(cos_hbm, sin_hbm, cos_ref, sin_ref, turns)
+    fetch = fetch_pair(kv_hbm, old_hbm, kv_ref, old_ref, ends)
+    core, chip = place[0], place[1]
     step = own_ref.shape[1]
     tokens = q_ref.shape[0]
     behind = tokens
@@ -309,13 +301,22 @@
     ).astype(jnp.float32)
     query_ids = jnp.broadcast_to(ids, (128, tokens)).T[:, :1]
     half = HEAD // 2
-    for copy in copies:
+    for layer in range(layers):
+        for slot, copy in copies:
+            if slot == layer:
+                copy.wait()
+        for ref, block in ((x_ref, 0), (other_ref, 1)):
+            part = jnp.dot(
+                ref[place[2 + layer], :, : held.shape[1]],
+                held[layer],
+                preferred_element_type=jnp.float32,
+            )
+            total[block] = part if layer == 0 else total[block] + part
+    for copy in tables:
         copy.wait()
-    for ref, block in ((x_ref, core), (other_ref, 1 - core)):
-        at = pl.ds(pl.multiple_of(block * step, step), step)
-        part = sum_ref[at, :] + jnp.dot(
-            ref[layer, :, : held.shape[0]], held[...], preferred_element_type=jnp.float32
-        )
+    for block, at in ((0, core), (1, 1 - core)):
+        part = total[block]
+        at = pl.ds(pl.multiple_of(at * step, step), step)
         cosine, sine = cos_ref[at, :], sin_ref[at, :]
         for h in range(GROUPS):
             a = part[:, h * HEAD : h * HEAD + half]
@@ -362,54 +363,33 @@
                 send_ref[h] = result
 
 
-def attend(x, other, arrays, slots, place, before, tables, kv, old, ids):
-    tokens, width = before.shape
-    depth = 4 * arrays[0].shape[1]
+def attend(x, other, arrays, slots, layers, place, tables, kv, old, ids):
+    tokens, depth, width = 2 * x.shape[1], 4 * arrays[0].shape[1], arrays[0].shape[2]
     work = GROUPS * tokens * 2 * tokens * HEAD
     vmem, left = pl.BlockSpec(memory_space=pltpu.VMEM), pl.BlockSpec(memory_space=pl.ANY)
     return pl.pallas_call(
-        functools.partial(attend_kernel, slots),
+        functools.partial(attend_kernel, slots, layers),
         out_shape=[jax.ShapeDtypeStruct((GROUPS, tokens // 2, HEAD), jnp.bfloat16)] * 2,
-        in_specs=[pl.BlockSpec(memory_space=pltpu.SMEM)] + [vmem] * 7 + [left] * (2 + len(arrays)),
+        in_specs=[pl.BlockSpec(memory_space=pltpu.SMEM)] + [vmem] * 4 + [left] * (4 + len(arrays)),
         out_specs=[vmem] * 2,
         scratch_shapes=[
-            pltpu.VMEM((depth, width), jnp.bfloat16),
+            pltpu.VMEM((layers, depth, width), jnp.bfloat16),
+            pltpu.VMEM((2, tokens // 2, width), jnp.float32),
             pltpu.VMEM((tokens, width), jnp.bfloat16),
+            pltpu.VMEM((tokens, HEAD // 2), jnp.float32),
+            pltpu.VMEM((tokens, HEAD // 2), jnp.float32),
             pltpu.VMEM(kv.shape, jnp.bfloat16),
             pltpu.VMEM(old.shape, jnp.bfloat16),
-            pltpu.SemaphoreType.DMA((sum(slots),)),
+            pltpu.SemaphoreType.DMA((sum(len(blocks) for blocks in slots),)),
+            pltpu.SemaphoreType.DMA((2,)),
             pltpu.SemaphoreType.DMA((2,)),
         ],
-        compiler_params=pltpu.CompilerParams(vmem_limit_bytes=16 * 1024 * 1024),
+        compiler_params=pltpu.CompilerParams(vmem_limit_bytes=20 * 1024 * 1024),
         cost_estimate=pl.CostEstimate(
             flops=4 * work, bytes_accessed=work // 256, transcendentals=0
         ),
         name="attend",
-    )(place, x, other, before, *in_hbm(tables), *ids, *in_hbm([kv, old]), *in_hbm(arrays))
-
-
-def fetch_layers(slots, first, marks, pieces, held, sems):
-    rows = pieces[0].shape[1]
-    copies = []
-    for piece, blocks in zip(pieces, slots):
-        for i, slot in enumerate(blocks):
-            at = pl.multiple_of(marks[first + len(copies)], rows)
-            copy = pltpu.make_async_copy(
-                piece.at[i], held.at[slot, pl.ds(at, rows), :], sems.at[len(copies)]
-            )
-            copy.start()
-            copies.append((slot, copy))
-    return copies
-
-
-def fetch_heads(own_hbm, other_hbm, own_ref, other_ref, ends):
-    copies = (
-        pltpu.make_async_copy(own_hbm, own_ref, ends.at[0]),
-        pltpu.make_async_copy(other_hbm, other_ref, ends.at[1]),
-    )
-    for copy in copies:
-        copy.start()
-    return copies
+    )(place, x, other, *ids, *in_hbm(tables), *in_hbm([kv, old]), *in_hbm(arrays))
 
 
 def head_of(own_ref, other_ref, core, head):
@@ -419,7 +399,7 @@
 def early_kernel(slots, heads, marks, own_hbm, other_hbm, *refs):
     pieces = refs[: len(slots)]
     out_ref, held, own_ref, other_ref, sems, ends = refs[len(slots) :]
-    fetch = fetch_heads(own_hbm, other_hbm, own_ref, other_ref, ends)
+    fetch = fetch_pair(own_hbm, other_hbm, own_ref, other_ref, ends)
     copies = fetch_layers(slots, heads + 1, marks, pieces, held, sems)
     for copy in fetch:
         copy.wait()
@@ -439,7 +419,7 @@
 def finish_kernel(slots, marks, own_hbm, other_hbm, early_ref, gain_ref, hid_hbm, *refs):
     pieces = refs[: len(slots)]
     out_hbm, held, own_ref, other_ref, hid_ref, sum_ref, out_ref, sems, ends = refs[len(slots) :]
-    heads = fetch_heads(own_hbm, other_hbm, own_ref, other_ref, ends)
+    heads = fetch_pair(own_hbm, other_hbm, own_ref, other_ref, ends)
     fetch = pltpu.make_async_copy(hid_hbm, hid_ref, ends.at[2])
     copies = fetch_layers(slots, 2, marks, pieces, held, sems)
     fetch.start()
@@ -512,7 +492,7 @@
             transcendentals=0,
         ),
         name="finish" if finish else "early",
-    )(marks, own, other, *extra, *in_hbm(arrays))
+    )(marks, own, other, *extra, *arrays)
 
 
 def per_device(hidden_in, segment_ids, pre_gain, w_qkv, w_out, post_gain):
@@ -543,32 +523,39 @@
     normed_other = swap_core(normed)
     ids = (segment_ids, swap_core(segment_ids))
 
-    def projected(pieces, backs, **more):
-        layers = [(line - back + line_count) % line_count for back in backs]
-        spots, arrays, slots = [], [], []
-        for block, blocks in pieces:
-            if not any(back in backs for back, _, _ in blocks):
-                continue
-            arrays.append(block)
-            slots.append(tuple(backs.index(back) for back, _, _ in blocks))
-            spots += [y * 2 + h for _, y, h in blocks]
-        spots = jnp.stack([jnp.asarray(spot, jnp.int32) for spot in layers + spots + [core]])
-        return project(normed, normed_other, arrays, tuple(slots), len(backs), spots, **more)
-
-    kv = projected(kv_pieces, [0, 1, 2, 3], turned=(True, False), tables=(cosine, sine), ids=ids)
+    backs = list(range(line_count))
+    layers = [(line - back + line_count) % line_count for back in backs]
+
+    def laid(pieces):
+        arrays = [block for block, _ in pieces]
+        slots = tuple(tuple(back for back, _, _ in blocks) for _, blocks in pieces)
+        rows = arrays[0].shape[1]
+        return arrays, slots, [(y * 2 + h) * rows for _, blocks in pieces for _, y, h in blocks]
+
+    def scalars(entries):
+        return jnp.stack([jnp.asarray(entry, jnp.int32) for entry in entries])
+
+    arrays, slots, spots = laid(kv_pieces)
+    kv = project(
+        normed,
+        normed_other,
+        arrays,
+        slots,
+        line_count,
+        scalars(layers + spots + [core]),
+        turned=(True, False),
+        tables=(cosine, sine),
+        ids=ids,
+    )
     old = from_chip_behind(kv, 1)
-    q = projected(q_pieces, [0, 1, 2])
-    last = line_count - 1
-    final = [(block, blocks) for block, blocks in q_pieces if blocks[0][0] == last]
-    place = [core, chip, (line - last + line_count) % line_count]
-    place += [y * 2 + h for _, blocks in final for _, y, h in blocks]
+    arrays, slots, spots = laid(q_pieces)
     att_own, att_send = attend(
         normed,
         normed_other,
-        [block for block, _ in final],
-        tuple(len(blocks) for _, blocks in final),
-        jnp.stack([jnp.asarray(entry, jnp.int32) for entry in place]),
-        q,
+        arrays,
+        slots,
+        line_count,
+        scalars([core, chip] + layers + spots),
         (cosine, sine),
         kv,
         old,
@@ -584,7 +571,7 @@
         for (block, blocks), other in zip(out_pieces, swapped):
             if blocks[0][0] not in backs:
                 continue
-            for array, c in ((block, core), (other, 1 - core)):
+            for array, c in ((in_hbm([block])[0], core), (other, 1 - core)):
                 arrays.append(array)
                 where.append(tuple(backs.index(back) for back, _, _ in blocks))
                 offsets += [((y * 2 + c) * 2 + h) * half_rows for _, y, h in blocks]
@@ -596,7 +583,7 @@
     return done[None]
 
 
-BY_BATCH = ("3n",)
+BY_BATCH = ()
 
 
 def from_behind(block, axis, distance):

time: 121 us -> 121 us (level)
  local copies, waits for them, and re-layouts: 4.97 us -> 10.8 us
  waiting for transfers between devices: 60.3 us -> 57.5 us
  starting transfers between devices: 27.8 us -> 25.7 us
  Pallas kernels: 25.4 us -> 23.8 us
    ppermute x8 -> x7, waiting for transfers between devices: 19.8 us -> 10.4 us  [swap_batch(): return lax.ppermute(block, 'batch', [(0, 1), (1, 0)])]
    ppermute x10 -> x11, waiting for transfers between devices: 16.5 us -> 24.4 us  [swap_pair(): lax.ppermute(block, 'seq', [(i, i ^ 2) for i in range(lax.axis_size('seq'...]
    unnamed x52 -> x54, local copies, waits for them, and re-layouts: 3.78 us -> 9.73 us
    pallas_call x3 -> x2, Pallas kernels: 13.6 us -> 11.4 us  [the longest x1 7.25 us: attend(): pl.pallas_call(functools.partial(attend_kernel, slots, layers), out_shape...]
    ppermute x10 -> x11, starting transfers between devices: 10.1 us -> 8.72 us  [swap_pair(): lax.ppermute(block, 'seq', [(i, i ^ 2) for i in range(lax.axis_size('seq'...]
    ppermute x9, waiting for transfers between devices: 21.8 us -> 20.5 us  [along_line(): lax.ppermute(block, 'seq', [(i, (i + 4 * steps) % count) for i in range(c...]
    ppermute x8 -> x7, starting transfers between devices: 9.19 us -> 8.36 us  [swap_batch(): return lax.ppermute(block, 'batch', [(0, 1), (1, 0)])]
  transfers between devices with their start and end apart: 42 -> 42, of which waited for: 18 -> 16; matrix products, arithmetic and copies ran while one was open for 1% -> 1% of each run, Pallas kernels for 15% -> 14%
where the time goes in v4:
time: 121 us; the launch traced here: 120 us
  waiting for transfers between devices  57.5 us (48%)
  starting transfers between devices  25.7 us (21%)
  Pallas kernels  23.8 us (20%)
  local copies, waits for them, and re-layouts  10.8 us (9%)
  other arithmetic  1.91 us (2%)
    ppermute x11, waiting for transfers between devices, swap_pair(): lax.ppermute(block, 'seq', [(i, i ^ 2) for i in range(lax.axis_size('seq'...  24.4 us
    ppermute x9, waiting for transfers between devices, along_line(): lax.ppermute(block, 'seq', [(i, (i + 4 * steps) % count) for i in range(c...  20.5 us
    ppermute x7, waiting for transfers between devices, swap_batch(): return lax.ppermute(block, 'batch', [(0, 1), (1, 0)])  10.4 us
    unnamed x54, local copies, waits for them, and re-layouts  9.73 us
    ppermute x11, starting transfers between devices, swap_pair(): lax.ppermute(block, 'seq', [(i, i ^ 2) for i in range(lax.axis_size('seq'...  8.72 us
    ppermute x7, starting transfers between devices, swap_batch(): return lax.ppermute(block, 'batch', [(0, 1), (1, 0)])  8.36 us
    pallas_call x2, Pallas kernels, out_project(): pl.pallas_call(body, out_shape=jax.ShapeDtypeStruct((tokens, width), jnp....  8.03 us
    pallas_call x1, Pallas kernels, attend(): pl.pallas_call(functools.partial(attend_kernel, slots, layers), out_shape...  7.25 us
  transfers between devices with their start and end apart: 42, of which 16 were waited for; matrix products, arithmetic and copies ran while one was open for 1% of the time, Pallas kernels for 14%

profile of v4, /device:TPU:0, one launch (start us, length us, event | category | flops | bytes accessed | tf_op | source)
XLA Modules:
  0.0 120.2 jit_solution(4886166562690482473)
XLA Ops:
  1.3 1.0 collective-permute-done.came_ref
  2.3 1.2 %prepare.1 = (bf16[2,144,512]{2,1,0:T(8,128)(2,1)S(1)}, bf16[2,144,512]{2,1,0:T(8,128)(2,1)S(1)}, bf16[144,512]{1,0:T(8,128)(2,1)S(1)}, bf16[144,512]{1,0:T(8,128)(2,1)S(1)}, bf16[32,2304]{1,0:T(8,128)(2,1)S(1)}) custom-call(s32[2]{0:T(128)S(1)} %pad_add_fusion.place, bf16[144,2048]{1,0:T(8,128)(2,1)} %w_ref.1, ...), custom_call_target="tpu_custom_call" | custom-call | flops 1000000 | bytes 589824 | tf_op jit(solution)/shard_map/prepare/pallas_call | solution.py:142
  3.6 1.8 %multiply_sine_fusion = (f32[512,128]{1,0:T(8,128)}, f32[512,128]{1,0:T(8,128)}) fusion(f32[128]{0:T(128)S(1)} %negate_power_fusion, f32[512]{0:T(512)S(1)} %add_convert_fusion), kind=kLoop, calls=%fused_computation | loop fusion | flops 65536 | bytes 526848 | tf_op jit(solution)/shard_map/sin | solution.py:31
  5.4 2.3 %norm.1.x_ref = bf16[4,256,640]{2,1,0:T(8,128)(2,1)S(1)} custom-call(bf16[256,2304]{1,0:T(8,128)(2,1)} %bitcast.40, f32[1,2304]{1,0:T(1,128)S(1)} %broadcast_in_dim.24.gain_ref, f32[512,128]{1,0:T(8,128)} %get-tuple-element.24.cos_ref.cos_hbm.refs_1_, f32[512,128]{1,0:T(8,128)} %get-tuple-element.23.sin_ref.sin_hbm.refs_2_), custom_call_target="tpu_custom_call" | custom-call | flops 1000000 | bytes 2359296 | tf_op jit(solution)/shard_map/norm/pallas_call | solution.py:179
  8.2 2.6 %collective-permute-start.23 = (bf16[2,32,2304]{2,1,0:T(8,128)(2,1)S(1)}, bf16[2,32,2304]{2,1,0:T(8,128)(2,1)}, u32[]{:S(2)}, u32[]{:S(2)}) collective-permute-start(bf16[2,32,2304]{2,1,0:T(8,128)(2,1)S(1)} %bitcast.43), channel_id=1, source_target_pairs={{0,4},{2,6},{4,0},{6,2},{8,12},{10,14},{12,8},{14,10},{16,20},{18,... | collective-permute-start | bytes 884744 | tf_op jit(solution)/shard_map/ppermute | solution.py:39
  10.9 1.6 %collective-permute-start.4 = (bf16[144,512]{1,0:T(8,128)(2,1)S(1)}, bf16[144,512]{1,0:T(8,128)(2,1)S(1)}, u32[]{:S(2)}, u32[]{:S(2)}) collective-permute-start(bf16[144,512]{1,0:T(8,128)(2,1)S(1)} %get-tuple-element.17), channel_id=1, source_target_pairs={{0,8},{2,10},{4,12},{6,14},{8,16},{10,18},{12,20},{14,22},{16,24},... | collective-permute-start | bytes 442376 | tf_op jit(solution)/shard_map/ppermute | solution.py:48
  12.4 1.6 %collective-permute-start.25 = (bf16[32,2304]{1,0:T(8,128)(2,1)S(1)}, bf16[32,2304]{1,0:T(8,128)(2,1)S(1)}, u32[]{:S(2)}, u32[]{:S(2)}) collective-permute-start(bf16[32,2304]{1,0:T(8,128)(2,1)S(1)} %get-tuple-element.22), channel_id=1, source_target_pairs={{0,8},{2,10},{4,12},{6,14},{8,16},{10,18},{12,20},{14,22},{16,24},... | collective-permute-start | bytes 442376 | tf_op jit(solution)/shard_map/ppermute | solution.py:48
  14.0 1.2 collective-permute-done.2.other_ids_ref.refs_0_
  15.7 3.7 %collective-permute-done.4.first_ref = bf16[144,512]{1,0:T(8,128)(2,1)S(1)} collective-permute-done((bf16[144,512]{1,0:T(8,128)(2,1)S(1)}, bf16[144,512]{1,0:T(8,128)(2,1)S(1)}, u32[]{:S(2)}, u32[]{:S(2)}) %collective-permute-start.4) | collective-permute-done | bytes 147488 | tf_op jit(solution)/shard_map/ppermute | solution.py:48
  19.4 2.3 %collective-permute-done.25.first_ref = bf16[32,2304]{1,0:T(8,128)(2,1)S(1)} collective-permute-done((bf16[32,2304]{1,0:T(8,128)(2,1)S(1)}, bf16[32,2304]{1,0:T(8,128)(2,1)S(1)}, u32[]{:S(2)}, u32[]{:S(2)}) %collective-permute-start.25) | collective-permute-done | bytes 147488 | tf_op jit(solution)/shard_map/ppermute | solution.py:48
  22.2 4.1 %collective-permute-done.5 = bf16[144,512]{1,0:T(8,128)(2,1)S(1)} collective-permute-done((bf16[144,512]{1,0:T(8,128)(2,1)S(1)}, bf16[144,512]{1,0:T(8,128)(2,1)S(1)}, u32[]{:S(2)}, u32[]{:S(2)}) %collective-permute-start.5) | collective-permute-done | bytes 147488 | tf_op jit(solution)/shard_map/ppermute | solution.py:48
  27.1 6.1 %collective-permute-done.26 = bf16[32,2304]{1,0:T(8,128)(2,1)S(1)} collective-permute-done((bf16[32,2304]{1,0:T(8,128)(2,1)S(1)}, bf16[32,2304]{1,0:T(8,128)(2,1)S(1)}, u32[]{:S(2)}, u32[]{:S(2)}) %collective-permute-start.26) | collective-permute-done | bytes 147488 | tf_op jit(solution)/shard_map/ppermute | solution.py:48
  34.0 1.5 %collective-permute-start.6 = (bf16[2,144,512]{2,1,0:T(8,128)(2,1)S(1)}, bf16[2,144,512]{2,1,0:T(8,128)(2,1)}, u32[]{:S(2)}, u32[]{:S(2)}) collective-permute-start(bf16[2,144,512]{2,1,0:T(8,128)(2,1)S(1)} %pack.3.refs_2_), channel_id=1, source_target_pairs={{0,1},{1,0},{2,3},{3,2},{4,5},{5,4},{6,7},{7,6},{8,9},{9,8},{10,11... | collective-permute-start | bytes 884744 | tf_op jit(solution)/shard_map/ppermute | solution.py:43
  35.8 1.5 %collective-permute-start.10 = (bf16[1,144,512]{2,1,0:T(8,128)(2,1)S(1)}, bf16[1,144,512]{2,1,0:T(8,128)(2,1)}, u32[]{:S(2)}, u32[]{:S(2)}) collective-permute-start(bf16[1,144,512]{2,1,0:T(8,128)(2,1)S(1)} %bitcast.45), channel_id=1, source_target_pairs={{0,1},{1,0},{2,3},{3,2},{4,5},{5,4},{6,7},{7,6},{8,9},{9,8},{10,11... | collective-permute-start | bytes 442376 | tf_op jit(solution)/shard_map/ppermute | solution.py:43
  37.3 3.9 %collective-permute-done.34 = bf16[32,2304]{1,0:T(8,128)(2,1)} collective-permute-done((bf16[32,2304]{1,0:T(8,128)(2,1)S(1)}, bf16[32,2304]{1,0:T(8,128)(2,1)}, u32[]{:S(2)}, u32[]{:S(2)}) %collective-permute-start.34) | collective-permute-done | bytes 147488 | tf_op jit(solution)/shard_map/ppermute | solution.py:48
  43.3 1.2 collective-permute-start.8
  44.7 6.9 %collective-permute-done.11.refs_8_ = bf16[1,144,512]{2,1,0:T(8,128)(2,1)S(1)} collective-permute-done((bf16[1,144,512]{2,1,0:T(8,128)(2,1)S(1)}, bf16[1,144,512]{2,1,0:T(8,128)(2,1)S(1)}, u32[]{:S(2)}, u32[]{:S(2)}) %collective-permute-start.11) | collective-permute-done | bytes 147488 | tf_op jit(solution)/shard_map/ppermute | solution.py:39
  55.0 3.9 %collective-permute-done.12.refs_9_ = bf16[1,144,512]{2,1,0:T(8,128)(2,1)} collective-permute-done((bf16[1,144,512]{2,1,0:T(8,128)(2,1)}, bf16[1,144,512]{2,1,0:T(8,128)(2,1)}, u32[]{:S(2)}, u32[]{:S(2)}) %collective-permute-start.12) | collective-permute-done | bytes 147488 | tf_op jit(solution)/shard_map/ppermute | solution.py:39
  58.9 1.5 %collective-permute-start.28 = (bf16[2,32,2304]{2,1,0:T(8,128)(2,1)}, bf16[2,32,2304]{2,1,0:T(8,128)(2,1)S(1)}, u32[]{:S(2)}, u32[]{:S(2)}) collective-permute-start(bf16[2,32,2304]{2,1,0:T(8,128)(2,1)} %pack.5.refs_4_), channel_id=1, source_target_pairs={{0,1},{1,0},{2,3},{3,2},{4,5},{5,4},{6,7},{7,6},{8,9},{9,8},{10,11... | collective-permute-start | bytes 884744 | tf_op jit(solution)/shard_map/ppermute | solution.py:43
  61.3 1.3 %collective-permute-start.19 = (bf16[2,144,512]{2,1,0:T(8,128)(2,1)}, bf16[2,144,512]{2,1,0:T(8,128)(2,1)}, u32[]{:S(2)}, u32[]{:S(2)}) collective-permute-start(bf16[2,144,512]{2,1,0:T(8,128)(2,1)} %collective-permute-done.17.refs_9_), channel_id=1, source_target_pairs={{0,8},{2,10},{4,12},{6,14},{8,16},{10,18},{12,20},{14,22},{16,24},... | collective-permute-start | bytes 884744 | tf_op jit(solution)/shard_map/ppermute | solution.py:48
  62.6 4.2 %project.1.refs_3_ = bf16[528,512]{1,0:T(8,128)(2,1)S(1)} custom-call(s32[21]{0:T(128)S(1)} %stack.186.spots, bf16[4,256,640]{2,1,0:T(8,128)(2,1)S(1)} %norm.1.x_ref, bf16[4,256,640]{2,1,0:T(8,128)(2,1)S(1)} %collective-permute-done.1.other_ref, f32[512,128]{1,0:T(8,128)} %get-tuple-element.24.cos_ref.cos_hbm.refs_1_, ...), custom_call_target="tpu_custom_call" | custom-call | flops 1207959552 | bytes 2359296 | tf_op jit(solution)/shard_map/project/pallas_call | solution.py:258
  67.3 3.1 %collective-permute-done.36.refs_2_ = bf16[1,32,2304]{2,1,0:T(8,128)(2,1)} collective-permute-done((bf16[1,32,2304]{2,1,0:T(8,128)(2,1)}, bf16[1,32,2304]{2,1,0:T(8,128)(2,1)}, u32[]{:S(2)}, u32[]{:S(2)}) %collective-permute-start.36) | collective-permute-done | bytes 147488 | tf_op jit(solution)/shard_map/ppermute | solution.py:43
  70.3 1.5 %collective-permute-start.16 = (bf16[2,144,512]{2,1,0:T(8,128)(2,1)}, bf16[2,144,512]{2,1,0:T(8,128)(2,1)S(1)}, u32[]{:S(2)}, u32[]{:S(2)}) collective-permute-start(bf16[2,144,512]{2,1,0:T(8,128)(2,1)} %collective-permute-done.15.refs_7_), channel_id=1, source_target_pairs={{0,1},{1,0},{2,3},{3,2},{4,5},{5,4},{6,7},{7,6},{8,9},{9,8},{10,11... | collective-permute-start | bytes 884744 | tf_op jit(solution)/shard_map/ppermute | solution.py:43
  72.7 1.7 %collective-permute-start.20 = (bf16[2,144,512]{2,1,0:T(8,128)(2,1)}, bf16[2,144,512]{2,1,0:T(8,128)(2,1)}, u32[]{:S(2)}, u32[]{:S(2)}) collective-permute-start(bf16[2,144,512]{2,1,0:T(8,128)(2,1)} %collective-permute-done.19.refs_11_), channel_id=1, source_target_pairs={{0,1},{1,0},{2,3},{3,2},{4,5},{5,4},{6,7},{7,6},{8,9},{9,8},{10,11... | collective-permute-start | bytes 884744 | tf_op jit(solution)/shard_map/ppermute | solution.py:43
  74.4 6.0 %collective-permute-done.16.refs_8_ = bf16[2,144,512]{2,1,0:T(8,128)(2,1)S(1)} collective-permute-done((bf16[2,144,512]{2,1,0:T(8,128)(2,1)}, bf16[2,144,512]{2,1,0:T(8,128)(2,1)S(1)}, u32[]{:S(2)}, u32[]{:S(2)}) %collective-permute-start.16) | collective-permute-done | bytes 294944 | tf_op jit(solution)/shard_map/ppermute | solution.py:43
  80.4 8.7 %collective-permute-done.32.refs_10_ = bf16[2,32,2304]{2,1,0:T(8,128)(2,1)S(1)} collective-permute-done((bf16[2,32,2304]{2,1,0:T(8,128)(2,1)S(1)}, bf16[2,32,2304]{2,1,0:T(8,128)(2,1)S(1)}, u32[]{:S(2)}, u32[]{:S(2)}) %collective-permute-start.32) | collective-permute-done | bytes 294944 | tf_op jit(solution)/shard_map/ppermute | solution.py:39
  90.9 7.3 %attend.1 = (bf16[2,256,256]{2,1,0:T(8,128)(2,1)S(1)}, bf16[2,256,256]{2,1,0:T(8,128)(2,1)}) custom-call(s32[22]{0:T(128)S(1)} %stack.183.place, bf16[4,256,640]{2,1,0:T(8,128)(2,1)S(1)} %norm.1.x_ref, bf16[4,256,640]{2,1,0:T(8,128)(2,1)S(1)} %collective-permute-done.1.other_ref, s32[1,256]{1,0:T(1,128)S(1)} %copy-done.15, ...), custom_call_target="tpu_custom_call" | custom-call | flops 1073741824 | bytes 1048576 | tf_op jit(solution)/shard_map/attend/pallas_call | solution.py:370
  98.4 1.4 %collective-permute-start.40 = (bf16[1,32,2304]{2,1,0:T(8,128)(2,1)}, bf16[1,32,2304]{2,1,0:T(8,128)(2,1)S(1)}, u32[]{:S(2)}, u32[]{:S(2)}) collective-permute-start(bf16[1,32,2304]{2,1,0:T(8,128)(2,1)} %collective-permute-done.36.refs_2_), channel_id=1, source_target_pairs={{0,4},{2,6},{4,0},{6,2},{8,12},{10,14},{12,8},{14,10},{16,20},{18,... | collective-permute-start | bytes 442376 | tf_op jit(solution)/shard_map/ppermute | solution.py:39
  99.7 5.0 %collective-permute-done.40.refs_6_ = bf16[1,32,2304]{2,1,0:T(8,128)(2,1)S(1)} collective-permute-done((bf16[1,32,2304]{2,1,0:T(8,128)(2,1)}, bf16[1,32,2304]{2,1,0:T(8,128)(2,1)S(1)}, u32[]{:S(2)}, u32[]{:S(2)}) %collective-permute-start.40) | collective-permute-done | bytes 147488 | tf_op jit(solution)/shard_map/ppermute | solution.py:39
  109.1 1.0 copy-done.8
  112.0 4.1 %early.1.early_ref = f32[256,2304]{1,0:T(8,128)S(1)} custom-call(s32[28]{0:T(128)S(1)} %stack.195.marks, bf16[2,256,256]{2,1,0:T(8,128)(2,1)S(1)} %get-tuple-element.20.own_hbm, bf16[2,256,256]{2,1,0:T(8,128)(2,1)S(1)} %collective-permute-done.21.other_hbm, bf16[2,32,2304]{2,1,0:T(8,128)(2,1)} %bitcast.42, bf16[2,32,2304]{2,1,0:T(8,128)(2,1)S(1)} %copy-done.4, ...), custom_call_target="tpu_custom_call" | custom-call | flops 905969664 | bytes 3538944 | tf_op jit(solution)/shard_map/early/pallas_call | solution.py:479
  116.1 4.0 %finish.1 = bf16[256,2304]{1,0:T(8,128)(2,1)} custom-call(s32[10]{0:T(128)S(1)} %stack.82.marks, bf16[2,256,256]{2,1,0:T(8,128)(2,1)S(1)} %get-tuple-element.20.own_hbm, bf16[2,256,256]{2,1,0:T(8,128)(2,1)S(1)} %collective-permute-done.21.other_hbm, f32[256,2304]{1,0:T(8,128)S(1)} %early.1.early_ref, f32[1,2304]{1,0:T(1,128)S(1)} %broadcast_in_dim.28.gain_ref, ...), custom_call_target="tpu_custom_call" | custom-call | flops 301989888 | bytes 1179648 | tf_op jit(solution)/shard_map/finish/pallas_call | solution.py:479
  (125 shorter events, 20.8 us)
Async XLA Ops:
  7.8 53.5 %collective-permute-start.1 = (bf16[4,256,640]{2,1,0:T(8,128)(2,1)S(1)}, bf16[4,256,640]{2,1,0:T(8,128)(2,1)S(1)}, u32[]{:S(2)}, u32[]{:S(2)}) collective-permute-start(bf16[4,256,640]{2,1,0:T(8,128)(2,1)S(1)} %norm.1.x_ref), channel_id=1, source_target_pairs={{0,2},{2,0},{4,6},{6,4},{8,10},{10,8},{12,14},{14,12},{16,18},{18,... | collective-permute-start | bytes 3932168 | tf_op jit(solution)/shard_map/ppermute | solution.py:35
  8.2 11.2 %collective-permute-start.23 = (bf16[2,32,2304]{2,1,0:T(8,128)(2,1)S(1)}, bf16[2,32,2304]{2,1,0:T(8,128)(2,1)}, u32[]{:S(2)}, u32[]{:S(2)}) collective-permute-start(bf16[2,32,2304]{2,1,0:T(8,128)(2,1)S(1)} %bitcast.43), channel_id=1, source_target_pairs={{0,4},{2,6},{4,0},{6,2},{8,12},{10,14},{12,8},{14,10},{16,20},{18,... | collective-permute-start | bytes 884744 | tf_op jit(solution)/shard_map/ppermute | solution.py:39
  12.4 9.3 %collective-permute-start.25 = (bf16[32,2304]{1,0:T(8,128)(2,1)S(1)}, bf16[32,2304]{1,0:T(8,128)(2,1)S(1)}, u32[]{:S(2)}, u32[]{:S(2)}) collective-permute-start(bf16[32,2304]{1,0:T(8,128)(2,1)S(1)} %get-tuple-element.22), channel_id=1, source_target_pairs={{0,8},{2,10},{4,12},{6,14},{8,16},{10,18},{12,20},{14,22},{16,24},... | collective-permute-start | bytes 442376 | tf_op jit(solution)/shard_map/ppermute | solution.py:48
  15.2 11.1 %collective-permute-start.14 = (bf16[2,144,512]{2,1,0:T(8,128)(2,1)S(1)}, bf16[2,144,512]{2,1,0:T(8,128)(2,1)S(1)}, u32[]{:S(2)}, u32[]{:S(2)}) collective-permute-start(bf16[2,144,512]{2,1,0:T(8,128)(2,1)S(1)} %get-tuple-element.18.refs_5_), channel_id=1, source_target_pairs={{0,4},{2,6},{4,0},{6,2},{8,12},{10,14},{12,8},{14,10},{16,20},{18,... | collective-permute-start | bytes 884744 | tf_op jit(solution)/shard_map/ppermute | solution.py:39
  19.4 13.9 %collective-permute-start.22 = (bf16[2,32,2304]{2,1,0:T(8,128)(2,1)S(1)}, bf16[2,32,2304]{2,1,0:T(8,128)(2,1)S(1)}, u32[]{:S(2)}, u32[]{:S(2)}) collective-permute-start(bf16[2,32,2304]{2,1,0:T(8,128)(2,1)S(1)} %bitcast.44), channel_id=1, source_target_pairs={{0,2},{2,0},{4,6},{6,4},{8,10},{10,8},{12,14},{14,12},{16,18},{18,... | collective-permute-start | bytes 884744 | tf_op jit(solution)/shard_map/ppermute | solution.py:35
  21.7 13.8 %collective-permute-start.3 = (bf16[2,144,512]{2,1,0:T(8,128)(2,1)S(1)}, bf16[2,144,512]{2,1,0:T(8,128)(2,1)S(1)}, u32[]{:S(2)}, u32[]{:S(2)}) collective-permute-start(bf16[2,144,512]{2,1,0:T(8,128)(2,1)S(1)} %get-tuple-element.16.refs_0_), channel_id=1, source_target_pairs={{0,4},{2,6},{4,0},{6,2},{8,12},{10,14},{12,8},{14,10},{16,20},{18,... | collective-permute-start | bytes 884744 | tf_op jit(solution)/shard_map/ppermute | solution.py:39
  26.3 9.5 %collective-permute-start.9 = (bf16[144,512]{1,0:T(8,128)(2,1)S(1)}, bf16[144,512]{1,0:T(8,128)(2,1)S(1)}, u32[]{:S(2)}, u32[]{:S(2)}) collective-permute-start(bf16[144,512]{1,0:T(8,128)(2,1)S(1)} %collective-permute-done.5), channel_id=1, source_target_pairs={{0,8},{2,10},{4,12},{6,14},{8,16},{10,18},{12,20},{14,22},{16,24},... | collective-permute-start | bytes 442376 | tf_op jit(solution)/shard_map/ppermute | solution.py:48
  34.0 9.3 %collective-permute-start.6 = (bf16[2,144,512]{2,1,0:T(8,128)(2,1)S(1)}, bf16[2,144,512]{2,1,0:T(8,128)(2,1)}, u32[]{:S(2)}, u32[]{:S(2)}) collective-permute-start(bf16[2,144,512]{2,1,0:T(8,128)(2,1)S(1)} %pack.3.refs_2_), channel_id=1, source_target_pairs={{0,1},{1,0},{2,3},{3,2},{4,5},{5,4},{6,7},{7,6},{8,9},{9,8},{10,11... | collective-permute-start | bytes 884744 | tf_op jit(solution)/shard_map/ppermute | solution.py:43
  35.5 8.9 %collective-permute-start.15 = (bf16[2,144,512]{2,1,0:T(8,128)(2,1)S(1)}, bf16[2,144,512]{2,1,0:T(8,128)(2,1)}, u32[]{:S(2)}, u32[]{:S(2)}) collective-permute-start(bf16[2,144,512]{2,1,0:T(8,128)(2,1)S(1)} %pack.4), channel_id=1, source_target_pairs={{0,8},{2,10},{4,12},{6,14},{8,16},{10,18},{12,20},{14,22},{16,24},... | collective-permute-start | bytes 884744 | tf_op jit(solution)/shard_map/ppermute | solution.py:48
  41.3 10.3 %collective-permute-start.7 = (bf16[2,144,512]{2,1,0:T(8,128)(2,1)S(1)}, bf16[2,144,512]{2,1,0:T(8,128)(2,1)S(1)}, u32[]{:S(2)}, u32[]{:S(2)}) collective-permute-start(bf16[2,144,512]{2,1,0:T(8,128)(2,1)S(1)} %pack.3.refs_2_), channel_id=1, source_target_pairs={{0,4},{2,6},{4,0},{6,2},{8,12},{10,14},{12,8},{14,10},{16,20},{18,... | collective-permute-start | bytes 884744 | tf_op jit(solution)/shard_map/ppermute | solution.py:39
  42.4 9.1 %collective-permute-start.11 = (bf16[1,144,512]{2,1,0:T(8,128)(2,1)S(1)}, bf16[1,144,512]{2,1,0:T(8,128)(2,1)S(1)}, u32[]{:S(2)}, u32[]{:S(2)}) collective-permute-start(bf16[1,144,512]{2,1,0:T(8,128)(2,1)S(1)} %bitcast.46), channel_id=1, source_target_pairs={{0,4},{2,6},{4,0},{6,2},{8,12},{10,14},{12,8},{14,10},{16,20},{18,... | collective-permute-start | bytes 442376 | tf_op jit(solution)/shard_map/ppermute | solution.py:39
  43.3 17.1 %collective-permute-start.8 = (bf16[2,144,512]{2,1,0:T(8,128)(2,1)}, bf16[2,144,512]{2,1,0:T(8,128)(2,1)}, u32[]{:S(2)}, u32[]{:S(2)}) collective-permute-start(bf16[2,144,512]{2,1,0:T(8,128)(2,1)} %collective-permute-done.6.refs_3_), channel_id=1, source_target_pairs={{0,4},{2,6},{4,0},{6,2},{8,12},{10,14},{12,8},{14,10},{16,20},{18,... | collective-permute-start | bytes 884744 | tf_op jit(solution)/shard_map/ppermute | solution.py:39
  44.5 16.4 %collective-permute-start.17 = (bf16[2,144,512]{2,1,0:T(8,128)(2,1)}, bf16[2,144,512]{2,1,0:T(8,128)(2,1)}, u32[]{:S(2)}, u32[]{:S(2)}) collective-permute-start(bf16[2,144,512]{2,1,0:T(8,128)(2,1)} %collective-permute-done.15.refs_7_), channel_id=1, source_target_pairs={{0,8},{2,10},{4,12},{6,14},{8,16},{10,18},{12,20},{14,22},{16,24},... | collective-permute-start | bytes 884744 | tf_op jit(solution)/shard_map/ppermute | solution.py:48
  51.6 15.2 %collective-permute-start.24 = (bf16[2,32,2304]{2,1,0:T(8,128)(2,1)}, bf16[2,32,2304]{2,1,0:T(8,128)(2,1)}, u32[]{:S(2)}, u32[]{:S(2)}) collective-permute-start(bf16[2,32,2304]{2,1,0:T(8,128)(2,1)} %collective-permute-done.23.refs_2_), channel_id=1, source_target_pairs={{0,2},{2,0},{4,6},{6,4},{8,10},{10,8},{12,14},{14,12},{16,18},{18,... | collective-permute-start | bytes 884744 | tf_op jit(solution)/shard_map/ppermute | solution.py:35
  58.9 12.9 %collective-permute-start.28 = (bf16[2,32,2304]{2,1,0:T(8,128)(2,1)}, bf16[2,32,2304]{2,1,0:T(8,128)(2,1)S(1)}, u32[]{:S(2)}, u32[]{:S(2)}) collective-permute-start(bf16[2,32,2304]{2,1,0:T(8,128)(2,1)} %pack.5.refs_4_), channel_id=1, source_target_pairs={{0,1},{1,0},{2,3},{3,2},{4,5},{5,4},{6,7},{7,6},{8,9},{9,8},{10,11... | collective-permute-start | bytes 884744 | tf_op jit(solution)/shard_map/ppermute | solution.py:43
  60.4 11.9 %collective-permute-start.30 = (bf16[2,32,2304]{2,1,0:T(8,128)(2,1)}, bf16[2,32,2304]{2,1,0:T(8,128)(2,1)S(1)}, u32[]{:S(2)}, u32[]{:S(2)}) collective-permute-start(bf16[2,32,2304]{2,1,0:T(8,128)(2,1)} %pack.5.refs_4_), channel_id=1, source_target_pairs={{0,4},{2,6},{4,0},{6,2},{8,12},{10,14},{12,8},{14,10},{16,20},{18,... | collective-permute-start | bytes 884744 | tf_op jit(solution)/shard_map/ppermute | solution.py:39
  60.9 9.4 %collective-permute-start.36 = (bf16[1,32,2304]{2,1,0:T(8,128)(2,1)}, bf16[1,32,2304]{2,1,0:T(8,128)(2,1)}, u32[]{:S(2)}, u32[]{:S(2)}) collective-permute-start(bf16[1,32,2304]{2,1,0:T(8,128)(2,1)} %bitcast.36.refs_0_), channel_id=1, source_target_pairs={{0,1},{1,0},{2,3},{3,2},{4,5},{5,4},{6,7},{7,6},{8,9},{9,8},{10,11... | collective-permute-start | bytes 442376 | tf_op jit(solution)/shard_map/ppermute | solution.py:43
  61.3 11.4 %collective-permute-start.19 = (bf16[2,144,512]{2,1,0:T(8,128)(2,1)}, bf16[2,144,512]{2,1,0:T(8,128)(2,1)}, u32[]{:S(2)}, u32[]{:S(2)}) collective-permute-start(bf16[2,144,512]{2,1,0:T(8,128)(2,1)} %collective-permute-done.17.refs_9_), channel_id=1, source_target_pairs={{0,8},{2,10},{4,12},{6,14},{8,16},{10,18},{12,20},{14,22},{16,24},... | collective-permute-start | bytes 884744 | tf_op jit(solution)/shard_map/ppermute | solution.py:48
  66.8 23.7 %collective-permute-start.13 = (bf16[528,512]{1,0:T(8,128)(2,1)S(1)}, bf16[528,512]{1,0:T(8,128)(2,1)}, u32[]{:S(2)}, u32[]{:S(2)}) collective-permute-start(bf16[528,512]{1,0:T(8,128)(2,1)S(1)} %project.1.refs_3_), channel_id=1, source_target_pairs={{0,4},{2,6},{4,8},{6,10},{8,12},{10,14},{12,16},{14,18},{16,20},{1... | collective-permute-start | bytes 1622024 | tf_op jit(solution)/shard_map/ppermute | solution.py:53
  70.3 10.1 %collective-permute-start.16 = (bf16[2,144,512]{2,1,0:T(8,128)(2,1)}, bf16[2,144,512]{2,1,0:T(8,128)(2,1)S(1)}, u32[]{:S(2)}, u32[]{:S(2)}) collective-permute-start(bf16[2,144,512]{2,1,0:T(8,128)(2,1)} %collective-permute-done.15.refs_7_), channel_id=1, source_target_pairs={{0,1},{1,0},{2,3},{3,2},{4,5},{5,4},{6,7},{7,6},{8,9},{9,8},{10,11... | collective-permute-start | bytes 884744 | tf_op jit(solution)/shard_map/ppermute | solution.py:43
  71.8 17.3 %collective-permute-start.32 = (bf16[2,32,2304]{2,1,0:T(8,128)(2,1)S(1)}, bf16[2,32,2304]{2,1,0:T(8,128)(2,1)S(1)}, u32[]{:S(2)}, u32[]{:S(2)}) collective-permute-start(bf16[2,32,2304]{2,1,0:T(8,128)(2,1)S(1)} %collective-permute-done.28.refs_6_), channel_id=1, source_target_pairs={{0,4},{2,6},{4,0},{6,2},{8,12},{10,14},{12,8},{14,10},{16,20},{18,... | collective-permute-start | bytes 884744 | tf_op jit(solution)/shard_map/ppermute | solution.py:39
  72.3 17.6 %collective-permute-start.18 = (bf16[2,144,512]{2,1,0:T(8,128)(2,1)}, bf16[2,144,512]{2,1,0:T(8,128)(2,1)}, u32[]{:S(2)}, u32[]{:S(2)}) collective-permute-start(bf16[2,144,512]{2,1,0:T(8,128)(2,1)} %collective-permute-done.17.refs_9_), channel_id=1, source_target_pairs={{0,1},{1,0},{2,3},{3,2},{4,5},{5,4},{6,7},{7,6},{8,9},{9,8},{10,11... | collective-permute-start | bytes 884744 | tf_op jit(solution)/shard_map/ppermute | solution.py:43
  72.7 17.7 %collective-permute-start.20 = (bf16[2,144,512]{2,1,0:T(8,128)(2,1)}, bf16[2,144,512]{2,1,0:T(8,128)(2,1)}, u32[]{:S(2)}, u32[]{:S(2)}) collective-permute-start(bf16[2,144,512]{2,1,0:T(8,128)(2,1)} %collective-permute-done.19.refs_11_), channel_id=1, source_target_pairs={{0,1},{1,0},{2,3},{3,2},{4,5},{5,4},{6,7},{7,6},{8,9},{9,8},{10,11... | collective-permute-start | bytes 884744 | tf_op jit(solution)/shard_map/ppermute | solution.py:43
  80.4 17.9 %collective-permute-start.27 = (bf16[2,32,2304]{2,1,0:T(8,128)(2,1)}, bf16[2,32,2304]{2,1,0:T(8,128)(2,1)}, u32[]{:S(2)}, u32[]{:S(2)}) collective-permute-start(bf16[2,32,2304]{2,1,0:T(8,128)(2,1)} %pack.5.refs_4_), channel_id=1, source_target_pairs={{0,2},{2,0},{4,6},{6,4},{8,10},{10,8},{12,14},{14,12},{16,18},{18,... | collective-permute-start | bytes 884744 | tf_op jit(solution)/shard_map/ppermute | solution.py:35
  89.1 9.1 %collective-permute-start.38 = (bf16[1,32,2304]{2,1,0:T(8,128)(2,1)}, bf16[1,32,2304]{2,1,0:T(8,128)(2,1)}, u32[]{:S(2)}, u32[]{:S(2)}) collective-permute-start(bf16[1,32,2304]{2,1,0:T(8,128)(2,1)} %bitcast.36.refs_0_), channel_id=1, source_target_pairs={{0,4},{2,6},{4,0},{6,2},{8,12},{10,14},{12,8},{14,10},{16,20},{18,... | collective-permute-start | bytes 442376 | tf_op jit(solution)/shard_map/ppermute | solution.py:39
  89.9 14.8 %collective-permute-start.29 = (bf16[2,32,2304]{2,1,0:T(8,128)(2,1)}, bf16[2,32,2304]{2,1,0:T(8,128)(2,1)S(1)}, u32[]{:S(2)}, u32[]{:S(2)}) collective-permute-start(bf16[2,32,2304]{2,1,0:T(8,128)(2,1)} %copy-done.18), channel_id=1, source_target_pairs={{0,2},{2,0},{4,6},{6,4},{8,10},{10,8},{12,14},{14,12},{16,18},{18,... | collective-permute-start | bytes 884744 | tf_op jit(solution)/shard_map/ppermute | solution.py:35
  90.4 15.6 %collective-permute-start.31 = (bf16[2,32,2304]{2,1,0:T(8,128)(2,1)}, bf16[2,32,2304]{2,1,0:T(8,128)(2,1)S(1)}, u32[]{:S(2)}, u32[]{:S(2)}) collective-permute-start(bf16[2,32,2304]{2,1,0:T(8,128)(2,1)} %copy-done.19), channel_id=1, source_target_pairs={{0,2},{2,0},{4,6},{6,4},{8,10},{10,8},{12,14},{14,12},{16,18},{18,... | collective-permute-start | bytes 884744 | tf_op jit(solution)/shard_map/ppermute | solution.py:35
  90.5 16.2 %collective-permute-start.33 = (bf16[2,32,2304]{2,1,0:T(8,128)(2,1)}, bf16[2,32,2304]{2,1,0:T(8,128)(2,1)S(1)}, u32[]{:S(2)}, u32[]{:S(2)}) collective-permute-start(bf16[2,32,2304]{2,1,0:T(8,128)(2,1)} %copy-done.21), channel_id=1, source_target_pairs={{0,2},{2,0},{4,6},{6,4},{8,10},{10,8},{12,14},{14,12},{16,18},{18,... | collective-permute-start | bytes 884744 | tf_op jit(solution)/shard_map/ppermute | solution.py:35
  98.2 10.0 %collective-permute-start.21 = (bf16[2,256,256]{2,1,0:T(8,128)(2,1)}, bf16[2,256,256]{2,1,0:T(8,128)(2,1)S(1)}, u32[]{:S(2)}, u32[]{:S(2)}) collective-permute-start(bf16[2,256,256]{2,1,0:T(8,128)(2,1)} %get-tuple-element.21), channel_id=1, source_target_pairs={{0,2},{2,0},{4,6},{6,4},{8,10},{10,8},{12,14},{14,12},{16,18},{18,... | collective-permute-start | bytes 786440 | tf_op jit(solution)/shard_map/ppermute | solution.py:35
  104.7 11.3 %collective-permute-start.35 = (bf16[1,32,2304]{2,1,0:T(8,128)(2,1)}, bf16[1,32,2304]{2,1,0:T(8,128)(2,1)S(1)}, u32[]{:S(2)}, u32[]{:S(2)}) collective-permute-start(bf16[1,32,2304]{2,1,0:T(8,128)(2,1)} %bitcast.36.refs_0_), channel_id=1, source_target_pairs={{0,2},{2,0},{4,6},{6,4},{8,10},{10,8},{12,14},{14,12},{16,18},{18,... | collective-permute-start | bytes 442376 | tf_op jit(solution)/shard_map/ppermute | solution.py:35
  105.5 10.6 %collective-permute-start.37 = (bf16[1,32,2304]{2,1,0:T(8,128)(2,1)}, bf16[1,32,2304]{2,1,0:T(8,128)(2,1)S(1)}, u32[]{:S(2)}, u32[]{:S(2)}) collective-permute-start(bf16[1,32,2304]{2,1,0:T(8,128)(2,1)} %collective-permute-done.36.refs_2_), channel_id=1, source_target_pairs={{0,2},{2,0},{4,6},{6,4},{8,10},{10,8},{12,14},{14,12},{16,18},{18,... | collective-permute-start | bytes 442376 | tf_op jit(solution)/shard_map/ppermute | solution.py:35
  106.7 9.4 %collective-permute-start.39 = (bf16[1,32,2304]{2,1,0:T(8,128)(2,1)}, bf16[1,32,2304]{2,1,0:T(8,128)(2,1)S(1)}, u32[]{:S(2)}, u32[]{:S(2)}) collective-permute-start(bf16[1,32,2304]{2,1,0:T(8,128)(2,1)} %collective-permute-done.38.refs_4_), channel_id=1, source_target_pairs={{0,2},{2,0},{4,6},{6,4},{8,10},{10,8},{12,14},{14,12},{16,18},{18,... | collective-permute-start | bytes 442376 | tf_op jit(solution)/shard_map/ppermute | solution.py:35
  (37 other events, 333.3 us)

commit v5 on v4

--- a/solution.py
+++ b/solution.py
@@ -396,15 +396,18 @@
     return jnp.where(head // GROUPS == core, own_ref[head % GROUPS], other_ref[head % GROUPS])
 
 
-def early_kernel(slots, heads, marks, own_hbm, other_hbm, *refs):
+def finish_kernel(slots, heads, marks, own_hbm, other_hbm, gain_ref, hid_hbm, *refs):
     pieces = refs[: len(slots)]
-    out_ref, held, own_ref, other_ref, sems, ends = refs[len(slots) :]
+    out_hbm, held, own_ref, other_ref, hid_ref, sum_ref, out_ref, sems, ends = refs[len(slots) :]
     fetch = fetch_pair(own_hbm, other_hbm, own_ref, other_ref, ends)
     copies = fetch_layers(slots, heads + 1, marks, pieces, held, sems)
+    hidden = pltpu.make_async_copy(hid_hbm, hid_ref, ends.at[2])
+    hidden.start()
     for copy in fetch:
         copy.wait()
-    width = out_ref.shape[1]
+    tokens, width = sum_ref.shape
     tile = next(t for t in (768, 512, 256, 128, width) if width % t == 0)
+    square = jnp.zeros((tokens, 1), jnp.float32)
     for s in range(heads):
         for slot, copy in copies:
             if slot == s:
@@ -412,34 +415,14 @@
         att = head_of(own_ref, other_ref, marks[heads], marks[s])
         for n in range(width // tile):
             part = slice(n * tile, (n + 1) * tile)
-            product = jnp.dot(att, held[s, :, part], preferred_element_type=jnp.float32)
-            out_ref[:, part] = product if s == 0 else out_ref[:, part] + product
-
-
-def finish_kernel(slots, marks, own_hbm, other_hbm, early_ref, gain_ref, hid_hbm, *refs):
-    pieces = refs[: len(slots)]
-    out_hbm, held, own_ref, other_ref, hid_ref, sum_ref, out_ref, sems, ends = refs[len(slots) :]
-    heads = fetch_pair(own_hbm, other_hbm, own_ref, other_ref, ends)
-    fetch = pltpu.make_async_copy(hid_hbm, hid_ref, ends.at[2])
-    copies = fetch_layers(slots, 2, marks, pieces, held, sems)
-    fetch.start()
-    tokens, width = sum_ref.shape
-    tile = next(t for t in (768, 512, 256, 128, width) if width % t == 0)
-    for copy in heads:
-        copy.wait()
-    att = head_of(own_ref, other_ref, marks[1], marks[0])
-    for _, copy in copies:
-        copy.wait()
-    square = jnp.zeros((tokens, 1), jnp.float32)
-    for n in range(width // tile):
-        part = slice(n * tile, (n + 1) * tile)
-        total = early_ref[:, part] + jnp.dot(
-            att, held[0, :, part], preferred_element_type=jnp.float32
-        )
-        sum_ref[:, part] = total
-        square = square + jnp.sum(total * total, axis=1, keepdims=True)
+            total = jnp.dot(att, held[s, :, part], preferred_element_type=jnp.float32)
+            if s > 0:
+                total = sum_ref[:, part] + total
+            sum_ref[:, part] = total
+            if s == heads - 1:
+                square = square + jnp.sum(total * total, axis=1, keepdims=True)
     scale = lax.rsqrt(square / width + EPS)
-    fetch.wait()
+    hidden.wait()
     step = 64
     stores = []
     for m in range(tokens // step):
@@ -454,45 +437,33 @@
         store.wait()
 
 
-def out_project(own, other, arrays, slots, marks, heads, rows, finish=None):
-    width = arrays[0].shape[2]
-    tokens = own.shape[1]
-    total = sum(len(blocks) for blocks in slots)
+def finish(own, other, arrays, slots, marks, heads, rows, gain, hidden):
+    tokens, width = hidden.shape
     vmem, left = pl.BlockSpec(memory_space=pltpu.VMEM), pl.BlockSpec(memory_space=pl.ANY)
-    held = [pltpu.VMEM((heads, rows, width), jnp.bfloat16)]
-    held += [pltpu.VMEM(own.shape, jnp.bfloat16)] * 2
-    sems = [pltpu.SemaphoreType.DMA((total,))]
-    extra, specs = [], []
-    if finish:
-        early, gain, hidden = finish
-        extra, specs = [early, gain] + in_hbm([hidden]), [vmem, vmem, left]
-        held += [
+    return pl.pallas_call(
+        functools.partial(finish_kernel, slots, heads),
+        out_shape=jax.ShapeDtypeStruct((tokens, width), jnp.bfloat16),
+        in_specs=[pl.BlockSpec(memory_space=pltpu.SMEM), left, left, vmem, left]
+        + [left] * len(arrays),
+        out_specs=left,
+        scratch_shapes=[
+            pltpu.VMEM((heads, rows, width), jnp.bfloat16),
+            pltpu.VMEM(own.shape, jnp.bfloat16),
+            pltpu.VMEM(own.shape, jnp.bfloat16),
             pltpu.VMEM((tokens, width), jnp.bfloat16),
             pltpu.VMEM((tokens, width), jnp.float32),
             pltpu.VMEM((tokens, width), jnp.bfloat16),
-        ]
-        sems.append(pltpu.SemaphoreType.DMA((3 + tokens // 64,)))
-        body = functools.partial(finish_kernel, slots)
-    else:
-        sems.append(pltpu.SemaphoreType.DMA((2,)))
-        body = functools.partial(early_kernel, slots, heads)
-    return pl.pallas_call(
-        body,
-        out_shape=jax.ShapeDtypeStruct((tokens, width), jnp.bfloat16 if finish else jnp.float32),
-        in_specs=[pl.BlockSpec(memory_space=pltpu.SMEM)]
-        + [left] * 2
-        + specs
-        + [left] * len(arrays),
-        out_specs=left if finish else vmem,
-        scratch_shapes=held + sems,
-        compiler_params=pltpu.CompilerParams(vmem_limit_bytes=14 * 1024 * 1024),
+            pltpu.SemaphoreType.DMA((sum(len(blocks) for blocks in slots),)),
+            pltpu.SemaphoreType.DMA((3 + tokens // 64,)),
+        ],
+        compiler_params=pltpu.CompilerParams(vmem_limit_bytes=18 * 1024 * 1024),
         cost_estimate=pl.CostEstimate(
             flops=2 * tokens * rows * heads * width,
             bytes_accessed=2 * rows * heads * width,
             transcendentals=0,
         ),
-        name="finish" if finish else "early",
-    )(marks, own, other, *extra, *arrays)
+        name="finish",
+    )(marks, own, other, gain, *in_hbm([hidden]), *arrays)
 
 
 def per_device(hidden_in, segment_ids, pre_gain, w_qkv, w_out, post_gain):
@@ -512,7 +483,9 @@
     half_rows = w_out.shape[0] // 2
     came = swap_core(w_qkv)
     own_kv, own_q, kv_unit, q_unit, out_unit = prepare(w_qkv, came, w_out, core, plane)
-    first_pos, out_unit = lax.optimization_barrier((chip * chip_rows, out_unit))
+    first_pos, out_unit, pre_gain = lax.optimization_barrier(
+        (chip * chip_rows, out_unit, pre_gain)
+    )
     kv_pieces = gather_near(own_kv, kv_unit, plane, pair, line_count, "1")
     q_pieces = gather_wide(own_q, q_unit, plane, pair, line_count)
     out_own = w_out.reshape(2, half_rows, model)
@@ -565,21 +538,23 @@
 
     swapped = [swap_core(block) for block, _ in out_pieces]
 
-    def out_part(backs, finish=None):
-        heads = [(line - back + line_count) % line_count for back in backs]
-        offsets, arrays, where = [], [], []
-        for (block, blocks), other in zip(out_pieces, swapped):
-            if blocks[0][0] not in backs:
-                continue
-            for array, c in ((in_hbm([block])[0], core), (other, 1 - core)):
-                arrays.append(array)
-                where.append(tuple(backs.index(back) for back, _, _ in blocks))
-                offsets += [((y * 2 + c) * 2 + h) * half_rows for _, y, h in blocks]
-        marks = jnp.stack([jnp.asarray(mark, jnp.int32) for mark in heads + [core] + offsets])
-        return out_project(att_own, att_other, arrays, tuple(where), marks, len(backs), 8 * half_rows, finish)
-
-    early = out_part([0, 1, 2])
-    done = out_part([3], (early, post_gain[None, :], hidden_in[0]))
+    offsets, arrays, slots = [], [], []
+    for (block, blocks), other in zip(out_pieces, swapped):
+        for array, c in zip(in_hbm([block, other]), (core, 1 - core)):
+            arrays.append(array)
+            slots.append(tuple(back for back, _, _ in blocks))
+            offsets += [((y * 2 + c) * 2 + h) * half_rows for _, y, h in blocks]
+    done = finish(
+        att_own,
+        att_other,
+        arrays,
+        tuple(slots),
+        scalars(layers + [core] + offsets),
+        line_count,
+        8 * half_rows,
+        post_gain[None, :],
+        hidden_in[0],
+    )
     return done[None]
 
 

time: 121 us -> 112 us (0.926)
  local copies, waits for them, and re-layouts: 10.8 us -> 2.63 us
  Pallas kernels: 23.8 us -> 21.3 us
  waiting for transfers between devices: 57.5 us -> 58.9 us
    unnamed x54 -> x48, local copies, waits for them, and re-layouts: 9.73 us -> 2.31 us
    pallas_call x2 -> x1, Pallas kernels: 8.03 us -> 5.58 us  [finish(): pl.pallas_call(functools.partial(finish_kernel, slots, heads), out_shape=...]
    ppermute x14, waiting for transfers between devices: 2.23 us -> 4.19 us  [swap_core(): lax.ppermute(block, 'seq', [(i, i ^ 1) for i in range(lax.axis_size('seq'...]
    ppermute x7, waiting for transfers between devices: 10.4 us -> 8.42 us  [swap_batch(): return lax.ppermute(block, 'batch', [(0, 1), (1, 0)])]
    ppermute x11, starting transfers between devices: 8.72 us -> 10.3 us  [swap_pair(): lax.ppermute(block, 'seq', [(i, i ^ 2) for i in range(lax.axis_size('seq'...]
    ppermute x11, waiting for transfers between devices: 24.4 us -> 25.7 us  [swap_pair(): lax.ppermute(block, 'seq', [(i, i ^ 2) for i in range(lax.axis_size('seq'...]
  transfers between devices with their start and end apart: 42 -> 42, of which waited for: 16 -> 17; matrix products, arithmetic and copies ran while one was open for 1% -> 2% of each run, Pallas kernels for 14% -> 14%
where the time goes in v5:
time: 112 us
  waiting for transfers between devices  58.9 us (53%)
  starting transfers between devices  26.4 us (24%)
  Pallas kernels  21.3 us (19%)
  local copies, waits for them, and re-layouts  2.63 us (2%)
  other arithmetic  1.91 us (2%)
    ppermute x11, waiting for transfers between devices, swap_pair(): lax.ppermute(block, 'seq', [(i, i ^ 2) for i in range(lax.axis_size('seq'...  25.7 us
    ppermute x9, waiting for transfers between devices, along_line(): lax.ppermute(block, 'seq', [(i, (i + 4 * steps) % count) for i in range(c...  20.6 us
    ppermute x11, starting transfers between devices, swap_pair(): lax.ppermute(block, 'seq', [(i, i ^ 2) for i in range(lax.axis_size('seq'...  10.3 us
    ppermute x7, waiting for transfers between devices, swap_batch(): return lax.ppermute(block, 'batch', [(0, 1), (1, 0)])  8.42 us
    ppermute x7, starting transfers between devices, swap_batch(): return lax.ppermute(block, 'batch', [(0, 1), (1, 0)])  7.92 us
    pallas_call x1, Pallas kernels, attend(): pl.pallas_call(functools.partial(attend_kernel, slots, layers), out_shape...  7.24 us
    pallas_call x1, Pallas kernels, finish(): pl.pallas_call(functools.partial(finish_kernel, slots, heads), out_shape=...  5.58 us
    ppermute x9, starting transfers between devices, along_line(): lax.ppermute(block, 'seq', [(i, (i + 4 * steps) % count) for i in range(c...  4.6 us
  transfers between devices with their start and end apart: 42, of which 17 were waited for; matrix products, arithmetic and copies ran while one was open for 2% of the time, Pallas kernels for 14%

profile of v5, /device:TPU:0, one launch (start us, length us, event | category | flops | bytes accessed | tf_op | source)
XLA Modules:
  0.0 111.6 jit_solution(17879609867330552859)
XLA Ops:
  0.6 1.7 %collective-permute-done.came_ref = bf16[144,2048]{1,0:T(8,128)(2,1)S(1)} collective-permute-done((bf16[144,2048]{1,0:T(8,128)(2,1)}, bf16[144,2048]{1,0:T(8,128)(2,1)S(1)}, u32[]{:S(2)}, u32[]{:S(2)}) %collective-permute-start) | collective-permute-done | bytes 589856 | tf_op jit(solution)/shard_map/ppermute | solution.py:35
  3.6 1.8 %multiply_sine_fusion = (f32[512,128]{1,0:T(8,128)}, f32[512,128]{1,0:T(8,128)}) fusion(f32[128]{0:T(128)S(1)} %negate_power_fusion, f32[512]{0:T(512)S(1)} %add_convert_fusion), kind=kLoop, calls=%fused_computation | loop fusion | flops 65536 | bytes 526848 | tf_op jit(solution)/shard_map/sin | solution.py:31
  5.5 2.3 %norm.1.x_ref = bf16[4,256,640]{2,1,0:T(8,128)(2,1)S(1)} custom-call(bf16[256,2304]{1,0:T(8,128)(2,1)} %bitcast.40, f32[1,2304]{1,0:T(1,128)S(1)} %broadcast_in_dim.24.gain_ref, f32[512,128]{1,0:T(8,128)} %get-tuple-element.26.cos_ref.cos_hbm.refs_1_, f32[512,128]{1,0:T(8,128)} %get-tuple-element.25.sin_ref.sin_hbm.refs_2_), custom_call_target="tpu_custom_call" | custom-call | flops 1000000 | bytes 2359296 | tf_op jit(solution)/shard_map/norm/pallas_call | solution.py:179
  8.2 2.6 %collective-permute-start.23 = (bf16[2,32,2304]{2,1,0:T(8,128)(2,1)S(1)}, bf16[2,32,2304]{2,1,0:T(8,128)(2,1)S(1)}, u32[]{:S(2)}, u32[]{:S(2)}) collective-permute-start(bf16[2,32,2304]{2,1,0:T(8,128)(2,1)S(1)} %bitcast.44), channel_id=1, source_target_pairs={{0,4},{2,6},{4,0},{6,2},{8,12},{10,14},{12,8},{14,10},{16,20},{18,... | collective-permute-start | bytes 884744 | tf_op jit(solution)/shard_map/ppermute | solution.py:39
  10.9 1.6 %collective-permute-start.4 = (bf16[144,512]{1,0:T(8,128)(2,1)S(1)}, bf16[144,512]{1,0:T(8,128)(2,1)S(1)}, u32[]{:S(2)}, u32[]{:S(2)}) collective-permute-start(bf16[144,512]{1,0:T(8,128)(2,1)S(1)} %get-tuple-element.19), channel_id=1, source_target_pairs={{0,8},{2,10},{4,12},{6,14},{8,16},{10,18},{12,20},{14,22},{16,24},... | collective-permute-start | bytes 442376 | tf_op jit(solution)/shard_map/ppermute | solution.py:48
  14.1 1.6 %collective-permute-start.25 = (bf16[32,2304]{1,0:T(8,128)(2,1)S(1)}, bf16[32,2304]{1,0:T(8,128)(2,1)S(1)}, u32[]{:S(2)}, u32[]{:S(2)}) collective-permute-start(bf16[32,2304]{1,0:T(8,128)(2,1)S(1)} %get-tuple-element.24), channel_id=1, source_target_pairs={{0,8},{2,10},{4,12},{6,14},{8,16},{10,18},{12,20},{14,22},{16,24},... | collective-permute-start | bytes 442376 | tf_op jit(solution)/shard_map/ppermute | solution.py:48
  15.7 3.0 %collective-permute-done.4.first_ref = bf16[144,512]{1,0:T(8,128)(2,1)S(1)} collective-permute-done((bf16[144,512]{1,0:T(8,128)(2,1)S(1)}, bf16[144,512]{1,0:T(8,128)(2,1)S(1)}, u32[]{:S(2)}, u32[]{:S(2)}) %collective-permute-start.4) | collective-permute-done | bytes 147488 | tf_op jit(solution)/shard_map/ppermute | solution.py:48
  18.9 2.9 %collective-permute-done.25.first_ref = bf16[32,2304]{1,0:T(8,128)(2,1)S(1)} collective-permute-done((bf16[32,2304]{1,0:T(8,128)(2,1)S(1)}, bf16[32,2304]{1,0:T(8,128)(2,1)S(1)}, u32[]{:S(2)}, u32[]{:S(2)}) %collective-permute-start.25) | collective-permute-done | bytes 147488 | tf_op jit(solution)/shard_map/ppermute | solution.py:48
  21.8 1.4 %collective-permute-start.3 = (bf16[2,144,512]{2,1,0:T(8,128)(2,1)S(1)}, bf16[2,144,512]{2,1,0:T(8,128)(2,1)S(1)}, u32[]{:S(2)}, u32[]{:S(2)}) collective-permute-start(bf16[2,144,512]{2,1,0:T(8,128)(2,1)S(1)} %get-tuple-element.18.refs_0_), channel_id=1, source_target_pairs={{0,4},{2,6},{4,0},{6,2},{8,12},{10,14},{12,8},{14,10},{16,20},{18,... | collective-permute-start | bytes 884744 | tf_op jit(solution)/shard_map/ppermute | solution.py:39
  23.2 2.5 %collective-permute-done.5 = bf16[144,512]{1,0:T(8,128)(2,1)S(1)} collective-permute-done((bf16[144,512]{1,0:T(8,128)(2,1)S(1)}, bf16[144,512]{1,0:T(8,128)(2,1)S(1)}, u32[]{:S(2)}, u32[]{:S(2)}) %collective-permute-start.5) | collective-permute-done | bytes 147488 | tf_op jit(solution)/shard_map/ppermute | solution.py:48
  25.7 1.4 %collective-permute-start.9 = (bf16[144,512]{1,0:T(8,128)(2,1)S(1)}, bf16[144,512]{1,0:T(8,128)(2,1)S(1)}, u32[]{:S(2)}, u32[]{:S(2)}) collective-permute-start(bf16[144,512]{1,0:T(8,128)(2,1)S(1)} %collective-permute-done.5), channel_id=1, source_target_pairs={{0,8},{2,10},{4,12},{6,14},{8,16},{10,18},{12,20},{14,22},{16,24},... | collective-permute-start | bytes 442376 | tf_op jit(solution)/shard_map/ppermute | solution.py:48
  27.1 5.7 %collective-permute-done.26 = bf16[32,2304]{1,0:T(8,128)(2,1)S(1)} collective-permute-done((bf16[32,2304]{1,0:T(8,128)(2,1)S(1)}, bf16[32,2304]{1,0:T(8,128)(2,1)S(1)}, u32[]{:S(2)}, u32[]{:S(2)}) %collective-permute-start.26) | collective-permute-done | bytes 147488 | tf_op jit(solution)/shard_map/ppermute | solution.py:48
  32.8 2.1 %collective-permute-done.9 = bf16[144,512]{1,0:T(8,128)(2,1)S(1)} collective-permute-done((bf16[144,512]{1,0:T(8,128)(2,1)S(1)}, bf16[144,512]{1,0:T(8,128)(2,1)S(1)}, u32[]{:S(2)}, u32[]{:S(2)}) %collective-permute-start.9) | collective-permute-done | bytes 147488 | tf_op jit(solution)/shard_map/ppermute | solution.py:48
  34.9 1.5 %collective-permute-start.10 = (bf16[1,144,512]{2,1,0:T(8,128)(2,1)S(1)}, bf16[1,144,512]{2,1,0:T(8,128)(2,1)S(1)}, u32[]{:S(2)}, u32[]{:S(2)}) collective-permute-start(bf16[1,144,512]{2,1,0:T(8,128)(2,1)S(1)} %bitcast.45), channel_id=1, source_target_pairs={{0,1},{1,0},{2,3},{3,2},{4,5},{5,4},{6,7},{7,6},{8,9},{9,8},{10,11... | collective-permute-start | bytes 442376 | tf_op jit(solution)/shard_map/ppermute | solution.py:43
  37.1 4.3 %collective-permute-done.34 = bf16[32,2304]{1,0:T(8,128)(2,1)} collective-permute-done((bf16[32,2304]{1,0:T(8,128)(2,1)S(1)}, bf16[32,2304]{1,0:T(8,128)(2,1)}, u32[]{:S(2)}, u32[]{:S(2)}) %collective-permute-start.34) | collective-permute-done | bytes 147488 | tf_op jit(solution)/shard_map/ppermute | solution.py:48
  42.7 4.7 %collective-permute-done.11.refs_8_ = bf16[1,144,512]{2,1,0:T(8,128)(2,1)S(1)} collective-permute-done((bf16[1,144,512]{2,1,0:T(8,128)(2,1)S(1)}, bf16[1,144,512]{2,1,0:T(8,128)(2,1)S(1)}, u32[]{:S(2)}, u32[]{:S(2)}) %collective-permute-start.11) | collective-permute-done | bytes 147488 | tf_op jit(solution)/shard_map/ppermute | solution.py:39
  47.3 1.6 %collective-permute-start.7 = (bf16[2,144,512]{2,1,0:T(8,128)(2,1)S(1)}, bf16[2,144,512]{2,1,0:T(8,128)(2,1)S(1)}, u32[]{:S(2)}, u32[]{:S(2)}) collective-permute-start(bf16[2,144,512]{2,1,0:T(8,128)(2,1)S(1)} %pack.3.refs_2_), channel_id=1, source_target_pairs={{0,4},{2,6},{4,0},{6,2},{8,12},{10,14},{12,8},{14,10},{16,20},{18,... | collective-permute-start | bytes 884744 | tf_op jit(solution)/shard_map/ppermute | solution.py:39
  48.9 1.5 %collective-permute-start.36 = (bf16[1,32,2304]{2,1,0:T(8,128)(2,1)}, bf16[1,32,2304]{2,1,0:T(8,128)(2,1)S(1)}, u32[]{:S(2)}, u32[]{:S(2)}) collective-permute-start(bf16[1,32,2304]{2,1,0:T(8,128)(2,1)} %bitcast.36.refs_12_), channel_id=1, source_target_pairs={{0,1},{1,0},{2,3},{3,2},{4,5},{5,4},{6,7},{7,6},{8,9},{9,8},{10,11... | collective-permute-start | bytes 442376 | tf_op jit(solution)/shard_map/ppermute | solution.py:43
  50.9 3.4 %collective-permute-done.36.refs_14_ = bf16[1,32,2304]{2,1,0:T(8,128)(2,1)S(1)} collective-permute-done((bf16[1,32,2304]{2,1,0:T(8,128)(2,1)}, bf16[1,32,2304]{2,1,0:T(8,128)(2,1)S(1)}, u32[]{:S(2)}, u32[]{:S(2)}) %collective-permute-start.36) | collective-permute-done | bytes 147488 | tf_op jit(solution)/shard_map/ppermute | solution.py:43
  55.7 1.5 %collective-permute-done.7.refs_4_ = bf16[2,144,512]{2,1,0:T(8,128)(2,1)S(1)} collective-permute-done((bf16[2,144,512]{2,1,0:T(8,128)(2,1)S(1)}, bf16[2,144,512]{2,1,0:T(8,128)(2,1)S(1)}, u32[]{:S(2)}, u32[]{:S(2)}) %collective-permute-start.7) | collective-permute-done | bytes 294944 | tf_op jit(solution)/shard_map/ppermute | solution.py:39
  57.2 5.8 %collective-permute-done.12.refs_9_ = bf16[1,144,512]{2,1,0:T(8,128)(2,1)S(1)} collective-permute-done((bf16[1,144,512]{2,1,0:T(8,128)(2,1)S(1)}, bf16[1,144,512]{2,1,0:T(8,128)(2,1)S(1)}, u32[]{:S(2)}, u32[]{:S(2)}) %collective-permute-start.12) | collective-permute-done | bytes 147488 | tf_op jit(solution)/shard_map/ppermute | solution.py:39
  63.7 1.3 %collective-permute-start.38 = (bf16[1,32,2304]{2,1,0:T(8,128)(2,1)}, bf16[1,32,2304]{2,1,0:T(8,128)(2,1)}, u32[]{:S(2)}, u32[]{:S(2)}) collective-permute-start(bf16[1,32,2304]{2,1,0:T(8,128)(2,1)} %bitcast.36.refs_12_), channel_id=1, source_target_pairs={{0,4},{2,6},{4,0},{6,2},{8,12},{10,14},{12,8},{14,10},{16,20},{18,... | collective-permute-start | bytes 442376 | tf_op jit(solution)/shard_map/ppermute | solution.py:39
  65.1 1.6 %collective-permute-start.28 = (bf16[2,32,2304]{2,1,0:T(8,128)(2,1)}, bf16[2,32,2304]{2,1,0:T(8,128)(2,1)}, u32[]{:S(2)}, u32[]{:S(2)}) collective-permute-start(bf16[2,32,2304]{2,1,0:T(8,128)(2,1)} %pack.5.refs_4_), channel_id=1, source_target_pairs={{0,1},{1,0},{2,3},{3,2},{4,5},{5,4},{6,7},{7,6},{8,9},{9,8},{10,11... | collective-permute-start | bytes 884744 | tf_op jit(solution)/shard_map/ppermute | solution.py:43
  67.4 4.2 %project.1.refs_3_ = bf16[528,512]{1,0:T(8,128)(2,1)S(1)} custom-call(s32[21]{0:T(128)S(1)} %stack.190.spots, bf16[4,256,640]{2,1,0:T(8,128)(2,1)S(1)} %norm.1.x_ref, bf16[4,256,640]{2,1,0:T(8,128)(2,1)S(1)} %collective-permute-done.1.other_ref, f32[512,128]{1,0:T(8,128)} %get-tuple-element.26.cos_ref.cos_hbm.refs_1_, ...), custom_call_target="tpu_custom_call" | custom-call | flops 1207959552 | bytes 2359296 | tf_op jit(solution)/shard_map/project/pallas_call | solution.py:258
  71.6 1.4 %collective-permute-start.13 = (bf16[528,512]{1,0:T(8,128)(2,1)S(1)}, bf16[528,512]{1,0:T(8,128)(2,1)}, u32[]{:S(2)}, u32[]{:S(2)}) collective-permute-start(bf16[528,512]{1,0:T(8,128)(2,1)S(1)} %project.1.refs_3_), channel_id=1, source_target_pairs={{0,4},{2,6},{4,8},{6,10},{8,12},{10,14},{12,16},{14,18},{16,20},{1... | collective-permute-start | bytes 1622024 | tf_op jit(solution)/shard_map/ppermute | solution.py:53
  73.7 6.0 %collective-permute-done.30.refs_8_ = bf16[2,32,2304]{2,1,0:T(8,128)(2,1)S(1)} collective-permute-done((bf16[2,32,2304]{2,1,0:T(8,128)(2,1)}, bf16[2,32,2304]{2,1,0:T(8,128)(2,1)S(1)}, u32[]{:S(2)}, u32[]{:S(2)}) %collective-permute-start.30) | collective-permute-done | bytes 294944 | tf_op jit(solution)/shard_map/ppermute | solution.py:39
  79.9 2.0 %collective-permute-start.20 = (bf16[2,144,512]{2,1,0:T(8,128)(2,1)}, bf16[2,144,512]{2,1,0:T(8,128)(2,1)}, u32[]{:S(2)}, u32[]{:S(2)}) collective-permute-start(bf16[2,144,512]{2,1,0:T(8,128)(2,1)} %collective-permute-done.19.refs_11_), channel_id=1, source_target_pairs={{0,1},{1,0},{2,3},{3,2},{4,5},{5,4},{6,7},{7,6},{8,9},{9,8},{10,11... | collective-permute-start | bytes 884744 | tf_op jit(solution)/shard_map/ppermute | solution.py:43
  84.0 7.6 %collective-permute-done.32.refs_10_ = bf16[2,32,2304]{2,1,0:T(8,128)(2,1)} collective-permute-done((bf16[2,32,2304]{2,1,0:T(8,128)(2,1)}, bf16[2,32,2304]{2,1,0:T(8,128)(2,1)}, u32[]{:S(2)}, u32[]{:S(2)}) %collective-permute-start.32) | collective-permute-done | bytes 294944 | tf_op jit(solution)/shard_map/ppermute | solution.py:39
  91.7 3.7 %collective-permute-done.20.refs_12_ = bf16[2,144,512]{2,1,0:T(8,128)(2,1)} collective-permute-done((bf16[2,144,512]{2,1,0:T(8,128)(2,1)}, bf16[2,144,512]{2,1,0:T(8,128)(2,1)}, u32[]{:S(2)}, u32[]{:S(2)}) %collective-permute-start.20) | collective-permute-done | bytes 294944 | tf_op jit(solution)/shard_map/ppermute | solution.py:43
  95.9 7.2 %attend.1 = (bf16[2,256,256]{2,1,0:T(8,128)(2,1)S(1)}, bf16[2,256,256]{2,1,0:T(8,128)(2,1)}) custom-call(s32[22]{0:T(128)S(1)} %stack.187.place, bf16[4,256,640]{2,1,0:T(8,128)(2,1)S(1)} %norm.1.x_ref, bf16[4,256,640]{2,1,0:T(8,128)(2,1)S(1)} %collective-permute-done.1.other_ref, s32[1,256]{1,0:T(1,128)S(1)} %copy-done.5, ...), custom_call_target="tpu_custom_call" | custom-call | flops 1073741824 | bytes 1048576 | tf_op jit(solution)/shard_map/attend/pallas_call | solution.py:370
  103.9 1.3 %collective-permute-done.41.refs_19_ = bf16[1,32,2304]{2,1,0:T(8,128)(2,1)S(1)} collective-permute-done((bf16[1,32,2304]{2,1,0:T(8,128)(2,1)}, bf16[1,32,2304]{2,1,0:T(8,128)(2,1)S(1)}, u32[]{:S(2)}, u32[]{:S(2)}) %collective-permute-start.41) | collective-permute-done | bytes 147488 | tf_op jit(solution)/shard_map/ppermute | solution.py:35
  105.9 5.6 %finish.1 = bf16[256,2304]{1,0:T(8,128)(2,1)} custom-call(s32[37]{0:T(128)S(1)} %stack.177.marks, bf16[2,256,256]{2,1,0:T(8,128)(2,1)S(1)} %get-tuple-element.22.own_hbm, bf16[2,256,256]{2,1,0:T(8,128)(2,1)S(1)} %collective-permute-done.21.other_hbm, f32[1,2304]{1,0:T(1,128)S(1)} %broadcast_in_dim.27.gain_ref, bf16[256,2304]{1,0:T(8,128)(2,1)} %bitcast.41, ...), custom_call_target="tpu_custom_call" | custom-call | flops 1207959552 | bytes 4718592 | tf_op jit(solution)/shard_map/finish/pallas_call | solution.py:443
  (117 shorter events, 14.1 us)
Async XLA Ops:
  0.5 13.6 %collective-permute-start.22 = (bf16[2,32,2304]{2,1,0:T(8,128)(2,1)}, bf16[2,32,2304]{2,1,0:T(8,128)(2,1)}, u32[]{:S(2)}, u32[]{:S(2)}) collective-permute-start(bf16[2,32,2304]{2,1,0:T(8,128)(2,1)} %bitcast.42), channel_id=1, source_target_pairs={{0,2},{2,0},{4,6},{6,4},{8,10},{10,8},{12,14},{14,12},{16,18},{18,... | collective-permute-start | bytes 884744 | tf_op jit(solution)/shard_map/ppermute | solution.py:35
  7.8 59.6 %collective-permute-start.1 = (bf16[4,256,640]{2,1,0:T(8,128)(2,1)S(1)}, bf16[4,256,640]{2,1,0:T(8,128)(2,1)S(1)}, u32[]{:S(2)}, u32[]{:S(2)}) collective-permute-start(bf16[4,256,640]{2,1,0:T(8,128)(2,1)S(1)} %norm.1.x_ref), channel_id=1, source_target_pairs={{0,2},{2,0},{4,6},{6,4},{8,10},{10,8},{12,14},{14,12},{16,18},{18,... | collective-permute-start | bytes 3932168 | tf_op jit(solution)/shard_map/ppermute | solution.py:35
  8.2 10.5 %collective-permute-start.23 = (bf16[2,32,2304]{2,1,0:T(8,128)(2,1)S(1)}, bf16[2,32,2304]{2,1,0:T(8,128)(2,1)S(1)}, u32[]{:S(2)}, u32[]{:S(2)}) collective-permute-start(bf16[2,32,2304]{2,1,0:T(8,128)(2,1)S(1)} %bitcast.44), channel_id=1, source_target_pairs={{0,4},{2,6},{4,0},{6,2},{8,12},{10,14},{12,8},{14,10},{16,20},{18,... | collective-permute-start | bytes 884744 | tf_op jit(solution)/shard_map/ppermute | solution.py:39
  10.9 7.9 %collective-permute-start.4 = (bf16[144,512]{1,0:T(8,128)(2,1)S(1)}, bf16[144,512]{1,0:T(8,128)(2,1)S(1)}, u32[]{:S(2)}, u32[]{:S(2)}) collective-permute-start(bf16[144,512]{1,0:T(8,128)(2,1)S(1)} %get-tuple-element.19), channel_id=1, source_target_pairs={{0,8},{2,10},{4,12},{6,14},{8,16},{10,18},{12,20},{14,22},{16,24},... | collective-permute-start | bytes 442376 | tf_op jit(solution)/shard_map/ppermute | solution.py:48
  13.6 12.1 %collective-permute-start.14 = (bf16[2,144,512]{2,1,0:T(8,128)(2,1)S(1)}, bf16[2,144,512]{2,1,0:T(8,128)(2,1)S(1)}, u32[]{:S(2)}, u32[]{:S(2)}) collective-permute-start(bf16[2,144,512]{2,1,0:T(8,128)(2,1)S(1)} %get-tuple-element.20.refs_5_), channel_id=1, source_target_pairs={{0,4},{2,6},{4,0},{6,2},{8,12},{10,14},{12,8},{14,10},{16,20},{18,... | collective-permute-start | bytes 884744 | tf_op jit(solution)/shard_map/ppermute | solution.py:39
  14.1 7.6 %collective-permute-start.25 = (bf16[32,2304]{1,0:T(8,128)(2,1)S(1)}, bf16[32,2304]{1,0:T(8,128)(2,1)S(1)}, u32[]{:S(2)}, u32[]{:S(2)}) collective-permute-start(bf16[32,2304]{1,0:T(8,128)(2,1)S(1)} %get-tuple-element.24), channel_id=1, source_target_pairs={{0,8},{2,10},{4,12},{6,14},{8,16},{10,18},{12,20},{14,22},{16,24},... | collective-permute-start | bytes 442376 | tf_op jit(solution)/shard_map/ppermute | solution.py:48
  18.8 17.7 %collective-permute-start.24 = (bf16[2,32,2304]{2,1,0:T(8,128)(2,1)S(1)}, bf16[2,32,2304]{2,1,0:T(8,128)(2,1)S(1)}, u32[]{:S(2)}, u32[]{:S(2)}) collective-permute-start(bf16[2,32,2304]{2,1,0:T(8,128)(2,1)S(1)} %collective-permute-done.23.refs_2_), channel_id=1, source_target_pairs={{0,2},{2,0},{4,6},{6,4},{8,10},{10,8},{12,14},{14,12},{16,18},{18,... | collective-permute-start | bytes 884744 | tf_op jit(solution)/shard_map/ppermute | solution.py:35
  21.8 15.3 %collective-permute-start.3 = (bf16[2,144,512]{2,1,0:T(8,128)(2,1)S(1)}, bf16[2,144,512]{2,1,0:T(8,128)(2,1)S(1)}, u32[]{:S(2)}, u32[]{:S(2)}) collective-permute-start(bf16[2,144,512]{2,1,0:T(8,128)(2,1)S(1)} %get-tuple-element.18.refs_0_), channel_id=1, source_target_pairs={{0,4},{2,6},{4,0},{6,2},{8,12},{10,14},{12,8},{14,10},{16,20},{18,... | collective-permute-start | bytes 884744 | tf_op jit(solution)/shard_map/ppermute | solution.py:39
  25.7 9.2 %collective-permute-start.9 = (bf16[144,512]{1,0:T(8,128)(2,1)S(1)}, bf16[144,512]{1,0:T(8,128)(2,1)S(1)}, u32[]{:S(2)}, u32[]{:S(2)}) collective-permute-start(bf16[144,512]{1,0:T(8,128)(2,1)S(1)} %collective-permute-done.5), channel_id=1, source_target_pairs={{0,8},{2,10},{4,12},{6,14},{8,16},{10,18},{12,20},{14,22},{16,24},... | collective-permute-start | bytes 442376 | tf_op jit(solution)/shard_map/ppermute | solution.py:48
  32.8 8.6 %collective-permute-start.34 = (bf16[32,2304]{1,0:T(8,128)(2,1)S(1)}, bf16[32,2304]{1,0:T(8,128)(2,1)}, u32[]{:S(2)}, u32[]{:S(2)}) collective-permute-start(bf16[32,2304]{1,0:T(8,128)(2,1)S(1)} %collective-permute-done.26), channel_id=1, source_target_pairs={{0,8},{2,10},{4,12},{6,14},{8,16},{10,18},{12,20},{14,22},{16,24},... | collective-permute-start | bytes 442376 | tf_op jit(solution)/shard_map/ppermute | solution.py:48
  34.9 7.7 %collective-permute-start.10 = (bf16[1,144,512]{2,1,0:T(8,128)(2,1)S(1)}, bf16[1,144,512]{2,1,0:T(8,128)(2,1)S(1)}, u32[]{:S(2)}, u32[]{:S(2)}) collective-permute-start(bf16[1,144,512]{2,1,0:T(8,128)(2,1)S(1)} %bitcast.45), channel_id=1, source_target_pairs={{0,1},{1,0},{2,3},{3,2},{4,5},{5,4},{6,7},{7,6},{8,9},{9,8},{10,11... | collective-permute-start | bytes 442376 | tf_op jit(solution)/shard_map/ppermute | solution.py:43
  36.5 13.9 %collective-permute-start.6 = (bf16[2,144,512]{2,1,0:T(8,128)(2,1)S(1)}, bf16[2,144,512]{2,1,0:T(8,128)(2,1)}, u32[]{:S(2)}, u32[]{:S(2)}) collective-permute-start(bf16[2,144,512]{2,1,0:T(8,128)(2,1)S(1)} %pack.3.refs_2_), channel_id=1, source_target_pairs={{0,1},{1,0},{2,3},{3,2},{4,5},{5,4},{6,7},{7,6},{8,9},{9,8},{10,11... | collective-permute-start | bytes 884744 | tf_op jit(solution)/shard_map/ppermute | solution.py:43
  37.1 13.8 %collective-permute-start.15 = (bf16[2,144,512]{2,1,0:T(8,128)(2,1)S(1)}, bf16[2,144,512]{2,1,0:T(8,128)(2,1)}, u32[]{:S(2)}, u32[]{:S(2)}) collective-permute-start(bf16[2,144,512]{2,1,0:T(8,128)(2,1)S(1)} %pack.4), channel_id=1, source_target_pairs={{0,8},{2,10},{4,12},{6,14},{8,16},{10,18},{12,20},{14,22},{16,24},... | collective-permute-start | bytes 884744 | tf_op jit(solution)/shard_map/ppermute | solution.py:48
  47.3 9.9 %collective-permute-start.7 = (bf16[2,144,512]{2,1,0:T(8,128)(2,1)S(1)}, bf16[2,144,512]{2,1,0:T(8,128)(2,1)S(1)}, u32[]{:S(2)}, u32[]{:S(2)}) collective-permute-start(bf16[2,144,512]{2,1,0:T(8,128)(2,1)S(1)} %pack.3.refs_2_), channel_id=1, source_target_pairs={{0,4},{2,6},{4,0},{6,2},{8,12},{10,14},{12,8},{14,10},{16,20},{18,... | collective-permute-start | bytes 884744 | tf_op jit(solution)/shard_map/ppermute | solution.py:39
  50.4 14.7 %collective-permute-start.8 = (bf16[2,144,512]{2,1,0:T(8,128)(2,1)}, bf16[2,144,512]{2,1,0:T(8,128)(2,1)}, u32[]{:S(2)}, u32[]{:S(2)}) collective-permute-start(bf16[2,144,512]{2,1,0:T(8,128)(2,1)} %collective-permute-done.6.refs_3_), channel_id=1, source_target_pairs={{0,4},{2,6},{4,0},{6,2},{8,12},{10,14},{12,8},{14,10},{16,20},{18,... | collective-permute-start | bytes 884744 | tf_op jit(solution)/shard_map/ppermute | solution.py:39
  50.9 15.8 %collective-permute-start.17 = (bf16[2,144,512]{2,1,0:T(8,128)(2,1)}, bf16[2,144,512]{2,1,0:T(8,128)(2,1)}, u32[]{:S(2)}, u32[]{:S(2)}) collective-permute-start(bf16[2,144,512]{2,1,0:T(8,128)(2,1)} %collective-permute-done.15.refs_7_), channel_id=1, source_target_pairs={{0,8},{2,10},{4,12},{6,14},{8,16},{10,18},{12,20},{14,22},{16,24},... | collective-permute-start | bytes 884744 | tf_op jit(solution)/shard_map/ppermute | solution.py:48
  54.3 8.7 %collective-permute-start.12 = (bf16[1,144,512]{2,1,0:T(8,128)(2,1)S(1)}, bf16[1,144,512]{2,1,0:T(8,128)(2,1)S(1)}, u32[]{:S(2)}, u32[]{:S(2)}) collective-permute-start(bf16[1,144,512]{2,1,0:T(8,128)(2,1)S(1)} %collective-permute-done.10.refs_7_), channel_id=1, source_target_pairs={{0,4},{2,6},{4,0},{6,2},{8,12},{10,14},{12,8},{14,10},{16,20},{18,... | collective-permute-start | bytes 442376 | tf_op jit(solution)/shard_map/ppermute | solution.py:39
  57.2 15.8 %collective-permute-start.27 = (bf16[2,32,2304]{2,1,0:T(8,128)(2,1)}, bf16[2,32,2304]{2,1,0:T(8,128)(2,1)}, u32[]{:S(2)}, u32[]{:S(2)}) collective-permute-start(bf16[2,32,2304]{2,1,0:T(8,128)(2,1)} %pack.5.refs_4_), channel_id=1, source_target_pairs={{0,2},{2,0},{4,6},{6,4},{8,10},{10,8},{12,14},{14,12},{16,18},{18,... | collective-permute-start | bytes 884744 | tf_op jit(solution)/shard_map/ppermute | solution.py:35
  63.7 7.9 %collective-permute-start.38 = (bf16[1,32,2304]{2,1,0:T(8,128)(2,1)}, bf16[1,32,2304]{2,1,0:T(8,128)(2,1)}, u32[]{:S(2)}, u32[]{:S(2)}) collective-permute-start(bf16[1,32,2304]{2,1,0:T(8,128)(2,1)} %bitcast.36.refs_12_), channel_id=1, source_target_pairs={{0,4},{2,6},{4,0},{6,2},{8,12},{10,14},{12,8},{14,10},{16,20},{18,... | collective-permute-start | bytes 442376 | tf_op jit(solution)/shard_map/ppermute | solution.py:39
  65.1 7.9 %collective-permute-start.28 = (bf16[2,32,2304]{2,1,0:T(8,128)(2,1)}, bf16[2,32,2304]{2,1,0:T(8,128)(2,1)}, u32[]{:S(2)}, u32[]{:S(2)}) collective-permute-start(bf16[2,32,2304]{2,1,0:T(8,128)(2,1)} %pack.5.refs_4_), channel_id=1, source_target_pairs={{0,1},{1,0},{2,3},{3,2},{4,5},{5,4},{6,7},{7,6},{8,9},{9,8},{10,11... | collective-permute-start | bytes 884744 | tf_op jit(solution)/shard_map/ppermute | solution.py:43
  66.7 13.1 %collective-permute-start.30 = (bf16[2,32,2304]{2,1,0:T(8,128)(2,1)}, bf16[2,32,2304]{2,1,0:T(8,128)(2,1)S(1)}, u32[]{:S(2)}, u32[]{:S(2)}) collective-permute-start(bf16[2,32,2304]{2,1,0:T(8,128)(2,1)} %pack.5.refs_4_), channel_id=1, source_target_pairs={{0,4},{2,6},{4,0},{6,2},{8,12},{10,14},{12,8},{14,10},{16,20},{18,... | collective-permute-start | bytes 884744 | tf_op jit(solution)/shard_map/ppermute | solution.py:39
  67.4 12.5 %collective-permute-start.19 = (bf16[2,144,512]{2,1,0:T(8,128)(2,1)}, bf16[2,144,512]{2,1,0:T(8,128)(2,1)}, u32[]{:S(2)}, u32[]{:S(2)}) collective-permute-start(bf16[2,144,512]{2,1,0:T(8,128)(2,1)} %collective-permute-done.17.refs_9_), channel_id=1, source_target_pairs={{0,8},{2,10},{4,12},{6,14},{8,16},{10,18},{12,20},{14,22},{16,24},... | collective-permute-start | bytes 884744 | tf_op jit(solution)/shard_map/ppermute | solution.py:48
  71.6 23.8 %collective-permute-start.13 = (bf16[528,512]{1,0:T(8,128)(2,1)S(1)}, bf16[528,512]{1,0:T(8,128)(2,1)}, u32[]{:S(2)}, u32[]{:S(2)}) collective-permute-start(bf16[528,512]{1,0:T(8,128)(2,1)S(1)} %project.1.refs_3_), channel_id=1, source_target_pairs={{0,4},{2,6},{4,8},{6,10},{8,12},{10,14},{12,16},{14,18},{16,20},{1... | collective-permute-start | bytes 1622024 | tf_op jit(solution)/shard_map/ppermute | solution.py:53
  73.0 10.2 %collective-permute-start.16 = (bf16[2,144,512]{2,1,0:T(8,128)(2,1)}, bf16[2,144,512]{2,1,0:T(8,128)(2,1)S(1)}, u32[]{:S(2)}, u32[]{:S(2)}) collective-permute-start(bf16[2,144,512]{2,1,0:T(8,128)(2,1)} %collective-permute-done.15.refs_7_), channel_id=1, source_target_pairs={{0,1},{1,0},{2,3},{3,2},{4,5},{5,4},{6,7},{7,6},{8,9},{9,8},{10,11... | collective-permute-start | bytes 884744 | tf_op jit(solution)/shard_map/ppermute | solution.py:43
  79.8 11.9 %collective-permute-start.32 = (bf16[2,32,2304]{2,1,0:T(8,128)(2,1)}, bf16[2,32,2304]{2,1,0:T(8,128)(2,1)}, u32[]{:S(2)}, u32[]{:S(2)}) collective-permute-start(bf16[2,32,2304]{2,1,0:T(8,128)(2,1)} %collective-permute-done.28.refs_6_), channel_id=1, source_target_pairs={{0,4},{2,6},{4,0},{6,2},{8,12},{10,14},{12,8},{14,10},{16,20},{18,... | collective-permute-start | bytes 884744 | tf_op jit(solution)/shard_map/ppermute | solution.py:39
  79.8 11.9 %collective-permute-start.18 = (bf16[2,144,512]{2,1,0:T(8,128)(2,1)}, bf16[2,144,512]{2,1,0:T(8,128)(2,1)}, u32[]{:S(2)}, u32[]{:S(2)}) collective-permute-start(bf16[2,144,512]{2,1,0:T(8,128)(2,1)} %collective-permute-done.17.refs_9_), channel_id=1, source_target_pairs={{0,1},{1,0},{2,3},{3,2},{4,5},{5,4},{6,7},{7,6},{8,9},{9,8},{10,11... | collective-permute-start | bytes 884744 | tf_op jit(solution)/shard_map/ppermute | solution.py:43
  79.9 15.5 %collective-permute-start.20 = (bf16[2,144,512]{2,1,0:T(8,128)(2,1)}, bf16[2,144,512]{2,1,0:T(8,128)(2,1)}, u32[]{:S(2)}, u32[]{:S(2)}) collective-permute-start(bf16[2,144,512]{2,1,0:T(8,128)(2,1)} %collective-permute-done.19.refs_11_), channel_id=1, source_target_pairs={{0,1},{1,0},{2,3},{3,2},{4,5},{5,4},{6,7},{7,6},{8,9},{9,8},{10,11... | collective-permute-start | bytes 884744 | tf_op jit(solution)/shard_map/ppermute | solution.py:43
  83.2 20.0 %collective-permute-start.39 = (bf16[1,32,2304]{2,1,0:T(8,128)(2,1)}, bf16[1,32,2304]{2,1,0:T(8,128)(2,1)}, u32[]{:S(2)}, u32[]{:S(2)}) collective-permute-start(bf16[1,32,2304]{2,1,0:T(8,128)(2,1)} %collective-permute-done.38.refs_16_), channel_id=1, source_target_pairs={{0,2},{2,0},{4,6},{6,4},{8,10},{10,8},{12,14},{14,12},{16,18},{18,... | collective-permute-start | bytes 442376 | tf_op jit(solution)/shard_map/ppermute | solution.py:35
  91.6 11.6 %collective-permute-start.40 = (bf16[1,32,2304]{2,1,0:T(8,128)(2,1)}, bf16[1,32,2304]{2,1,0:T(8,128)(2,1)}, u32[]{:S(2)}, u32[]{:S(2)}) collective-permute-start(bf16[1,32,2304]{2,1,0:T(8,128)(2,1)} %copy-done.18), channel_id=1, source_target_pairs={{0,4},{2,6},{4,0},{6,2},{8,12},{10,14},{12,8},{14,10},{16,20},{18,... | collective-permute-start | bytes 442376 | tf_op jit(solution)/shard_map/ppermute | solution.py:39
  91.7 13.6 %collective-permute-start.29 = (bf16[2,32,2304]{2,1,0:T(8,128)(2,1)}, bf16[2,32,2304]{2,1,0:T(8,128)(2,1)}, u32[]{:S(2)}, u32[]{:S(2)}) collective-permute-start(bf16[2,32,2304]{2,1,0:T(8,128)(2,1)} %collective-permute-done.28.refs_6_), channel_id=1, source_target_pairs={{0,2},{2,0},{4,6},{6,4},{8,10},{10,8},{12,14},{14,12},{16,18},{18,... | collective-permute-start | bytes 884744 | tf_op jit(solution)/shard_map/ppermute | solution.py:35
  95.4 9.8 %collective-permute-start.31 = (bf16[2,32,2304]{2,1,0:T(8,128)(2,1)}, bf16[2,32,2304]{2,1,0:T(8,128)(2,1)}, u32[]{:S(2)}, u32[]{:S(2)}) collective-permute-start(bf16[2,32,2304]{2,1,0:T(8,128)(2,1)} %copy-done.10), channel_id=1, source_target_pairs={{0,2},{2,0},{4,6},{6,4},{8,10},{10,8},{12,14},{14,12},{16,18},{18,... | collective-permute-start | bytes 884744 | tf_op jit(solution)/shard_map/ppermute | solution.py:35
  95.4 9.8 %collective-permute-start.33 = (bf16[2,32,2304]{2,1,0:T(8,128)(2,1)}, bf16[2,32,2304]{2,1,0:T(8,128)(2,1)}, u32[]{:S(2)}, u32[]{:S(2)}) collective-permute-start(bf16[2,32,2304]{2,1,0:T(8,128)(2,1)} %collective-permute-done.32.refs_10_), channel_id=1, source_target_pairs={{0,2},{2,0},{4,6},{6,4},{8,10},{10,8},{12,14},{14,12},{16,18},{18,... | collective-permute-start | bytes 884744 | tf_op jit(solution)/shard_map/ppermute | solution.py:35
  (34 other events, 343.4 us)
